TPU v7x, 16 devices: a 4x2x1 block of a 4x4x8 slice. The times are simulated.
16 devices in a mesh: req: 2 (over y, z), dap: 8 (over x, core).
Axes of the slice: x: 4, y: 2, z: 1, core: 2. Of those that a mesh axis runs over, the one named last changes fastest.
The devices are a block of a 4x4x8 slice.
Arguments:
- msa_act: bfloat16 [512, 256, 256], P(('req', 'dap')), parts along dimension 0
- pair_act: bfloat16 [512, 256, 128], P(('req', 'dap')), parts along dimension 0
- msa_mask: int32 [512, 256], P(('req', 'dap')), parts along dimension 0
- pair_mask: int32 [512, 256], P(('req', 'dap')), parts along dimension 0
- row_qkvg: bfloat16 [2, 256, 1024], replicated
- row_bias: bfloat16 [2, 128, 8], replicated
- row_out: bfloat16 [2, 256, 256], replicated
- col_qkvg: bfloat16 [2, 256, 1024], replicated
- col_out: bfloat16 [2, 256, 256], replicated
- mtr_in: bfloat16 [2, 256, 1024], replicated
- mtr_out: bfloat16 [2, 1024, 256], replicated
- opm_proj: bfloat16 [2, 256, 64], replicated
- opm_out: bfloat16 [2, 1024, 128], replicated
- tmo_proj: bfloat16 [2, 128, 640], replicated
- tmo_out: bfloat16 [2, 128, 128], replicated
- tmi_proj: bfloat16 [2, 128, 640], replicated
- tmi_out: bfloat16 [2, 128, 128], replicated
- tas_qkvg: bfloat16 [2, 128, 512], replicated
- tas_bias: bfloat16 [2, 128, 4], replicated
- tas_out: bfloat16 [2, 128, 128], replicated
- tae_qkvg: bfloat16 [2, 128, 512], replicated
- tae_bias: bfloat16 [2, 128, 4], replicated
- tae_out: bfloat16 [2, 128, 128], replicated
- ptr_in: bfloat16 [2, 128, 512], replicated
- ptr_out: bfloat16 [2, 512, 128], replicated
Outputs:
- output 1: bfloat16 [512, 256, 256], P(('req', 'dap')), parts along dimension 0
- output 2: bfloat16 [512, 256, 128], P(('req', 'dap')), parts along dimension 0
There are 2 independent parts. A program takes and returns all parts, laid end to end along the dimension named above; an argument that names none is the same for every part.
All inputs are finite; a program needn't handle non-finite values.
Results may differ from a plain program's by a relative error of at most 0.02.
Values are sent between devices in bfloat16 or wider.
A program may use at most 768 MiB of HBM per device.

v0:
```python
import jax
import jax.numpy as jnp
from jax import lax
from jax.sharding import PartitionSpec as P

GROUP_AXIS = 'dap'
PARTS_AXIS = 'req'
MASKED_LOGIT = -1e9


def layer_norm(x):
    values = x.astype(jnp.float32)
    centered = values - jnp.mean(values, axis=-1, keepdims=True)
    variance = jnp.mean(centered * centered, axis=-1, keepdims=True)
    return (centered * lax.rsqrt(variance + 1e-5)).astype(jnp.bfloat16)


def residual(x, update):
    return (x.astype(jnp.float32) + update).astype(jnp.bfloat16)


def dense(x, weight):
    return jnp.einsum('...c,cf->...f', x, weight, preferred_element_type=jnp.float32)


def attend(queries, gate_raw, keyvals, num_heads, pair_bias, key_mask, w_out):
    n_batch, q_len, head_width = queries.shape
    k_len = keyvals.shape[1]
    head_dim = head_width // num_heads
    q_heads = queries.reshape(n_batch, q_len, num_heads, head_dim)
    k_heads = keyvals[..., :head_width].reshape(n_batch, k_len, num_heads, head_dim)
    v_heads = keyvals[..., head_width:].reshape(n_batch, k_len, num_heads, head_dim)
    logits = jnp.einsum('bqhd,bkhd->bhqk', q_heads, k_heads, preferred_element_type=jnp.float32) * head_dim ** -0.5
    if pair_bias is not None:
        logits = logits + pair_bias.astype(jnp.float32)
    logits = jnp.where(key_mask[:, None, None, :] > 0, logits, MASKED_LOGIT)
    attn_prob = jax.nn.softmax(logits, axis=-1).astype(jnp.bfloat16)
    attended = jnp.einsum('bhqk,bkhd->bqhd', attn_prob, v_heads, preferred_element_type=jnp.float32)
    gated = (attended.reshape(n_batch, q_len, head_width) * jax.nn.sigmoid(gate_raw.astype(jnp.float32))).astype(jnp.bfloat16)
    return dense(gated, w_out)


def self_attention(x_norm, w_qkvg, num_heads, pair_bias, key_mask, w_out):
    head_width = w_out.shape[0]
    projected = dense(x_norm, w_qkvg).astype(jnp.bfloat16)
    return attend(projected[..., :head_width], projected[..., 3 * head_width:], projected[..., head_width:3 * head_width], num_heads, pair_bias, key_mask, w_out)


def head_bias(pair_norm, w_bias):
    return jnp.einsum('ijc,ch->hij', pair_norm, w_bias, preferred_element_type=jnp.float32).astype(jnp.bfloat16)


def transition(x, w_in, w_out):
    hidden = jnp.maximum(dense(layer_norm(x), w_in), 0.0).astype(jnp.bfloat16)
    return dense(hidden, w_out)


def outer_update(array_b7, res_mask, full_mask, w_proj, w_out):
    opm_dim = w_proj.shape[1] // 2
    projected = dense(layer_norm(array_b7), w_proj).astype(jnp.bfloat16)
    mask_bf = res_mask.astype(jnp.bfloat16)[:, :, None]
    left_act = projected[..., :opm_dim] * mask_bf
    right_act = projected[..., opm_dim:] * mask_bf
    right_full = lax.all_gather(right_act, GROUP_AXIS, axis=1, tiled=True)
    outer_prod = jnp.einsum('sic,sje->ijce', left_act, right_full, preferred_element_type=jnp.float32).astype(jnp.bfloat16)
    n_rows, n_cols = outer_prod.shape[:2]
    update = dense(outer_prod.reshape(n_rows, n_cols, opm_dim * opm_dim), w_out)
    overlap = jnp.einsum('si,sj->ij', res_mask.astype(jnp.float32), full_mask.astype(jnp.float32))
    return update / (1e-3 + overlap)[:, :, None]


def tri_gates(pair_rows, mask_rows, w_proj):
    tri_dim = (w_proj.shape[1] - pair_rows.shape[-1]) // 4
    projected = dense(layer_norm(pair_rows), w_proj)
    mask_f = mask_rows.astype(jnp.float32)[:, :, None]
    left_act = (mask_f * jax.nn.sigmoid(projected[..., 2 * tri_dim:3 * tri_dim]) * projected[..., :tri_dim]).astype(jnp.bfloat16)
    right_act = (mask_f * jax.nn.sigmoid(projected[..., 3 * tri_dim:4 * tri_dim]) * projected[..., tri_dim:2 * tri_dim]).astype(jnp.bfloat16)
    gate_act = jax.nn.sigmoid(projected[..., 4 * tri_dim:])
    return left_act, right_act, gate_act


def tri_finish(product, gate_act, w_out):
    return gate_act * dense(layer_norm(product), w_out)


def tri_attention(pair_rows, mask_rows, w_qkvg, w_bias, w_out):
    pair_norm = layer_norm(pair_rows)
    bias_full = lax.all_gather(head_bias(pair_norm, w_bias), GROUP_AXIS, axis=1, tiled=True)
    return self_attention(pair_norm, w_qkvg, w_bias.shape[1], bias_full, mask_rows, w_out)


def pair_stack(pair_loc, pair_mask, pair_mask_t, pair_w):
    (tmo_proj, tmo_out, tmi_proj, tmi_out, tas_qkvg, tas_bias, tas_out,
     tae_qkvg, tae_bias, tae_out, ptr_in, ptr_out) = pair_w
    left_act, right_act, gate_act = tri_gates(pair_loc, pair_mask, tmo_proj)
    right_full = lax.all_gather(right_act, GROUP_AXIS, axis=0, tiled=True)
    product = jnp.einsum('ikc,jkc->ijc', left_act, right_full, preferred_element_type=jnp.float32)
    pair_loc = residual(pair_loc, tri_finish(product, gate_act, tmo_out))
    left_act, right_act, gate_act = tri_gates(pair_loc, pair_mask, tmi_proj)
    left_cols = lax.all_to_all(left_act, GROUP_AXIS, 1, 0, tiled=True)
    right_full = lax.all_gather(right_act, GROUP_AXIS, axis=0, tiled=True)
    product = jnp.einsum('kic,kjc->ijc', left_cols, right_full, preferred_element_type=jnp.float32)
    pair_loc = residual(pair_loc, tri_finish(product, gate_act, tmi_out))
    pair_loc = residual(pair_loc, tri_attention(pair_loc, pair_mask, tas_qkvg, tas_bias, tas_out))
    pair_cols = lax.all_to_all(pair_loc, GROUP_AXIS, 1, 0, tiled=True)
    pair_t = jnp.swapaxes(pair_cols, 0, 1)
    pair_t = residual(pair_t, tri_attention(pair_t, pair_mask_t, tae_qkvg, tae_bias, tae_out))
    pair_loc = lax.all_to_all(jnp.swapaxes(pair_t, 0, 1), GROUP_AXIS, 0, 1, tiled=True)
    return residual(pair_loc, transition(pair_loc, ptr_in, ptr_out))


def evoformer_block(value_a7, pair_loc, full_mask, full_pair_mask, layer_w):
    (row_qkvg, row_bias, row_out, col_qkvg, col_out, mtr_in, mtr_out, opm_proj, opm_out) = layer_w[:9]
    shard_idx = lax.axis_index(GROUP_AXIS)
    seq_loc = value_a7.shape[0]
    res_loc = pair_loc.shape[0]
    seq_mask = lax.dynamic_slice_in_dim(full_mask, shard_idx * seq_loc, seq_loc, 0)
    res_mask = lax.dynamic_slice_in_dim(full_mask, shard_idx * res_loc, res_loc, 1)
    pair_mask = lax.dynamic_slice_in_dim(full_pair_mask, shard_idx * res_loc, res_loc, 0)
    pair_mask_t = lax.dynamic_slice_in_dim(full_pair_mask, shard_idx * res_loc, res_loc, 1).T
    value_a9 = row_bias.shape[1]
    row_bias_full = lax.all_gather(head_bias(layer_norm(pair_loc), row_bias), GROUP_AXIS, axis=1, tiled=True)
    value_a7 = residual(value_a7, self_attention(layer_norm(value_a7), row_qkvg, value_a9, row_bias_full, seq_mask, row_out))
    array_b7 = lax.all_to_all(value_a7, GROUP_AXIS, 1, 0, tiled=True)
    col_norm = jnp.swapaxes(layer_norm(array_b7), 0, 1)
    col_update = self_attention(col_norm, col_qkvg, value_a9, None, res_mask.T, col_out)
    array_b7 = residual(array_b7, jnp.swapaxes(col_update, 0, 1))
    array_b7 = residual(array_b7, transition(array_b7, mtr_in, mtr_out))
    pair_loc = residual(pair_loc, outer_update(array_b7, res_mask, full_mask, opm_proj, opm_out))
    pair_loc = pair_stack(pair_loc, pair_mask, pair_mask_t, layer_w[9:])
    value_a7 = lax.all_to_all(array_b7, GROUP_AXIS, 0, 1, tiled=True)
    return value_a7, pair_loc


def solution(mesh):
    row_spec = P((PARTS_AXIS, GROUP_AXIS))

    def local_body(value_a7, pair_loc, value_a12, pair_mask_loc, *weights):
        full_mask = lax.all_gather(value_a12, GROUP_AXIS, axis=0, tiled=True)
        full_pair_mask = lax.all_gather(pair_mask_loc, GROUP_AXIS, axis=0, tiled=True)
        for layer_idx in range(weights[0].shape[0]):
            layer_w = tuple(weight[layer_idx] for weight in weights)
            value_a7, pair_loc = evoformer_block(value_a7, pair_loc, full_mask, full_pair_mask, layer_w)
        return value_a7, pair_loc

    def run_blocks(*arrays):
        n_weights = len(arrays) - 4
        return jax.shard_map(local_body, mesh=mesh, in_specs=(row_spec,) * 4 + (P(),) * n_weights, out_specs=(row_spec, row_spec), check_vma=False)(*arrays)

    return run_blocks
```

profile of v0, /device:TPU:112, one launch (start us, length us, event | category | flops | bytes accessed | tf_op | source)
XLA Modules:
  0.0 2024.7 jit_solution(17877931721203026430)
XLA Ops:
  57.2 25.1 %all_gather.42 = s32[256,256]{1,0:T(8,128)S(1)} all-gather(s32[32,256]{1,0:T(8,128)S(1)} %copy-done.55), channel_id=1, replica_groups=mesh['req'=2,'dap'=8] {'dap'}, dimensions={0}, use_global_device_ids=true | all-gather | bytes 294912 | tf_op jit(solution)/shard_map/all_gather | solution.py:139
  84.3 33.8 %fusion.455 = (f32[32,8,256]{2,1,0:T(8,128)S(1)}, f32[32,8,256,256]{2,3,1,0:T(8,128)}) fusion(f32[8,256,256]{1,2,0:T(8,128)S(1)} %copy.1195, pred[32,256]{1,0:T(8,128)(4,1)S(1)} %dynamic-slice_compare_fusion, bf16[32,256,8,32]{1,3,2,0:T(8,128)(2,1)} %bitcast.549, bf16[32,256,8,32]{1,3,2,0:T(8,128)(2,1)} %bitcast.551), kind=kOutput, calls=%fused_computation.607 | convolution fusion | flops 1157628160 | bytes 77864960 | tf_op jit(solution)/shard_map/sub | solution.py:37
  118.1 26.4 %fusion.26 = f32[32,8,32,256]{3,2,1,0:T(8,128)} fusion(bf16[32,256,8,32]{1,3,2,0:T(8,128)(2,1)} %bitcast.550, f32[32,8,256,256]{2,3,1,0:T(8,128)} %get-tuple-element.39, f32[32,8,256]{2,1,0:T(8,128)S(1)} %get-tuple-element.38), kind=kOutput, calls=%fused_computation.52 | convolution fusion | flops 1107296256 | bytes 79953920 | tf_op jit(solution)/shard_map/bhqk,bkhd->bqhd/dot_general | solution.py:38
  171.5 64.5 %all_gather.45 = s32[256,256]{1,0:T(8,128)S(1)} all-gather(s32[32,256]{1,0:T(8,128)S(1)} %copy-done.56), channel_id=1, replica_groups=mesh['req'=2,'dap'=8] {'dap'}, dimensions={0}, use_global_device_ids=true | all-gather | bytes 294912 | tf_op jit(solution)/shard_map/all_gather | solution.py:140
  255.7 15.7 convolution_convert_fusion.2
  299.8 32.7 %fusion.456 = (f32[32,8,256]{2,1,0:T(8,128)S(1)}, f32[32,8,256,256]{2,3,1,0:T(8,128)}) fusion(pred[32,256]{1,0:T(8,128)(4,1)S(1)} %compare_bitcast_fusion.1, bf16[32,256,8,32]{1,3,2,0:T(8,128)(2,1)} %bitcast.556, bf16[32,256,8,32]{1,3,2,0:T(8,128)(2,1)} %bitcast.559), kind=kOutput, calls=%fused_computation.608 | convolution fusion | flops 1140850944 | bytes 75767808 | tf_op jit(solution)/shard_map/sub | solution.py:37
  332.5 26.4 %fusion.27 = f32[32,8,32,256]{3,2,1,0:T(8,128)} fusion(bf16[32,256,8,32]{1,3,2,0:T(8,128)(2,1)} %bitcast.560, f32[32,8,256,256]{2,3,1,0:T(8,128)} %get-tuple-element.41, f32[32,8,256]{2,1,0:T(8,128)S(1)} %get-tuple-element.40), kind=kOutput, calls=%fused_computation.53 | convolution fusion | flops 1107296256 | bytes 79953920 | tf_op jit(solution)/shard_map/bhqk,bkhd->bqhd/dot_general | solution.py:38
  390.0 14.5 convert_reduce_fusion.4
  411.5 27.2 %all-gather.11.cloned.1.call-done = bf16[256,256,32]{0,2,1:T(8,128)(2,1)} async-done(((bf16[256,32,32]{0,2,1:T(8,128)(2,1)}), bf16[256,256,32]{0,2,1:T(8,128)(2,1)}) %all-gather.11.cloned.1.call-update) | async-done | bytes 4194320 | tf_op jit(solution)/shard_map/all_gather | solution.py:64
  438.7 12.7 convert_bitcast_fusion.1
  451.4 16.0 copy.1224
  486.4 81.1 %all-gather.13.cloned.1.call-done = bf16[256,256,128]{2,1,0:T(8,128)(2,1)} async-done(((bf16[32,256,128]{2,1,0:T(8,128)(2,1)}), bf16[256,256,128]{2,1,0:T(8,128)(2,1)}) %all-gather.13.cloned.1.call-update) | async-done | bytes 16777232 | tf_op jit(solution)/shard_map/all_gather | solution.py:96
  567.4 23.1 %copy.1234 = bf16[256,256,128]{1,0,2:T(8,128)(2,1)} copy(bf16[256,256,128]{2,1,0:T(8,128)(2,1)} %all-gather.13.cloned.1.call-done) | data formatting | bytes 33554432 | tf_op jit(solution)/shard_map/all_gather | solution.py:96
  629.1 47.6 %all-to-all-done.2 = bf16[32,256,128]{2,0,1:T(8,128)(2,1)S(1)} async-done(((bf16[32,256,128]{2,0,1:T(8,128)(2,1)}), bf16[32,256,128]{2,0,1:T(8,128)(2,1)S(1)}, u32[]{:S(2)}, u32[]{:S(2)}) %all-to-all-start.2) | async-done | bytes 2097184 | tf_op jit(solution)/shard_map/all_to_all | solution.py:100
  682.7 41.3 %all-gather.15.cloned.1.call-done = bf16[256,256,128]{2,1,0:T(8,128)(2,1)} async-done(((bf16[32,256,128]{2,1,0:T(8,128)(2,1)}), bf16[256,256,128]{2,1,0:T(8,128)(2,1)}) %all-gather.15.cloned.1.call-update) | async-done | bytes 16777232 | tf_op jit(solution)/shard_map/all_gather | solution.py:101
  724.0 23.1 %copy.1248 = bf16[256,256,128]{1,0,2:T(8,128)(2,1)} copy(bf16[256,256,128]{2,1,0:T(8,128)(2,1)} %all-gather.15.cloned.1.call-done) | data formatting | bytes 33554432 | tf_op jit(solution)/shard_map/all_gather | solution.py:101
  763.7 22.1 %all_gather.48 = bf16[4,256,256]{2,0,1:T(4,128)(2,1)S(1)} all-gather(bf16[4,32,256]{2,0,1:T(4,128)(2,1)S(1)} %fusion.311), channel_id=1, replica_groups=mesh['req'=2,'dap'=8] {'dap'}, dimensions={1}, use_global_device_ids=true | all-gather | bytes 589824 | tf_op jit(solution)/shard_map/all_gather | solution.py:88
  794.7 18.3 fusion.461
  813.0 16.2 fusion.54
  851.8 19.0 all-to-all-done.3
  894.5 46.6 %all_gather.49 = bf16[4,256,256]{2,0,1:T(4,128)(2,1)S(1)} all-gather(bf16[4,32,256]{2,0,1:T(4,128)(2,1)S(1)} %fusion.309), channel_id=1, replica_groups=mesh['req'=2,'dap'=8] {'dap'}, dimensions={1}, use_global_device_ids=true | all-gather | bytes 589824 | tf_op jit(solution)/shard_map/all_gather | solution.py:88
  942.5 18.5 fusion.462
  961.0 13.9 fusion.55
  1000.9 12.4 all-to-all-done.4
  1040.1 10.9 convolution_convert_fusion.1
  1088.7 33.8 %fusion.465 = (f32[32,8,256]{2,1,0:T(8,128)S(1)}, f32[32,8,256,256]{2,3,1,0:T(8,128)}) fusion(f32[8,256,256]{1,2,0:T(8,128)S(1)} %copy.1279, pred[32,256]{1,0:T(8,128)(4,1)S(1)} %copy-done.66, bf16[32,256,8,32]{1,3,2,0:T(8,128)(2,1)} %bitcast.552, bf16[32,256,8,32]{1,3,2,0:T(8,128)(2,1)} %bitcast.554), kind=kOutput, calls=%fused_computation.611 | convolution fusion | flops 1157628160 | bytes 77864960 | tf_op jit(solution)/shard_map/sub | solution.py:37
  1122.5 26.4 %fusion.28 = f32[32,8,32,256]{3,2,1,0:T(8,128)} fusion(bf16[32,256,8,32]{1,3,2,0:T(8,128)(2,1)} %bitcast.553, f32[32,8,256,256]{2,3,1,0:T(8,128)} %get-tuple-element.63, f32[32,8,256]{2,1,0:T(8,128)S(1)} %get-tuple-element.62), kind=kOutput, calls=%fused_computation.54 | convolution fusion | flops 1107296256 | bytes 79953920 | tf_op jit(solution)/shard_map/bhqk,bkhd->bqhd/dot_general | solution.py:38
  1170.0 52.4 %all_to_all.117 = bf16[32,256,256]{2,0,1:T(8,128)(2,1)S(1)} all-to-all(bf16[32,256,256]{2,0,1:T(8,128)(2,1)S(1)} %copy.1282), channel_id=1, replica_groups=mesh['req'=2,'dap'=8] {'dap'}, dimensions={1} | all-to-all | bytes 8388608 | tf_op jit(solution)/shard_map/all_to_all | solution.py:124
  1238.0 15.7 convolution_convert_fusion
  1282.4 32.3 %fusion.466 = (f32[32,8,256]{2,1,0:T(8,128)S(1)}, f32[32,8,256,256]{2,3,1,0:T(8,128)}) fusion(pred[32,256]{1,0:T(8,128)(4,1)S(1)} %copy-done.60, bf16[32,256,8,32]{1,3,2,0:T(8,128)(2,1)} %bitcast.555, bf16[32,256,8,32]{1,3,2,0:T(8,128)(2,1)} %bitcast.557), kind=kOutput, calls=%fused_computation.612 | convolution fusion | flops 1140850944 | bytes 75767808 | tf_op jit(solution)/shard_map/sub | solution.py:37
  1314.8 26.4 %fusion.29 = f32[32,8,32,256]{3,2,1,0:T(8,128)} fusion(bf16[32,256,8,32]{1,3,2,0:T(8,128)(2,1)} %bitcast.558, f32[32,8,256,256]{2,3,1,0:T(8,128)} %get-tuple-element.65, f32[32,8,256]{2,1,0:T(8,128)S(1)} %get-tuple-element.64), kind=kOutput, calls=%fused_computation.55 | convolution fusion | flops 1107296256 | bytes 79953920 | tf_op jit(solution)/shard_map/bhqk,bkhd->bqhd/dot_general | solution.py:38
  1372.5 14.4 convert_reduce_fusion.3
  1392.8 27.2 %all-gather.19.cloned.1.call-done = bf16[256,256,32]{0,2,1:T(8,128)(2,1)} async-done(((bf16[256,32,32]{0,2,1:T(8,128)(2,1)}), bf16[256,256,32]{0,2,1:T(8,128)(2,1)}) %all-gather.19.cloned.1.call-update) | async-done | bytes 4194320 | tf_op jit(solution)/shard_map/all_gather | solution.py:64
  1420.0 12.7 convert_bitcast_fusion
  1432.7 16.0 copy.1303
  1467.7 81.1 %all-gather.21.cloned.1.call-done = bf16[256,256,128]{2,1,0:T(8,128)(2,1)} async-done(((bf16[32,256,128]{2,1,0:T(8,128)(2,1)}), bf16[256,256,128]{2,1,0:T(8,128)(2,1)}) %all-gather.21.cloned.1.call-update) | async-done | bytes 16777232 | tf_op jit(solution)/shard_map/all_gather | solution.py:96
  1548.8 23.1 %copy.1313 = bf16[256,256,128]{1,0,2:T(8,128)(2,1)} copy(bf16[256,256,128]{2,1,0:T(8,128)(2,1)} %all-gather.21.cloned.1.call-done) | data formatting | bytes 33554432 | tf_op jit(solution)/shard_map/all_gather | solution.py:96
  1605.6 52.4 %all_to_all.118 = bf16[32,256,128]{2,0,1:T(8,128)(2,1)S(1)} all-to-all(bf16[32,256,128]{2,0,1:T(8,128)(2,1)} %copy.1324), channel_id=1, replica_groups=mesh['req'=2,'dap'=8] {'dap'}, dimensions={1} | all-to-all | bytes 4194304 | tf_op jit(solution)/shard_map/all_to_all | solution.py:100
  1664.1 41.6 %all-gather.23.cloned.1.call-done = bf16[256,256,128]{2,1,0:T(8,128)(2,1)} async-done(((bf16[32,256,128]{2,1,0:T(8,128)(2,1)}), bf16[256,256,128]{2,1,0:T(8,128)(2,1)}) %all-gather.23.cloned.1.call-update) | async-done | bytes 16777232 | tf_op jit(solution)/shard_map/all_gather | solution.py:101
  1705.7 23.1 %copy.1327 = bf16[256,256,128]{1,0,2:T(8,128)(2,1)} copy(bf16[256,256,128]{2,1,0:T(8,128)(2,1)} %all-gather.23.cloned.1.call-done) | data formatting | bytes 33554432 | tf_op jit(solution)/shard_map/all_gather | solution.py:101
  1750.9 22.1 %all_gather.54 = bf16[4,256,256]{2,0,1:T(4,128)(2,1)S(1)} all-gather(bf16[4,32,256]{2,0,1:T(4,128)(2,1)S(1)} %fusion.314), channel_id=1, replica_groups=mesh['req'=2,'dap'=8] {'dap'}, dimensions={1}, use_global_device_ids=true | all-gather | bytes 589824 | tf_op jit(solution)/shard_map/all_gather | solution.py:88
  1780.3 18.3 fusion.471
  1798.6 16.3 fusion.56
  1837.3 19.1 all-to-all-done.8
  1879.5 47.2 %all_gather.55 = bf16[4,256,256]{2,0,1:T(4,128)(2,1)S(1)} all-gather(bf16[4,32,256]{2,0,1:T(4,128)(2,1)S(1)} %fusion.310), channel_id=1, replica_groups=mesh['req'=2,'dap'=8] {'dap'}, dimensions={1}, use_global_device_ids=true | all-gather | bytes 589824 | tf_op jit(solution)/shard_map/all_gather | solution.py:88
  1928.1 18.5 fusion.472
  1946.7 13.9 fusion.57
  1977.0 22.1 %all-to-all-done.9 = bf16[256,32,128]{2,1,0:T(8,128)(2,1)S(1)} async-done(((bf16[256,32,128]{2,1,0:T(8,128)(2,1)}), bf16[256,32,128]{2,1,0:T(8,128)(2,1)S(1)}, u32[]{:S(2)}, u32[]{:S(2)}) %all-to-all-start.9) | async-done | bytes 2097184 | tf_op jit(solution)/shard_map/all_to_all | solution.py:108
  (444 shorter events, 663.3 us)
Async XLA Ops:
  7.2 75.1 %all-gather.9.cloned.1.call-start = ((), (), s32[]{:S(2)}) async-start(), calls=%async_computation.10 | async-start | bytes 1179648 | tf_op jit(solution)/shard_map/all_gather | solution.py:122
  10.5 5.9 copy-start.14
  13.0 6.0 copy-start.29
  50.8 6.4 copy-start.55
  82.3 153.7 %copy-start.27 = (s32[256,256]{1,0:T(8,128)}, s32[256,256]{1,0:T(8,128)S(1)}, u32[]{:S(2)}) copy-start(s32[256,256]{1,0:T(8,128)S(1)} %all_gather.42) | copy-start | bytes 786436
  82.3 35.8 %copy-start.65 = (pred[32,256]{1,0:T(8,128)(4,1)}, pred[32,256]{1,0:T(8,128)(4,1)S(1)}, u32[]{:S(2)}) copy-start(pred[32,256]{1,0:T(8,128)(4,1)S(1)} %dynamic-slice_compare_fusion) | copy-start | bytes 24580
  144.5 9.2 copy-start.75
  166.5 71.0 %all-to-all-start = ((bf16[32,256,256]{2,0,1:T(8,128)(2,1)}), bf16[32,256,256]{2,0,1:T(8,128)(2,1)}, u32[]{:S(2)}, u32[]{:S(2)}) async-start(bf16[32,256,256]{2,0,1:T(8,128)(2,1)} %copy.1198), calls=%async_computation | async-start | bytes 8388608 | tf_op jit(solution)/shard_map/all_to_all | solution.py:124
  171.4 267.3 %all-gather.11.cloned.1.call-start = ((), (), s32[]{:S(2)}) async-start(), calls=%async_computation.11 | async-start | bytes 4718592 | tf_op jit(solution)/shard_map/all_gather | solution.py:64
  237.5 62.3 %copy-start.59 = (pred[32,256]{1,0:T(8,128)(4,1)}, pred[32,256]{1,0:T(8,128)(4,1)S(1)}, u32[]{:S(2)}) copy-start(pred[32,256]{1,0:T(8,128)(4,1)S(1)} %compare_bitcast_fusion.1) | copy-start | bytes 24580
  367.9 10.0 copy-start.77
  410.5 157.0 %all-gather.13.cloned.1.call-start = ((), (), s32[]{:S(2)}) async-start(), calls=%async_computation.12 | async-start | bytes 18874368 | tf_op jit(solution)/shard_map/all_gather | solution.py:96
  411.3 198.2 %copy-start.35 = (f32[32,256]{1,0:T(8,128)}, f32[32,256]{1,0:T(8,128)S(1)}, u32[]{:S(2)}) copy-start(f32[32,256]{1,0:T(8,128)S(1)} %dynamic-slice_convert_fusion) | copy-start | bytes 98308
  411.5 55.9 %copy-start.57 = (f32[32,256]{1,0:T(8,128)}, f32[32,256]{1,0:T(8,128)S(1)}, u32[]{:S(2)}) copy-start(f32[32,256]{1,0:T(8,128)S(1)} %convolution_add_fusion) | copy-start | bytes 98308
  451.4 16.0 copy-start.15
  451.4 16.0 copy-start.73
  474.0 8.3 copy-start.8
  486.3 237.7 %all-gather.15.cloned.1.call-start = ((), (), s32[]{:S(2)}) async-start(), calls=%async_computation.13 | async-start | bytes 18874368 | tf_op jit(solution)/shard_map/all_gather | solution.py:101
  609.5 7.6 copy-start.6
  624.3 52.4 %all-to-all-start.2 = ((bf16[32,256,128]{2,0,1:T(8,128)(2,1)}), bf16[32,256,128]{2,0,1:T(8,128)(2,1)S(1)}, u32[]{:S(2)}, u32[]{:S(2)}) async-start(bf16[32,256,128]{2,0,1:T(8,128)(2,1)} %copy.1245), calls=%async_computation.2 | async-start | bytes 4194304 | tf_op jit(solution)/shard_map/all_to_all | solution.py:100
  629.1 165.6 %copy-start.63 = (pred[32,256]{1,0:T(8,128)(4,1)}, pred[32,256]{1,0:T(8,128)(4,1)S(1)}, u32[]{:S(2)}) copy-start(pred[32,256]{1,0:T(8,128)(4,1)S(1)} %dynamic-slice_compare_fusion.1) | copy-start | bytes 24580
  763.0 24.2 %copy-start.47 = (bf16[2,128,512]{2,1,0:T(8,128)(2,1)S(1)}, bf16[2,128,512]{2,1,0:T(8,128)(2,1)}, u32[]{:S(2)}) copy-start(bf16[2,128,512]{2,1,0:T(8,128)(2,1)} %param.42) | copy-start | bytes 786436
  835.4 8.4 copy-start.38
  840.0 30.8 %all-to-all-start.3 = ((bf16[32,256,128]{2,0,1:T(8,128)(2,1)}), bf16[32,256,128]{2,0,1:T(8,128)(2,1)S(1)}, u32[]{:S(2)}, u32[]{:S(2)}) async-start(bf16[32,256,128]{2,0,1:T(8,128)(2,1)} %copy.1260), calls=%async_computation.3 | async-start | bytes 4194304 | tf_op jit(solution)/shard_map/all_to_all | solution.py:105
  843.9 98.5 %copy-start.61 = (pred[32,256]{1,0:T(8,128)(4,1)}, pred[32,256]{1,0:T(8,128)(4,1)S(1)}, u32[]{:S(2)}) copy-start(pred[32,256]{1,0:T(8,128)(4,1)S(1)} %compare_bitcast_fusion) | copy-start | bytes 24580
  870.8 111.7 %all-to-all-start.1 = ((bf16[256,32,256]{2,1,0:T(8,128)(2,1)}), bf16[256,32,256]{2,1,0:T(8,128)(2,1)}, u32[]{:S(2)}, u32[]{:S(2)}) async-start(bf16[256,32,256]{2,1,0:T(8,128)(2,1)} %copy.1216), calls=%async_computation.1 | async-start | bytes 8388608 | tf_op jit(solution)/shard_map/all_to_all | solution.py:131
  982.4 30.8 %all-to-all-start.4 = ((bf16[256,32,128]{2,1,0:T(8,128)(2,1)}), bf16[256,32,128]{2,1,0:T(8,128)(2,1)S(1)}, u32[]{:S(2)}, u32[]{:S(2)}) async-start(bf16[256,32,128]{2,1,0:T(8,128)(2,1)} %copy.1269), calls=%async_computation.4 | async-start | bytes 4194304 | tf_op jit(solution)/shard_map/all_to_all | solution.py:108
  986.3 100.6 %all-gather.17.cloned.1.call-start = ((), (), s32[]{:S(2)}) async-start(), calls=%async_computation.14 | async-start | bytes 1179648 | tf_op jit(solution)/shard_map/all_gather | solution.py:122
  1030.1 8.6 copy-start.90
  1038.0 13.0 copy-start.24
  1040.0 380.0 %all-gather.19.cloned.1.call-start = ((), (), s32[]{:S(2)}) async-start(), calls=%async_computation.15 | async-start | bytes 4718592 | tf_op jit(solution)/shard_map/all_gather | solution.py:64
  1082.7 6.0 copy-start.66
  1149.0 9.2 copy-start.76
  1276.0 6.4 copy-start.60
  1350.2 10.0 copy-start.78
  1392.7 156.1 %all-gather.21.cloned.1.call-start = ((), (), s32[]{:S(2)}) async-start(), calls=%async_computation.16 | async-start | bytes 18874368 | tf_op jit(solution)/shard_map/all_gather | solution.py:96
  1432.7 16.0 copy-start.25
  1432.7 16.0 copy-start.58
  1432.7 16.0 copy-start.74
  1455.3 8.3 copy-start.9
  1467.7 238.0 %all-gather.23.cloned.1.call-start = ((), (), s32[]{:S(2)}) async-start(), calls=%async_computation.17 | async-start | bytes 18874368 | tf_op jit(solution)/shard_map/all_gather | solution.py:101
  1590.8 7.6 copy-start.7
  1774.4 5.9 copy-start.32
  1774.4 5.9 copy-start.64
  1825.7 30.8 %all-to-all-start.8 = ((bf16[32,256,128]{2,0,1:T(8,128)(2,1)}), bf16[32,256,128]{2,0,1:T(8,128)(2,1)S(1)}, u32[]{:S(2)}, u32[]{:S(2)}) async-start(bf16[32,256,128]{2,0,1:T(8,128)(2,1)} %copy.1339), calls=%async_computation.8 | async-start | bytes 4194304 | tf_op jit(solution)/shard_map/all_to_all | solution.py:105
  1856.5 111.7 %all-to-all-start.6 = ((bf16[256,32,256]{2,1,0:T(8,128)(2,1)}), bf16[256,32,256]{2,1,0:T(8,128)(2,1)}, u32[]{:S(2)}, u32[]{:S(2)}) async-start(bf16[256,32,256]{2,1,0:T(8,128)(2,1)} %copy.1299), calls=%async_computation.6 | async-start | bytes 8388608 | tf_op jit(solution)/shard_map/all_to_all | solution.py:131
  1879.5 48.6 %copy-start.62 = (pred[32,256]{1,0:T(8,128)(4,1)S(1)}, pred[32,256]{1,0:T(8,128)(4,1)}, u32[]{:S(2)}) copy-start(pred[32,256]{1,0:T(8,128)(4,1)} %copy-done.61) | copy-start | bytes 24580
  1968.1 31.0 %all-to-all-start.9 = ((bf16[256,32,128]{2,1,0:T(8,128)(2,1)}), bf16[256,32,128]{2,1,0:T(8,128)(2,1)S(1)}, u32[]{:S(2)}, u32[]{:S(2)}) async-start(bf16[256,32,128]{2,1,0:T(8,128)(2,1)} %copy.1347), calls=%async_computation.9 | async-start | bytes 4194304 | tf_op jit(solution)/shard_map/all_to_all | solution.py:108
  (61 other events, 210.0 us)
Sparse Core Ops, SparseCore 0:
  13.1 21.8 all-gather.8
  410.6 28.0 all-gather.10
  486.4 80.9 all-gather.12
  621.3 102.6 all-gather.14
  1040.1 18.3 all-gather.16
  1392.8 27.1 all-gather.18
  1467.8 80.9 all-gather.20
  1602.7 102.9 all-gather.22
where the time goes:
time: 2040 us; the launch traced here: 2020 us
  matrix products  627 us (31%)
  local copies, waits for them, and re-layouts  459 us (22%)
  waiting for transfers between devices  420 us (21%)
  blocking collectives  332 us (16%)
  other arithmetic  135 us (7%)
  starting transfers between devices  35.1 us (2%)
    all_gather x4, waiting for transfers between devices, pair_stack(): right_full = lax.all_gather(right_act, GROUP_AXIS, axis=0, tiled=True)  245 us
    sub x8, matrix products, attend(): attn_prob = jax.nn.softmax(logits, axis=-1).astype(jnp.bfloat16)  206 us
    dot_general x32, matrix products, dense(): jnp.einsum('...c,cf->...f', x, weight, preferred_element_type=jnp.float32)  187 us
    dot_general x8, matrix products, attend(): jnp.einsum('bhqk,bkhd->bqhd', attn_prob, v_heads, preferred_element_type=...  166 us
    all_gather x4, blocking collectives, tri_attention(): lax.all_gather(head_bias(pair_norm, w_bias), GROUP_AXIS, axis=1, tiled=True)  138 us
    all_gather x4, local copies, waits for them, and re-layouts, pair_stack(): right_full = lax.all_gather(right_act, GROUP_AXIS, axis=0, tiled=True)  92.3 us
    convert_element_type x18, local copies, waits for them, and re-layouts, residual(): return (x.astype(jnp.float32) + update).astype(jnp.bfloat16)  80 us
    slice x12, local copies, waits for them, and re-layouts, attend(): keyvals[..., :head_width].reshape(n_batch, k_len, num_heads, head_dim)  77.9 us
  transfers between devices with their start and end apart: 16, of which 11 were waited for; matrix products, arithmetic and copies ran while one was open for 13% of the time, Pallas kernels for 0%

commit v1 on v0

v1 whole, which is shorter than its diff:
```python
import functools
import math

import jax
import jax.numpy as jnp
from jax import lax
from jax.experimental import pallas as pl
from jax.experimental.pallas import tpu as pltpu
from jax.sharding import PartitionSpec as P

GROUP_AXIS = 'dap'
PARTS_AXIS = 'req'
LOG2E = math.log2(math.e)
MASKED = -1e9 * LOG2E
F32, BF16 = jnp.float32, jnp.bfloat16
VMEM_LIMIT = 60 * 1024 * 1024


def nn(a, b):
    return lax.dot_general(a, b, (((1,), (0,)), ((), ())), preferred_element_type=F32)


def nt(a, b):
    return lax.dot_general(a, b, (((1,), (1,)), ((), ())), preferred_element_type=F32)


def tn(a, b):
    return lax.dot_general(a, b, (((0,), (0,)), ((), ())), preferred_element_type=F32)


def norm(x):
    centered = x - jnp.mean(x, axis=-1, keepdims=True)
    variance = jnp.mean(centered * centered, axis=-1, keepdims=True)
    return (centered * lax.rsqrt(variance + 1e-5)).astype(BF16)


def flip(w):
    return w.astype(F32).T.astype(w.dtype)


def key_column(mask_row):
    return jnp.broadcast_to(mask_row, (128, mask_row.shape[1])).T


def project_row(r, x_norm, mask_row, wt_ref, proj_s, keep_s):
    proj_s[r] = nt(wt_ref[...], x_norm).astype(BF16)
    keep_s[r] = key_column(mask_row)


def attend_row(r, proj_s, keep_s, gated_s, bias_ref, heads):
    width, length = gated_s.shape[1:]
    dim = width // heads
    column = keep_s[r]
    kept = jnp.concatenate([column] * (length // 128), axis=1) > 0

    def part(n, h):
        return proj_s[r, n * width + h * dim:n * width + (h + 1) * dim, :]

    def scores(h):
        logits = tn(part(1, h), part(0, h)) * (dim ** -0.5 * LOG2E)
        if bias_ref is not None:
            logits = logits + bias_ref[h]
        return jnp.where(kept, logits, MASKED)

    def weigh(logits):
        expd = jnp.exp2(logits - jnp.max(logits, axis=0, keepdims=True))
        return (expd * (1.0 / jnp.sum(expd, axis=0, keepdims=True))).astype(BF16)

    def gate(h, probs):
        gated = nn(part(2, h), probs) * jax.nn.sigmoid(part(3, h).astype(F32))
        gated_s[r, h * dim:(h + 1) * dim, :] = gated.astype(BF16)

    probs = None
    ahead = scores(0)
    for h in range(heads):
        logits, ahead = ahead, scores(h + 1) if h + 1 < heads else None
        if probs is not None:
            gate(h - 1, probs)
        probs = weigh(logits)
    gate(heads - 1, probs)


def attend_rows(rows, proj_s, keep_s, gated_s, bias_ref, heads):
    def body(r, carry):
        attend_row(r, proj_s, keep_s, gated_s, bias_ref, heads)
        return carry
    lax.fori_loop(0, rows, body, 0)


def attention_scratch(rows, length, w, w_out):
    return [pltpu.VMEM((rows, w.shape[1], length), BF16), pltpu.VMEM((rows, length, 128), F32),
            pltpu.VMEM((rows, w_out.shape[0], length), BF16)]


def each(count, body, unroll=1):
    def step(n, carry):
        body(n)
        return carry
    lax.fori_loop(0, count, step, 0, unroll=unroll)


def load_bias(bias_ref, bias_s, transposed):
    for h in range(bias_s.shape[0]):
        bias = bias_ref[h].astype(F32) * LOG2E
        bias_s[h] = bias.T if transposed else bias


def transition(x, w_in_ref, w_out_ref):
    hidden = jnp.maximum(nn(norm(x), w_in_ref[...]), 0.0).astype(BF16)
    return nn(hidden, w_out_ref[...])


def residual(x, update):
    total = (x + update).astype(BF16)
    return total, total.astype(F32)


def rows_of(ref, start, count, step):
    return ref[pl.ds(start, count, stride=step), :]


def call(kernel, grid, in_specs, out_specs, out_shape, scratch, flops):
    return pl.pallas_call(
        kernel, grid=grid, in_specs=in_specs, out_specs=out_specs, out_shape=out_shape, scratch_shapes=scratch,
        compiler_params=pltpu.CompilerParams(vmem_limit_bytes=VMEM_LIMIT),
        cost_estimate=pl.CostEstimate(flops=flops, bytes_accessed=1 << 24, transcendentals=0))


def full_spec(array):
    zeros = (0,) * array.ndim
    return pl.BlockSpec(array.shape, lambda n: zeros)


def lead_spec(block, axis):
    return pl.BlockSpec(block, lambda n: tuple(n if d == axis else 0 for d in range(len(block))))


def bias_rows(store, n, x_norm, wbt_ref):
    values = nt(wbt_ref[...], x_norm)
    for t in range(store.shape[0]):
        store[t, pl.ds(pl.multiple_of(n * 8, 8), 8), :] = values[:, t * 128:(t + 1) * 128]


def bias_scratch(rows, length):
    return pltpu.VMEM((length // 128, rows * 8, 128), F32)


def write_bias(out_ref, store, rows):
    for h in range(out_ref.shape[0]):
        out_ref[h] = take_row(store, h, rows, 8).astype(BF16)


def bias_kernel(z_ref, wbt_ref, out_ref, store):
    rows = z_ref.shape[0]

    def body(n, carry):
        bias_rows(store, n, norm(z_ref[n].astype(F32)), wbt_ref)
        return carry
    lax.fori_loop(0, rows, body, 0)
    write_bias(out_ref, store, rows)


def pair_bias(z, wbt, heads):
    rows, length, _ = z.shape
    return call(bias_kernel, (1,), [full_spec(z), full_spec(wbt)], lead_spec((heads, rows, length), 1),
                jax.ShapeDtypeStruct((heads, rows, length), BF16), [bias_scratch(rows, length)], 10 ** 8)(z, wbt)


def row_kernel(transposed, heads, m_ref, mask_ref, bias_ref, w_ref, w_out_ref, out_ref, bias_s, wt_s, proj_s, keep_s, gated_s):
    rows = m_ref.shape[0]

    @pl.when(pl.program_id(0) == 0)
    def _():
        load_bias(bias_ref, bias_s, transposed)
        wt_s[...] = flip(w_ref[...])

    def project(s):
        project_row(s, norm(m_ref[s].astype(F32)), mask_ref[pl.ds(s, 1), :], wt_s, proj_s, keep_s)
    each(rows, project, 2)
    attend_rows(rows, proj_s, keep_s, gated_s, bias_s, heads)

    def finish(s):
        out_ref[s] = residual(m_ref[s].astype(F32), tn(gated_s[s], w_out_ref[...]))[0]
    each(rows, finish, 2)


def row_attention(m, mask, bias, transposed, w, w_out):
    seqs, length, chans = m.shape
    heads = bias.shape[0]
    block = 8
    return call(functools.partial(row_kernel, transposed, heads), (seqs // block,),
                [lead_spec((block, length, chans), 0), lead_spec((block, length), 0), full_spec(bias), full_spec(w), full_spec(w_out)],
                lead_spec((block, length, chans), 0), jax.ShapeDtypeStruct(m.shape, BF16),
                [pltpu.VMEM((heads, length, length), F32), pltpu.VMEM(w.shape[::-1], BF16)] + attention_scratch(block, length, w, w_out),
                2 * 10 ** 10)(m, mask, bias, w, w_out)


def split_store(dst, x):
    seqs, rows, chans = x.shape
    flat = x.astype(F32).reshape(seqs * rows, chans)
    for t in range(chans // 128):
        dst[t] = flat[:, t * 128:(t + 1) * 128]


def take_row(src, r, count, step):
    return jnp.concatenate([src[t, pl.ds(r, count, stride=step), :] for t in range(src.shape[0])], axis=1)


def put_row(dst, r, count, step, value):
    for t in range(dst.shape[0]):
        dst[t, pl.ds(r, count, stride=step), :] = value[:, t * 128:(t + 1) * 128]


def join_store(src, shape):
    seqs, rows, chans = shape
    return jnp.concatenate([src[t] for t in range(src.shape[0])], axis=1).reshape(seqs, rows, chans).astype(BF16)


def col_kernel(heads, m_ref, mask_ref, w_ref, w_out_ref, tin_ref, tout_ref, op_ref, out_ref, a_ref, b_ref, x_s, b_s, wt_s, opt_s, proj_s, keep_s, gated_s):
    seqs, rows, chans = m_ref.shape
    dim = op_ref.shape[1] // 2

    @pl.when(pl.program_id(0) == 0)
    def _():
        wt_s[...] = flip(w_ref[...])
        opt_s[...] = flip(op_ref[...])
    split_store(x_s, m_ref[...])

    def project(r):
        project_row(r, norm(take_row(x_s, r, seqs, rows)), mask_ref[pl.ds(r, 1), :], wt_s, proj_s, keep_s)
    each(rows, project, 2)
    attend_rows(rows, proj_s, keep_s, gated_s, None, heads)

    def finish(r):
        mask_row = mask_ref[pl.ds(r, 1), :]
        x = take_row(x_s, r, seqs, rows)
        x = residual(x, tn(gated_s[r], w_out_ref[...]))[1]
        x = residual(x, transition(x, tin_ref, tout_ref))[1]
        put_row(x_s, r, seqs, rows, x)
        proj = nt(opt_s[...], norm(x)).astype(BF16).astype(F32) * mask_row
        a_ref[r] = proj[:dim].astype(BF16)
        for t in range(seqs // 128):
            b_s[t, pl.ds(r, dim, stride=rows), :] = proj[dim:, t * 128:(t + 1) * 128]
    each(rows, finish)
    out_ref[...] = join_store(x_s, m_ref.shape)
    b_ref[...] = join_store(b_s, b_ref.shape)


def column_block(m, mask_t, heads, w, w_out, t_in, t_out, o_proj):
    seqs, rows, chans = m.shape
    dim = o_proj.shape[1] // 2
    block = 16
    weights = (w, w_out, t_in, t_out, o_proj)
    return call(functools.partial(col_kernel, heads), (rows // block,),
                [lead_spec((seqs, block, chans), 1), lead_spec((block, seqs), 0)] + [full_spec(x) for x in weights],
                [lead_spec((seqs, block, chans), 1), lead_spec((block, dim, seqs), 0), lead_spec((dim, block, seqs), 1)],
                [jax.ShapeDtypeStruct(m.shape, BF16), jax.ShapeDtypeStruct((rows, dim, seqs), BF16), jax.ShapeDtypeStruct((dim, rows, seqs), BF16)],
                [pltpu.VMEM((chans // 128, seqs * block, 128), F32), pltpu.VMEM((seqs // 128, dim * block, 128), F32),
                 pltpu.VMEM(w.shape[::-1], BF16), pltpu.VMEM(o_proj.shape[::-1], BF16)] + attention_scratch(block, seqs, w, w_out),
                3 * 10 ** 10)(m, mask_t, *weights)


def gate_parts(z_norm, mask_row, wt_ref, tri):
    proj = nt(wt_ref[pl.ds(0, 4 * tri), :], z_norm)
    left = mask_row * jax.nn.sigmoid(proj[2 * tri:3 * tri]) * proj[:tri]
    right = mask_row * jax.nn.sigmoid(proj[3 * tri:]) * proj[tri:2 * tri]
    return left, right


def put_channels(dst, n, step, value):
    for t in range(dst.shape[0]):
        dst[t, pl.ds(n, value.shape[0], stride=step), :] = value[:, t * 128:(t + 1) * 128]


def opm_kernel(a_ref, b_ref, z_ref, rmask_ref, fmask_ref, pmask_ref, w_ref, proj_ref,
               z_out, l_out, r_out, wf_s, wt_s, gt_s, o_s, scale_s, l_s, r_s):
    rows, dim, seqs = a_ref.shape
    tri = l_out.shape[0]

    @pl.when(pl.program_id(0) == 0)
    def _():
        gt_s[...] = flip(proj_ref[...])
        wf_s[...] = w_ref[...].astype(F32)
        swapped = [rows_of(wf_s, e, dim, dim) for e in range(dim)]
        wt_s[...] = jnp.concatenate(swapped, axis=0).T.astype(BF16)
    scale_s[...] = 1.0 / (1e-3 + nt(rmask_ref[...].astype(BF16), fmask_ref[...].astype(BF16)))

    def outer(e, carry):
        prod = nt(a_ref[...].reshape(rows * dim, seqs), b_ref[e]).astype(BF16)
        for i in range(rows):
            o_s[i, pl.ds(pl.multiple_of(e * dim, dim), dim), :] = prod[i * dim:(i + 1) * dim]
        return carry
    lax.fori_loop(0, dim, outer, 0, unroll=2)

    def finish(i, carry):
        update = (nn(wt_s[...], o_s[i]) * scale_s[pl.ds(i, 1), :]).T
        total, total_f = residual(z_ref[i].astype(F32), update)
        z_out[i] = total
        left, right = gate_parts(norm(total_f), pmask_ref[pl.ds(i, 1), :], gt_s, tri)
        put_channels(l_s, i, rows, left)
        put_channels(r_s, i, rows, right)
        return carry
    lax.fori_loop(0, rows, finish, 0)
    l_out[...] = join_store(l_s, l_out.shape)
    r_out[...] = join_store(r_s, r_out.shape)


def outer_block(a, b_full, z, rmask, fmask, pmask, w_out, tri_proj):
    rows, dim, seqs = a.shape
    length, out_dim = z.shape[1:]
    tri = (tri_proj.shape[1] - out_dim) // 4
    block = 16
    consts = (w_out, tri_proj)
    chan_shape = jax.ShapeDtypeStruct((tri, rows, length), BF16)
    chan_scratch = pltpu.VMEM((length // 128, tri * block, 128), F32)
    return call(opm_kernel, (rows // block,),
                [lead_spec((block, dim, seqs), 0), full_spec(b_full), lead_spec((block, length, out_dim), 0), lead_spec((block, seqs), 0),
                 full_spec(fmask), lead_spec((block, length), 0)] + [full_spec(x) for x in consts],
                [lead_spec((block, length, out_dim), 0), lead_spec((tri, block, length), 1), lead_spec((tri, block, length), 1)],
                [jax.ShapeDtypeStruct(z.shape, BF16), chan_shape, chan_shape],
                [pltpu.VMEM(w_out.shape, F32), pltpu.VMEM(w_out.shape[::-1], BF16), pltpu.VMEM(tri_proj.shape[::-1], BF16),
                 pltpu.VMEM((block, dim * dim, length), BF16), pltpu.VMEM((block, length), F32), chan_scratch, chan_scratch],
                10 ** 10)(a, b_full, z, rmask, fmask, pmask, *consts)


def put_product(x_s, c, rows, prod):
    for t in range(x_s.shape[0]):
        x_s[t, pl.ds(pl.multiple_of(c * rows, rows), rows), :] = prod[:, t * 128:(t + 1) * 128]


def tri_finish(x_s, z, i, rows, proj_ref, w_out_ref):
    out_dim = z.shape[1]
    chans = w_out_ref.shape[0]
    x = take_row(x_s, i, chans, rows)
    centered = x - jnp.mean(x, axis=0, keepdims=True)
    variance = jnp.mean(centered * centered, axis=0, keepdims=True)
    x_norm = (centered * lax.rsqrt(variance + 1e-5)).astype(BF16)
    gate = jax.nn.sigmoid(nn(norm(z), proj_ref[:, 4 * chans:4 * chans + out_dim]))
    return residual(z, gate * tn(x_norm, w_out_ref[...]))


def outgoing_kernel(a_ref, b_ref, z_ref, pmask_ref, proj_ref, w_out_ref, next_ref, z_out, l_out, r_out, x_s, r_s, gt_s):
    step, steps = pl.program_id(0), pl.num_programs(0)
    block, rows, _ = a_ref.shape
    tri = w_out_ref.shape[0]

    def product(c, carry):
        put_product(x_s, step * block + c, rows, nt(a_ref[c], b_ref[c]))
        return carry
    lax.fori_loop(0, block, product, 0, unroll=4)

    @pl.when(step == steps - 1)
    def _():
        gt_s[...] = flip(next_ref[...])

        def finish(i, carry):
            total, total_f = tri_finish(x_s, z_ref[i].astype(F32), i, rows, proj_ref, w_out_ref)
            z_out[i] = total
            z_norm = norm(total_f)
            mask_row = pmask_ref[pl.ds(i, 1), :]
            value = nn(z_norm, next_ref[:, :tri])
            value_gate = nn(z_norm, next_ref[:, 2 * tri:3 * tri])
            l_out[i] = (key_column(mask_row) * jax.nn.sigmoid(value_gate) * value).astype(BF16)
            right = nt(gt_s[pl.ds(tri, tri), :], z_norm)
            right_gate = nt(gt_s[pl.ds(3 * tri, tri), :], z_norm)
            put_channels(r_s, i, rows, mask_row * jax.nn.sigmoid(right_gate) * right)
            return carry
        lax.fori_loop(0, rows, finish, 0)
        r_out[...] = join_store(r_s, r_out.shape)


def outgoing(a, b_full, z, pmask, proj, w_out, next_proj):
    tri, rows, length = a.shape
    block = 16
    consts = (z, pmask, proj, w_out, next_proj)
    scratch = pltpu.VMEM((length // 128, tri * rows, 128), F32)
    outs = [jax.ShapeDtypeStruct(z.shape, BF16), jax.ShapeDtypeStruct((rows, length, tri), BF16), jax.ShapeDtypeStruct((tri, rows, length), BF16)]
    return call(outgoing_kernel, (tri // block,),
                [lead_spec((block, rows, length), 0), lead_spec((block, length, length), 0)] + [full_spec(x) for x in consts],
                [full_spec(x) for x in outs], outs, [scratch, scratch, pltpu.VMEM(next_proj.shape[::-1], BF16)], 10 ** 10)(a, b_full, *consts)


def incoming_kernel(a_ref, b_ref, z_ref, proj_ref, w_out_ref, wbt_ref, z_out, bias_out, af_s, a_s, x_s, bias_s):
    step, steps = pl.program_id(0), pl.num_programs(0)
    block = b_ref.shape[0]
    length, rows, tri = a_ref.shape

    @pl.when(step == 0)
    def _():
        af_s[...] = a_ref[...].astype(F32).reshape(length * rows, tri)

        def turn(i, carry):
            put_channels(a_s, i, rows, rows_of(af_s, i, length, rows).T)
            return carry
        lax.fori_loop(0, rows, turn, 0)

    def product(c, carry):
        place = pl.ds(pl.multiple_of((step * block + c) * rows, rows), rows)
        left = jnp.concatenate([a_s[t, place, :] for t in range(a_s.shape[0])], axis=1).astype(BF16)
        put_product(x_s, step * block + c, rows, nn(left, b_ref[c]))
        return carry
    lax.fori_loop(0, block, product, 0, unroll=4)

    @pl.when(step == steps - 1)
    def _():
        def finish(i, carry):
            total, total_f = tri_finish(x_s, z_ref[i].astype(F32), i, rows, proj_ref, w_out_ref)
            z_out[i] = total
            bias_rows(bias_s, i, norm(total_f), wbt_ref)
            return carry
        lax.fori_loop(0, rows, finish, 0)
        write_bias(bias_out, bias_s, rows)


def incoming(a, b_full, z, proj, w_out, wbt, heads):
    length, rows, tri = a.shape
    block = 16
    consts = (z, proj, w_out, wbt)
    scratch = pltpu.VMEM((length // 128, tri * rows, 128), F32)
    outs = [jax.ShapeDtypeStruct(z.shape, BF16), jax.ShapeDtypeStruct((heads, rows, length), BF16)]
    return call(incoming_kernel, (tri // block,),
                [full_spec(a), lead_spec((block, length, length), 0)] + [full_spec(x) for x in consts],
                [full_spec(x) for x in outs], outs,
                [pltpu.VMEM((length * rows, tri), F32), scratch, scratch, bias_scratch(rows, length)],
                10 ** 10)(a, b_full, *consts)


def start_kernel(heads, z_ref, mask_ref, bias_ref, w_ref, w_out_ref, wbt_ref, z_out, bias_out, bias_s, wt_s, next_s, proj_s, keep_s, gated_s):
    rows = z_ref.shape[0]

    @pl.when(pl.program_id(0) == 0)
    def _():
        load_bias(bias_ref, bias_s, True)
        wt_s[...] = flip(w_ref[...])

    def project(i):
        project_row(i, norm(z_ref[i].astype(F32)), mask_ref[pl.ds(i, 1), :], wt_s, proj_s, keep_s)
    each(rows, project, 4)
    attend_rows(rows, proj_s, keep_s, gated_s, bias_s, heads)

    def finish(i):
        total, total_f = residual(z_ref[i].astype(F32), tn(gated_s[i], w_out_ref[...]))
        z_out[i] = total
        bias_rows(next_s, i, norm(total_f), wbt_ref)
    each(rows, finish, 4)
    write_bias(bias_out, next_s, rows)


def start_attention(z, mask, bias, w, w_out, wbt):
    rows, length, chans = z.shape
    heads = bias.shape[0]
    block = 16
    consts = (bias, w, w_out, wbt)
    return call(functools.partial(start_kernel, heads), (rows // block,),
                [lead_spec((block, length, chans), 0), lead_spec((block, length), 0)] + [full_spec(x) for x in consts],
                [lead_spec((block, length, chans), 0), lead_spec((heads, block, length), 1)],
                [jax.ShapeDtypeStruct(z.shape, BF16), jax.ShapeDtypeStruct((heads, rows, length), BF16)],
                [pltpu.VMEM((heads, length, length), F32), pltpu.VMEM(w.shape[::-1], BF16), bias_scratch(block, length)]
                + attention_scratch(block, length, w, w_out), 10 ** 10)(z, mask, *consts)


def end_kernel(heads, z_ref, mask_ref, bias_ref, w_ref, w_out_ref, tin_ref, tout_ref, wbt_ref, z_out, bias_out, x_s, bias_s, wt_s, next_s, proj_s, keep_s, gated_s):
    length, cols, chans = z_ref.shape

    @pl.when(pl.program_id(0) == 0)
    def _():
        load_bias(bias_ref, bias_s, False)
        wt_s[...] = flip(w_ref[...])
    split_store(x_s, z_ref[...])

    def project(j):
        project_row(j, norm(take_row(x_s, j, length, cols)), mask_ref[pl.ds(j, 1), :], wt_s, proj_s, keep_s)
    each(cols, project, 4)
    attend_rows(cols, proj_s, keep_s, gated_s, bias_s, heads)

    def finish(j):
        x = take_row(x_s, j, length, cols)
        x = residual(x, tn(gated_s[j], w_out_ref[...]))[1]
        x = residual(x, transition(x, tin_ref, tout_ref))[1]
        put_row(x_s, j, length, cols, x)
        bias_rows(next_s, j, norm(x), wbt_ref)
    each(cols, finish, 2)
    z_out[...] = join_store(x_s, z_ref.shape)
    write_bias(bias_out, next_s, cols)


def end_attention(z, mask_t, bias, w, w_out, t_in, t_out, wbt, next_heads):
    length, cols, chans = z.shape
    heads = bias.shape[0]
    block = 16
    consts = (bias, w, w_out, t_in, t_out, wbt)
    return call(functools.partial(end_kernel, heads), (cols // block,),
                [lead_spec((length, block, chans), 1), lead_spec((block, length), 0)] + [full_spec(x) for x in consts],
                [lead_spec((length, block, chans), 1), lead_spec((next_heads, block, length), 1)],
                [jax.ShapeDtypeStruct(z.shape, BF16), jax.ShapeDtypeStruct((next_heads, cols, length), BF16)],
                [pltpu.VMEM((chans // 128, length * block, 128), F32), pltpu.VMEM((heads, length, length), F32),
                 pltpu.VMEM(w.shape[::-1], BF16), bias_scratch(block, length)] + attention_scratch(block, length, w, w_out),
                10 ** 10)(z, mask_t, *consts)


def gather(x, axis):
    return lax.all_gather(x, GROUP_AXIS, axis=axis, tiled=True)


def exchange(x, split, concat):
    return lax.all_to_all(x, GROUP_AXIS, split, concat, tiled=True)


def bias_weight(w):
    return jnp.pad(w.T, ((0, 8 - w.shape[1]), (0, 0)))


def solution(mesh):
    row_spec = P((PARTS_AXIS, GROUP_AXIS))

    def local_body(m, z, msa_mask, pair_mask, *weights):
        layers = weights[0].shape[0]
        seq_loc, res_loc = m.shape[0], z.shape[0]
        shard = lax.axis_index(GROUP_AXIS)
        heads = weights[1].shape[2]
        pair_heads = weights[14].shape[2]
        row_bias_w = [bias_weight(weights[1][n]) for n in range(layers)]
        seq_mask, row_mask = msa_mask.astype(F32), pair_mask.astype(F32)
        bias = pair_bias(z, row_bias_w[0], heads)
        packed = gather(jnp.concatenate([bias, msa_mask.astype(BF16)[None], pair_mask.astype(BF16)[None]]), 1)
        bias = packed[:heads]
        masks_t = jnp.swapaxes(packed[heads:].astype(F32), 1, 2)
        full_mask_t = masks_t[0]
        res_mask_t, col_mask = (lax.dynamic_slice_in_dim(x, shard * res_loc, res_loc, 0) for x in masks_t)
        for n in range(layers):
            (row_qkvg, _, row_out, col_qkvg, col_out, mtr_in, mtr_out, opm_proj, opm_out, tmo_proj, tmo_out, tmi_proj, tmi_out,
             tas_qkvg, tas_bias, tas_out, tae_qkvg, tae_bias, tae_out, ptr_in, ptr_out) = (weight[n] for weight in weights)
            m = row_attention(m, seq_mask, bias, n == 0, row_qkvg, row_out)
            m = exchange(m, 1, 0)
            m, left, right = column_block(m, res_mask_t, heads, col_qkvg, col_out, mtr_in, mtr_out, opm_proj)
            right = gather(right, 1)
            m = exchange(m, 0, 1)
            z, left, right = outer_block(left, right, z, res_mask_t, full_mask_t, row_mask, opm_out, tmo_proj)
            z, left, right = outgoing(left, gather(right, 1), z, row_mask, tmo_proj, tmo_out, tmi_proj)
            z, bias = incoming(exchange(left, 1, 0), gather(right, 1), z, tmi_proj, tmi_out, bias_weight(tas_bias), pair_heads)
            z, bias = start_attention(z, row_mask, gather(bias, 1), tas_qkvg, tas_out, bias_weight(tae_bias))
            bias = gather(bias, 1)
            z, bias = end_attention(exchange(z, 1, 0), col_mask, bias, tae_qkvg, tae_out, ptr_in, ptr_out,
                                    row_bias_w[min(n + 1, layers - 1)], heads)
            if n < layers - 1:
                bias = gather(bias, 1)
            z = exchange(z, 0, 1)
        return m, z

    def run_blocks(*arrays):
        n_weights = len(arrays) - 4
        return jax.shard_map(local_body, mesh=mesh, in_specs=(row_spec,) * 4 + (P(),) * n_weights, out_specs=(row_spec, row_spec), check_vma=False)(*arrays)

    return run_blocks
```

time: 2040 us -> 1740 us (0.85)
  Pallas kernels: 0 us -> 802 us
  matrix products: 627 us -> 0 us
  local copies, waits for them, and re-layouts: 459 us -> 85.4 us
  other arithmetic: 135 us -> 3.09 us
  waiting for transfers between devices: 420 us -> 518 us
  blocking collectives: 332 us -> 279 us
    pallas_call x0 -> x15, Pallas kernels: none -> 802 us  [the longest x2 197 us: column_block(): call(functools.partial(col_kernel, heads), (rows // block,), [lead_spec((...]
    dot_general x53 -> x0, matrix products: 420 us -> none  [the longest x32 187 us: dense(): jnp.einsum('...c,cf->...f', x, weight, preferred_element_type=jnp.float32)]
    sub x8 -> x0, matrix products: 206 us -> none  [attend(): attn_prob = jax.nn.softmax(logits, axis=-1).astype(jnp.bfloat16)]
    convert_element_type x35 -> x0, local copies, waits for them, and re-layouts: 150 us -> none  [the longest x18 80 us: residual(): return (x.astype(jnp.float32) + update).astype(jnp.bfloat16)]
    slice x20 -> x4, local copies, waits for them, and re-layouts: 129 us -> 2.27 us  [the longest x1 2.26 us: local_body(): bias = packed[:heads]]
    all_gather x4 -> x0, local copies, waits for them, and re-layouts: 92.3 us -> none  [pair_stack(): right_full = lax.all_gather(right_act, GROUP_AXIS, axis=0, tiled=True)]
    all_to_all x8 -> x7, waiting for transfers between devices: 120 us -> 209 us  [exchange(): return lax.all_to_all(x, GROUP_AXIS, split, concat, tiled=True)]
    convert_element_type x28 -> x0, other arithmetic: 61.1 us -> none  [the longest x9 17.6 us: layer_norm(): return (centered * lax.rsqrt(variance + 1e-05)).astype(jnp.bfloat16)]
  transfers between devices with their start and end apart: 16 -> 15, of which waited for: 11 -> 12; matrix products, arithmetic and copies ran while one was open for 13% -> 3% of each run, Pallas kernels for 0% -> 7%
where the time goes in v1:
time: 1740 us; the launch traced here: 1730 us
  Pallas kernels  802 us (46%)
  waiting for transfers between devices  518 us (30%)
  blocking collectives  279 us (16%)
  local copies, waits for them, and re-layouts  85.4 us (5%)
  starting transfers between devices  32.2 us (2%)
    all_gather x8, waiting for transfers between devices, gather(): return lax.all_gather(x, GROUP_AXIS, axis=axis, tiled=True)  308 us
    all_to_all x7, waiting for transfers between devices, exchange(): return lax.all_to_all(x, GROUP_AXIS, split, concat, tiled=True)  209 us
    pallas_call x2, Pallas kernels, column_block(): call(functools.partial(col_kernel, heads), (rows // block,), [lead_spec((...  197 us
    all_gather x4, blocking collectives, gather(): return lax.all_gather(x, GROUP_AXIS, axis=axis, tiled=True)  173 us
    pallas_call x2, Pallas kernels, end_attention(): call(functools.partial(end_kernel, heads), (cols // block,), [lead_spec((...  127 us
    pallas_call x2, Pallas kernels, row_attention(): call(functools.partial(row_kernel, transposed, heads), (seqs // block,),...  116 us
    all_to_all x3, blocking collectives, exchange(): return lax.all_to_all(x, GROUP_AXIS, split, concat, tiled=True)  107 us
    pallas_call x2, Pallas kernels, incoming(): call(incoming_kernel, (tri // block,), [full_spec(a), lead_spec((block, l...  91.9 us
  transfers between devices with their start and end apart: 15, of which 12 were waited for; matrix products, arithmetic and copies ran while one was open for 3% of the time, Pallas kernels for 7%

profile of v1, /device:TPU:112, one launch (start us, length us, event | category | flops | bytes accessed | tf_op | source)
XLA Modules:
  0.0 1734.7 jit_solution(7058569751966496802)
XLA Ops:
  10.1 12.4 shard_map.248
  26.0 20.7 %all-gather.9.cloned.1.call-done = bf16[10,256,256]{2,1,0:T(8,128)(2,1)} async-done(((bf16[10,32,256]{2,1,0:T(8,128)(2,1)}), bf16[10,256,256]{2,1,0:T(8,128)(2,1)}) %all-gather.9.cloned.1.call-update) | async-done | bytes 1310736 | tf_op jit(solution)/shard_map/all_gather | solution.py:502
  49.0 58.3 %shard_map.249 = bf16[32,256,256]{2,1,0:T(8,128)(2,1)} custom-call(bf16[32,256,256]{2,1,0:T(8,128)(2,1)} %m_ref.1, f32[32,256]{1,0:T(8,128)} %get-tuple-element.102.mask_ref, bf16[8,256,256]{2,1,0:T(8,128)(2,1)} %slice.177.bias_ref, bf16[256,1024]{1,0:T(8,128)(2,1)} %get-tuple-element.67.w_ref, bf16[256,256]{1,0:T(8,128)(2,1)} %get-tuple-element.88.w_out_ref), custom_call_target="tpu_custom_call" | custom-call | flops 20000000000 | bytes 16777216 | tf_op jit(solution)/shard_map/pallas_call | solution.py:191
  107.3 6.6 copy.43
  113.9 4.9 all-to-all-start
  124.5 43.7 %all-to-all-done = bf16[32,256,256]{2,0,1:T(8,128)(2,1)} async-done(((bf16[32,256,256]{2,0,1:T(8,128)(2,1)}), bf16[32,256,256]{2,0,1:T(8,128)(2,1)}, u32[]{:S(2)}, u32[]{:S(2)}) %all-to-all-start) | async-done | bytes 4194336 | tf_op jit(solution)/shard_map/all_to_all | solution.py:506
  168.2 6.8 copy.44
  175.0 98.7 %shard_map.250 = (bf16[256,32,256]{2,1,0:T(8,128)(2,1)}, bf16[32,32,256]{2,1,0:T(8,128)(2,1)}, bf16[32,32,256]{2,1,0:T(8,128)(2,1)}) custom-call(bf16[256,32,256]{2,1,0:T(8,128)(2,1)} %bitcast.155, f32[32,256]{1,0:T(8,128)} %dynamic-slice_bitcast_fusion.1.mask_ref.rmask_ref, bf16[256,1024]{1,0:T(8,128)(2,1)} %get-tuple-element.111.w_ref, ...), custom_call_target="tpu_custom_call" | custom-call | flops 30000001024 | bytes 16777216 | tf_op jit(solution)/shard_map/pallas_call | solution.py:254
  275.4 25.6 %all-gather.11.cloned.1.call-done.b_ref = bf16[32,256,256]{2,1,0:T(8,128)(2,1)} async-done(((bf16[32,32,256]{2,1,0:T(8,128)(2,1)}), bf16[32,256,256]{2,1,0:T(8,128)(2,1)}) %all-gather.11.cloned.1.call-update) | async-done | bytes 4194320 | tf_op jit(solution)/shard_map/all_gather | solution.py:502
  301.0 44.8 %shard_map.251 = (bf16[32,256,128]{2,1,0:T(8,128)(2,1)}, bf16[128,32,256]{2,1,0:T(8,128)(2,1)}, bf16[128,32,256]{2,1,0:T(8,128)(2,1)}) custom-call(bf16[32,32,256]{2,1,0:T(8,128)(2,1)} %get-tuple-element.32.a_ref, bf16[32,256,256]{2,1,0:T(8,128)(2,1)} %all-gather.11.cloned.1.call-done.b_ref, bf16[32,256,128]{2,1,0:T(8,128)(2,1)} %z_ref.3, ...), custom_call_target="tpu_custom_call" | custom-call | flops 10000000000 | bytes 16777216 | tf_op jit(solution)/shard_map/pallas_call | solution.py:316
  348.0 79.0 %all-gather.13.cloned.1.call-done.b_ref = bf16[128,256,256]{2,1,0:T(8,128)(2,1)} async-done(((bf16[128,32,256]{2,1,0:T(8,128)(2,1)}), bf16[128,256,256]{2,1,0:T(8,128)(2,1)}) %all-gather.13.cloned.1.call-update) | async-done | bytes 16777232 | tf_op jit(solution)/shard_map/all_gather | solution.py:502
  427.0 44.1 %shard_map.252 = (bf16[32,256,128]{2,1,0:T(8,128)(2,1)}, bf16[32,256,128]{2,1,0:T(8,128)(2,1)}, bf16[128,32,256]{2,1,0:T(8,128)(2,1)}) custom-call(bf16[128,32,256]{2,1,0:T(8,128)(2,1)} %get-tuple-element.34.a_ref, bf16[128,256,256]{2,1,0:T(8,128)(2,1)} %all-gather.13.cloned.1.call-done.b_ref, bf16[32,256,128]{2,1,0:T(8,128)(2,1)} %get-tuple-element.36.z_ref, ...), custom_call_target="tpu_custom_call" | custom-call | flops 10000000000 | bytes 16777216 | tf_op jit(solution)/shard_map/pallas_call | solution.py:378
  475.4 4.2 all-to-all-start.2
  482.8 46.3 %all-to-all-done.2 = bf16[32,256,128]{2,0,1:T(8,128)(2,1)S(1)} async-done(((bf16[32,256,128]{2,0,1:T(8,128)(2,1)}), bf16[32,256,128]{2,0,1:T(8,128)(2,1)S(1)}, u32[]{:S(2)}, u32[]{:S(2)}) %all-to-all-start.2) | async-done | bytes 2097184 | tf_op jit(solution)/shard_map/all_to_all | solution.py:506
  531.2 44.1 %all-gather.15.cloned.1.call-done.b_ref = bf16[128,256,256]{2,1,0:T(8,128)(2,1)} async-done(((bf16[128,32,256]{2,1,0:T(8,128)(2,1)}), bf16[128,256,256]{2,1,0:T(8,128)(2,1)}) %all-gather.15.cloned.1.call-update) | async-done | bytes 16777232 | tf_op jit(solution)/shard_map/all_gather | solution.py:502
  575.3 45.9 %shard_map.253 = (bf16[32,256,128]{2,1,0:T(8,128)(2,1)}, bf16[4,32,256]{2,1,0:T(8,128)(2,1)}) custom-call(bf16[256,32,128]{2,1,0:T(8,128)(2,1)} %bitcast.159, bf16[128,256,256]{2,1,0:T(8,128)(2,1)} %all-gather.15.cloned.1.call-done.b_ref, bf16[32,256,128]{2,1,0:T(8,128)(2,1)} %get-tuple-element.39.z_ref, ...), custom_call_target="tpu_custom_call" | custom-call | flops 10000000000 | bytes 16777216 | tf_op jit(solution)/shard_map/pallas_call | solution.py:421
  621.3 22.6 %all_gather.40.bias_ref = bf16[4,256,256]{2,1,0:T(8,128)(2,1)} all-gather(bf16[4,32,256]{2,1,0:T(8,128)(2,1)} %get-tuple-element.41), channel_id=1, replica_groups=mesh['req'=2,'dap'=8] {'dap'}, dimensions={1}, use_global_device_ids=true | all-gather | bytes 589824 | tf_op jit(solution)/shard_map/all_gather | solution.py:502
  643.9 39.4 %shard_map.254 = (bf16[32,256,128]{2,1,0:T(8,128)(2,1)}, bf16[4,32,256]{2,1,0:T(8,128)(2,1)}) custom-call(bf16[32,256,128]{2,1,0:T(8,128)(2,1)} %get-tuple-element.40.z_ref, f32[32,256]{1,0:T(8,128)} %get-tuple-element.110.pmask_ref.mask_ref, bf16[4,256,256]{2,1,0:T(8,128)(2,1)} %all_gather.40.bias_ref, bf16[128,512]{1,0:T(8,128)(2,1)} %get-tuple-element.84.w_ref, ...), custom_call_target="tpu_custom_call" | custom-call | flops 10000000000 | bytes 16777216 | tf_op jit(solution)/shard_map/pallas_call | solution.py:454
  683.3 2.9 copy.50
  686.3 30.1 %all_to_all.180 = bf16[32,256,128]{2,0,1:T(8,128)(2,1)S(1)} all-to-all(bf16[32,256,128]{2,0,1:T(8,128)(2,1)S(1)} %copy.50), channel_id=1, replica_groups=mesh['req'=2,'dap'=8] {'dap'}, dimensions={1} | all-to-all | bytes 4194304 | tf_op jit(solution)/shard_map/all_to_all | solution.py:506
  716.3 4.9 all-to-all-start.1
  724.1 62.3 %all_gather.41.bias_ref = bf16[4,256,256]{2,1,0:T(8,128)(2,1)} all-gather(bf16[4,32,256]{2,1,0:T(8,128)(2,1)S(1)} %copy-done.16), channel_id=1, replica_groups=mesh['req'=2,'dap'=8] {'dap'}, dimensions={1}, use_global_device_ids=true | all-gather | bytes 589824 | tf_op jit(solution)/shard_map/all_gather | solution.py:502
  788.5 63.7 %shard_map.255 = (bf16[256,32,128]{2,1,0:T(8,128)(2,1)}, bf16[8,32,256]{2,1,0:T(8,128)(2,1)}) custom-call(bf16[256,32,128]{2,1,0:T(8,128)(2,1)} %bitcast.161, f32[32,256]{1,0:T(8,128)} %dynamic-slice_bitcast_fusion.mask_ref, bf16[4,256,256]{2,1,0:T(8,128)(2,1)} %all_gather.41.bias_ref, bf16[128,512]{1,0:T(8,128)(2,1)} %get-tuple-element.113.w_ref, ...), custom_call_target="tpu_custom_call" | custom-call | flops 10000000000 | bytes 16777216 | tf_op jit(solution)/shard_map/pallas_call | solution.py:492
  852.2 4.8 copy.47
  857.1 14.0 all-gather.17.cloned.1.call-done.bias_ref
  871.1 58.0 %shard_map.256 = bf16[32,256,256]{2,1,0:T(8,128)(2,1)} custom-call(bf16[32,256,256]{2,1,0:T(8,128)(2,1)} %bitcast.154, f32[32,256]{1,0:T(8,128)} %get-tuple-element.102.mask_ref, bf16[8,256,256]{2,1,0:T(8,128)(2,1)} %all-gather.17.cloned.1.call-done.bias_ref, bf16[256,1024]{1,0:T(8,128)(2,1)} %get-tuple-element.66.w_ref, ...), custom_call_target="tpu_custom_call" | custom-call | flops 20000000000 | bytes 16777216 | tf_op jit(solution)/shard_map/pallas_call | solution.py:191
  929.1 6.6 copy.52
  935.7 4.7 all-to-all-start.4
  941.4 48.5 %all-to-all-done.4 = bf16[32,256,256]{2,0,1:T(8,128)(2,1)} async-done(((bf16[32,256,256]{2,0,1:T(8,128)(2,1)}), bf16[32,256,256]{2,0,1:T(8,128)(2,1)}, u32[]{:S(2)}, u32[]{:S(2)}) %all-to-all-start.4) | async-done | bytes 4194336 | tf_op jit(solution)/shard_map/all_to_all | solution.py:506
  989.8 6.8 copy.53
  996.6 98.7 %shard_map.257 = (bf16[256,32,256]{2,1,0:T(8,128)(2,1)}, bf16[32,32,256]{2,1,0:T(8,128)(2,1)}, bf16[32,32,256]{2,1,0:T(8,128)(2,1)}) custom-call(bf16[256,32,256]{2,1,0:T(8,128)(2,1)} %bitcast.153, f32[32,256]{1,0:T(8,128)} %dynamic-slice_bitcast_fusion.1.mask_ref.rmask_ref, bf16[256,1024]{1,0:T(8,128)(2,1)} %get-tuple-element.112.w_ref, ...), custom_call_target="tpu_custom_call" | custom-call | flops 30000001024 | bytes 16777216 | tf_op jit(solution)/shard_map/pallas_call | solution.py:254
  1095.5 46.7 %all_to_all.181 = bf16[256,32,128]{2,1,0:T(8,128)(2,1)S(1)} all-to-all(bf16[256,32,128]{2,1,0:T(8,128)(2,1)S(1)} %copy-done), channel_id=1, replica_groups=mesh['req'=2,'dap'=8] {'dap'}, dimensions={0} | all-to-all | bytes 4194304 | tf_op jit(solution)/shard_map/all_to_all | solution.py:506
  1144.1 44.9 %shard_map.258 = (bf16[32,256,128]{2,1,0:T(8,128)(2,1)}, bf16[128,32,256]{2,1,0:T(8,128)(2,1)}, bf16[128,32,256]{2,1,0:T(8,128)(2,1)}) custom-call(bf16[32,32,256]{2,1,0:T(8,128)(2,1)} %get-tuple-element.46.a_ref, bf16[32,256,256]{2,1,0:T(8,128)(2,1)} %all-gather.19.cloned.1.call-done.b_ref, bf16[32,256,128]{2,1,0:T(8,128)(2,1)} %bitcast.157, ...), custom_call_target="tpu_custom_call" | custom-call | flops 10000000000 | bytes 16777216 | tf_op jit(solution)/shard_map/pallas_call | solution.py:316
  1189.1 80.5 %all-gather.21.cloned.1.call-done.b_ref = bf16[128,256,256]{2,1,0:T(8,128)(2,1)} async-done(((bf16[128,32,256]{2,1,0:T(8,128)(2,1)}), bf16[128,256,256]{2,1,0:T(8,128)(2,1)}) %all-gather.21.cloned.1.call-update) | async-done | bytes 16777232 | tf_op jit(solution)/shard_map/all_gather | solution.py:502
  1269.6 44.2 %shard_map.259 = (bf16[32,256,128]{2,1,0:T(8,128)(2,1)}, bf16[32,256,128]{2,1,0:T(8,128)(2,1)}, bf16[128,32,256]{2,1,0:T(8,128)(2,1)}) custom-call(bf16[128,32,256]{2,1,0:T(8,128)(2,1)} %get-tuple-element.49.a_ref, bf16[128,256,256]{2,1,0:T(8,128)(2,1)} %all-gather.21.cloned.1.call-done.b_ref, bf16[32,256,128]{2,1,0:T(8,128)(2,1)} %get-tuple-element.51.z_ref, ...), custom_call_target="tpu_custom_call" | custom-call | flops 10000000000 | bytes 16777216 | tf_op jit(solution)/shard_map/pallas_call | solution.py:378
  1318.1 4.0 all-to-all-start.7
  1323.2 48.4 %all-to-all-done.7 = bf16[32,256,128]{2,0,1:T(8,128)(2,1)S(1)} async-done(((bf16[32,256,128]{2,0,1:T(8,128)(2,1)}), bf16[32,256,128]{2,0,1:T(8,128)(2,1)S(1)}, u32[]{:S(2)}, u32[]{:S(2)}) %all-to-all-start.7) | async-done | bytes 2097184 | tf_op jit(solution)/shard_map/all_to_all | solution.py:506
  1373.8 44.3 %all-gather.23.cloned.1.call-done.b_ref = bf16[128,256,256]{2,1,0:T(8,128)(2,1)} async-done(((bf16[128,32,256]{2,1,0:T(8,128)(2,1)}), bf16[128,256,256]{2,1,0:T(8,128)(2,1)}) %all-gather.23.cloned.1.call-update) | async-done | bytes 16777232 | tf_op jit(solution)/shard_map/all_gather | solution.py:502
  1418.0 46.0 %shard_map.260 = (bf16[32,256,128]{2,1,0:T(8,128)(2,1)}, bf16[4,32,256]{2,1,0:T(8,128)(2,1)}) custom-call(bf16[256,32,128]{2,1,0:T(8,128)(2,1)} %bitcast.158, bf16[128,256,256]{2,1,0:T(8,128)(2,1)} %all-gather.23.cloned.1.call-done.b_ref, bf16[32,256,128]{2,1,0:T(8,128)(2,1)} %get-tuple-element.54.z_ref, ...), custom_call_target="tpu_custom_call" | custom-call | flops 10000000000 | bytes 16777216 | tf_op jit(solution)/shard_map/pallas_call | solution.py:421
  1464.0 22.6 %all_gather.46.bias_ref = bf16[4,256,256]{2,1,0:T(8,128)(2,1)} all-gather(bf16[4,32,256]{2,1,0:T(8,128)(2,1)} %get-tuple-element.56), channel_id=1, replica_groups=mesh['req'=2,'dap'=8] {'dap'}, dimensions={1}, use_global_device_ids=true | all-gather | bytes 589824 | tf_op jit(solution)/shard_map/all_gather | solution.py:502
  1486.6 39.4 %shard_map.261 = (bf16[32,256,128]{2,1,0:T(8,128)(2,1)}, bf16[4,32,256]{2,1,0:T(8,128)(2,1)}) custom-call(bf16[32,256,128]{2,1,0:T(8,128)(2,1)} %get-tuple-element.55.z_ref, f32[32,256]{1,0:T(8,128)} %get-tuple-element.110.pmask_ref.mask_ref, bf16[4,256,256]{2,1,0:T(8,128)(2,1)} %all_gather.46.bias_ref, bf16[128,512]{1,0:T(8,128)(2,1)} %get-tuple-element.83.w_ref, ...), custom_call_target="tpu_custom_call" | custom-call | flops 10000000000 | bytes 16777216 | tf_op jit(solution)/shard_map/pallas_call | solution.py:454
  1529.0 30.1 %all_to_all.182 = bf16[32,256,128]{2,0,1:T(8,128)(2,1)S(1)} all-to-all(bf16[32,256,128]{2,0,1:T(8,128)(2,1)S(1)} %copy.59), channel_id=1, replica_groups=mesh['req'=2,'dap'=8] {'dap'}, dimensions={1} | all-to-all | bytes 4194304 | tf_op jit(solution)/shard_map/all_to_all | solution.py:506
  1559.1 4.9 all-to-all-start.5
  1564.0 65.1 %all_gather.47.bias_ref = bf16[4,256,256]{2,1,0:T(8,128)(2,1)} all-gather(bf16[4,32,256]{2,1,0:T(8,128)(2,1)S(1)} %copy-done.17), channel_id=1, replica_groups=mesh['req'=2,'dap'=8] {'dap'}, dimensions={1}, use_global_device_ids=true | all-gather | bytes 589824 | tf_op jit(solution)/shard_map/all_gather | solution.py:502
  1631.2 63.7 %shard_map.262 = (bf16[256,32,128]{2,1,0:T(8,128)(2,1)}, bf16[8,32,256]{2,1,0:T(8,128)(2,1)}) custom-call(bf16[256,32,128]{2,1,0:T(8,128)(2,1)} %bitcast.160, f32[32,256]{1,0:T(8,128)} %dynamic-slice_bitcast_fusion.mask_ref, bf16[4,256,256]{2,1,0:T(8,128)(2,1)} %all_gather.47.bias_ref, bf16[128,512]{1,0:T(8,128)(2,1)} %get-tuple-element.114.w_ref, ...), custom_call_target="tpu_custom_call" | custom-call | flops 10000000000 | bytes 16777216 | tf_op jit(solution)/shard_map/pallas_call | solution.py:492
  1694.9 3.8 all-to-all-start.9
  1698.7 4.8 copy.55
  1703.5 22.1 %all-to-all-done.9 = bf16[256,32,128]{2,1,0:T(8,128)(2,1)S(1)} async-done(((bf16[256,32,128]{2,1,0:T(8,128)(2,1)}), bf16[256,32,128]{2,1,0:T(8,128)(2,1)S(1)}, u32[]{:S(2)}, u32[]{:S(2)}) %all-to-all-start.9) | async-done | bytes 2097184 | tf_op jit(solution)/shard_map/all_to_all | solution.py:506
  (113 shorter events, 50.5 us)
Async XLA Ops:
  7.2 17.0 copy-start.10
  7.2 17.7 %copy-start.3 = (bf16[2,256,1024]{2,1,0:T(8,128)(2,1)S(1)}, bf16[2,256,1024]{2,1,0:T(8,128)(2,1)}, u32[]{:S(2)}) copy-start(bf16[2,256,1024]{2,1,0:T(8,128)(2,1)} %param.29) | copy-start | bytes 3145732
  7.2 39.5 %all-gather.9.cloned.1.call-start = ((), (), s32[]{:S(2)}) async-start(), calls=%async_computation.10 | async-start | bytes 1474560 | tf_op jit(solution)/shard_map/all_gather | solution.py:502
  113.9 5.2 copy-start.18
  113.9 5.9 copy-start.11
  113.9 6.6 copy-start.4
  113.9 54.3 %all-to-all-start = ((bf16[32,256,256]{2,0,1:T(8,128)(2,1)}), bf16[32,256,256]{2,0,1:T(8,128)(2,1)}, u32[]{:S(2)}, u32[]{:S(2)}) async-start(bf16[32,256,256]{2,0,1:T(8,128)(2,1)} %copy.43), calls=%async_computation | async-start | bytes 8388608 | tf_op jit(solution)/shard_map/all_to_all | solution.py:506
  118.8 2.9 copy-start.5
  118.8 2.8 copy-start.6
  118.8 182.1 %all-gather.11.cloned.1.call-start = ((), (), s32[]{:S(2)}) async-start(), calls=%async_computation.11 | async-start | bytes 4718592 | tf_op jit(solution)/shard_map/all_gather | solution.py:502
  121.7 1.3 slice-start
  175.0 98.8 %copy-start.8 = (bf16[2,128,640]{2,1,0:T(8,128)(2,1)S(1)}, bf16[2,128,640]{2,1,0:T(8,128)(2,1)}, u32[]{:S(2)}) copy-start(bf16[2,128,640]{2,1,0:T(8,128)(2,1)} %param.38) | copy-start | bytes 983044
  175.0 99.6 %copy-start.7 = (bf16[2,1024,128]{2,1,0:T(8,128)(2,1)S(1)}, bf16[2,1024,128]{2,1,0:T(8,128)(2,1)}, u32[]{:S(2)}) copy-start(bf16[2,1024,128]{2,1,0:T(8,128)(2,1)} %param.37) | copy-start | bytes 1572868
  273.7 153.3 %all-gather.13.cloned.1.call-start = ((), (), s32[]{:S(2)}) async-start(), calls=%async_computation.12 | async-start | bytes 18874368 | tf_op jit(solution)/shard_map/all_gather | solution.py:502
  345.8 0.8 copy-start.19
  345.8 1.5 copy-start.9
  345.9 229.4 %all-gather.15.cloned.1.call-start = ((), (), s32[]{:S(2)}) async-start(), calls=%async_computation.13 | async-start | bytes 18874368 | tf_op jit(solution)/shard_map/all_gather | solution.py:502
  471.1 1.6 copy-start.1
  475.4 4.2 copy-start.23
  475.4 4.8 copy-start.24
  475.4 5.4 copy-start.20
  475.4 6.1 copy-start.21
  475.4 6.7 copy-start.12
  475.4 53.7 %all-to-all-start.2 = ((bf16[32,256,128]{2,0,1:T(8,128)(2,1)}), bf16[32,256,128]{2,0,1:T(8,128)(2,1)S(1)}, u32[]{:S(2)}, u32[]{:S(2)}) async-start(bf16[32,256,128]{2,0,1:T(8,128)(2,1)} %copy.48), calls=%async_computation.2 | async-start | bytes 4194304 | tf_op jit(solution)/shard_map/all_to_all | solution.py:506
  716.3 5.0 copy-start.22
  716.3 5.6 copy-start.13
  716.3 6.3 copy-start.14
  716.3 6.3 copy-start.15
  716.3 7.7 copy-start.16
  716.3 135.9 %all-to-all-start.1 = ((bf16[256,32,256]{2,1,0:T(8,128)(2,1)}), bf16[256,32,256]{2,1,0:T(8,128)(2,1)}, u32[]{:S(2)}, u32[]{:S(2)}) async-start(bf16[256,32,256]{2,1,0:T(8,128)(2,1)} %get-tuple-element.31), calls=%async_computation.1 | async-start | bytes 8388608 | tf_op jit(solution)/shard_map/all_to_all | solution.py:506
  721.2 149.8 %all-gather.17.cloned.1.call-start = ((), (), s32[]{:S(2)}) async-start(), calls=%async_computation.14 | async-start | bytes 1179648 | tf_op jit(solution)/shard_map/all_gather | solution.py:502
  935.7 54.2 %all-to-all-start.4 = ((bf16[32,256,256]{2,0,1:T(8,128)(2,1)}), bf16[32,256,256]{2,0,1:T(8,128)(2,1)}, u32[]{:S(2)}, u32[]{:S(2)}) async-start(bf16[32,256,256]{2,0,1:T(8,128)(2,1)} %copy.52), calls=%async_computation.4 | async-start | bytes 8388608 | tf_op jit(solution)/shard_map/all_to_all | solution.py:506
  940.4 203.7 %all-gather.19.cloned.1.call-start = ((), (), s32[]{:S(2)}) async-start(), calls=%async_computation.15 | async-start | bytes 4718592 | tf_op jit(solution)/shard_map/all_gather | solution.py:502
  996.6 98.9 %copy-start = (bf16[256,32,128]{2,1,0:T(8,128)(2,1)S(1)}, bf16[256,32,128]{2,1,0:T(8,128)(2,1)}, u32[]{:S(2)}) copy-start(bf16[256,32,128]{2,1,0:T(8,128)(2,1)} %get-tuple-element.48) | copy-start | bytes 6291460
  1095.4 174.2 %all-gather.21.cloned.1.call-start = ((), (), s32[]{:S(2)}) async-start(), calls=%async_computation.16 | async-start | bytes 18874368 | tf_op jit(solution)/shard_map/all_gather | solution.py:502
  1189.0 229.0 %all-gather.23.cloned.1.call-start = ((), (), s32[]{:S(2)}) async-start(), calls=%async_computation.17 | async-start | bytes 18874368 | tf_op jit(solution)/shard_map/all_gather | solution.py:502
  1313.8 1.6 copy-start.2
  1318.1 53.5 %all-to-all-start.7 = ((bf16[32,256,128]{2,0,1:T(8,128)(2,1)}), bf16[32,256,128]{2,0,1:T(8,128)(2,1)S(1)}, u32[]{:S(2)}, u32[]{:S(2)}) async-start(bf16[32,256,128]{2,0,1:T(8,128)(2,1)} %copy.57), calls=%async_computation.7 | async-start | bytes 4194304 | tf_op jit(solution)/shard_map/all_to_all | solution.py:506
  1559.1 4.9 copy-start.17
  1559.1 135.8 %all-to-all-start.5 = ((bf16[256,32,256]{2,1,0:T(8,128)(2,1)}), bf16[256,32,256]{2,1,0:T(8,128)(2,1)}, u32[]{:S(2)}, u32[]{:S(2)}) async-start(bf16[256,32,256]{2,1,0:T(8,128)(2,1)} %get-tuple-element.45), calls=%async_computation.5 | async-start | bytes 8388608 | tf_op jit(solution)/shard_map/all_to_all | solution.py:506
  1694.9 30.8 %all-to-all-start.9 = ((bf16[256,32,128]{2,1,0:T(8,128)(2,1)}), bf16[256,32,128]{2,1,0:T(8,128)(2,1)S(1)}, u32[]{:S(2)}, u32[]{:S(2)}) async-start(bf16[256,32,128]{2,1,0:T(8,128)(2,1)} %get-tuple-element.59), calls=%async_computation.9 | async-start | bytes 4194304 | tf_op jit(solution)/shard_map/all_to_all | solution.py:506
Sparse Core Ops, SparseCore 0:
  24.3 22.3 all-gather.8
  273.8 27.0 all-gather.10
  346.0 80.9 all-gather.12
  471.3 103.9 all-gather.14
  852.4 18.6 all-gather.16
  1095.5 46.7 all-gather.18
  1189.2 80.4 all-gather.20
  1314.0 103.9 all-gather.22

commit v2 on v1

v2 whole, which is shorter than its diff:
```python
import functools
import math

import jax
import jax.numpy as jnp
from jax import lax
from jax.experimental import pallas as pl
from jax.experimental.pallas import tpu as pltpu
from jax.sharding import PartitionSpec as P

GROUP_AXIS = 'dap'
PARTS_AXIS = 'req'
LOG2E = math.log2(math.e)
MASKED = -1e9 * LOG2E
F32, BF16 = jnp.float32, jnp.bfloat16
VMEM_LIMIT = 60 * 1024 * 1024


def nn(a, b):
    return lax.dot_general(a, b, (((1,), (0,)), ((), ())), preferred_element_type=F32)


def nt(a, b):
    return lax.dot_general(a, b, (((1,), (1,)), ((), ())), preferred_element_type=F32)


def tn(a, b):
    return lax.dot_general(a, b, (((0,), (0,)), ((), ())), preferred_element_type=F32)


def norm(x):
    centered = x - jnp.mean(x, axis=-1, keepdims=True)
    variance = jnp.mean(centered * centered, axis=-1, keepdims=True)
    return (centered * lax.rsqrt(variance + 1e-5)).astype(BF16)


def norm_steps(x):
    centered = x - jnp.mean(x, axis=-1, keepdims=True)
    yield
    variance = jnp.mean(centered * centered, axis=-1, keepdims=True)
    yield
    return (centered * lax.rsqrt(variance + 1e-5)).astype(BF16)


def together(count, body, group):
    def step(n, carry):
        live = [body(n * group + g) for g in range(group)]
        while live:
            going = []
            for member in live:
                try:
                    next(member)
                    going.append(member)
                except StopIteration:
                    pass
            live = going
        return carry
    lax.fori_loop(0, count // group, step, 0)


def flip(w):
    return w.astype(F32).T.astype(w.dtype)


def key_column(mask_row):
    return jnp.broadcast_to(mask_row, (128, mask_row.shape[1])).T


def project_row(r, x, mask_row, wt_ref, proj_s, keep_s):
    x_norm = yield from norm_steps(x)
    proj_s[r] = nt(wt_ref[...], x_norm).astype(BF16)
    keep_s[r] = key_column(mask_row)


def attend_rows(rows, proj_s, keep_s, gated_s, bias_ref, heads, group):
    width, length = gated_s.shape[1:]
    dim = width // heads

    def part(n, r, h):
        return proj_s[r, n * width + h * dim:n * width + (h + 1) * dim, :]

    def scores(r, h):
        logits = tn(part(1, r, h), part(0, r, h)) * (dim ** -0.5 * LOG2E)
        if bias_ref is not None:
            logits = logits + bias_ref[h]
        kept = jnp.concatenate([keep_s[r]] * (length // 128), axis=1) > 0
        return jnp.where(kept, logits, MASKED)

    def weigh(logits):
        expd = jnp.exp2(logits - jnp.max(logits, axis=0, keepdims=True))
        return (expd * (1.0 / jnp.sum(expd, axis=0, keepdims=True))).astype(BF16)

    def gate(r, h, probs):
        gated = nn(part(2, r, h), probs) * jax.nn.sigmoid(part(3, r, h).astype(F32))
        gated_s[r, h * dim:(h + 1) * dim, :] = gated.astype(BF16)

    def body(n):
        items = [(n * group + g, h) for g in range(group) for h in range(heads)]
        probs = None
        ahead = scores(*items[0])
        for k, item in enumerate(items):
            logits, ahead = ahead, scores(*items[k + 1]) if k + 1 < len(items) else None
            if probs is not None:
                gate(*items[k - 1], probs)
            probs = weigh(logits)
        gate(*items[-1], probs)
    each(rows // group, body)


def attention_scratch(rows, length, w, w_out):
    return [pltpu.VMEM((rows, w.shape[1], length), BF16), pltpu.VMEM((rows, length, 128), F32),
            pltpu.VMEM((rows, w_out.shape[0], length), BF16)]


def each(count, body, unroll=1):
    def step(n, carry):
        body(n)
        return carry
    lax.fori_loop(0, count, step, 0, unroll=unroll)


def load_bias(bias_ref, bias_s, transposed):
    for h in range(bias_s.shape[0]):
        bias = bias_ref[h].astype(F32) * LOG2E
        bias_s[h] = bias.T if transposed else bias


def transition_steps(x, w_in_ref, w_out_ref):
    x_norm = yield from norm_steps(x)
    hidden = jnp.maximum(nn(x_norm, w_in_ref[...]), 0.0).astype(BF16)
    yield
    update = nn(hidden, w_out_ref[...])
    yield
    return update


def residual(x, update):
    total = (x + update).astype(BF16)
    return total, total.astype(F32)


def rows_of(ref, start, count, step):
    return ref[pl.ds(start, count, stride=step), :]


def call(kernel, grid, in_specs, out_specs, out_shape, scratch, flops):
    return pl.pallas_call(
        kernel, grid=grid, in_specs=in_specs, out_specs=out_specs, out_shape=out_shape, scratch_shapes=scratch,
        compiler_params=pltpu.CompilerParams(vmem_limit_bytes=VMEM_LIMIT),
        cost_estimate=pl.CostEstimate(flops=flops, bytes_accessed=1 << 24, transcendentals=0))


def row_at(ref, n):
    if len(ref.shape) == 3:
        return ref[n]
    return jnp.concatenate([ref[d, n] for d in range(ref.shape[0])], axis=0)


def put_pieces(ref, n, value):
    size = ref.shape[2]
    for d in range(ref.shape[0]):
        ref[d, n] = value[d * size:(d + 1) * size]


def row_spec_of(x, block, first):
    if x.ndim == 3:
        return pl.BlockSpec((block,) + x.shape[1:], lambda n: (n + first, 0, 0))
    return pl.BlockSpec((x.shape[0], block) + x.shape[2:], lambda n: (0, n + first, 0, 0))


def full_spec(array):
    zeros = (0,) * array.ndim
    return pl.BlockSpec(array.shape, lambda n: zeros)


def lead_spec(block, axis):
    return pl.BlockSpec(block, lambda n: tuple(n if d == axis else 0 for d in range(len(block))))


def bias_rows(store, n, x_norm, wbt_ref):
    values = nt(wbt_ref[...], x_norm)
    for t in range(store.shape[0]):
        store[t, pl.ds(pl.multiple_of(n * 8, 8), 8), :] = values[:, t * 128:(t + 1) * 128]


def bias_scratch(rows, length):
    return pltpu.VMEM((length // 128, rows * 8, 128), F32)


def write_bias(out_ref, store, rows):
    for h in range(out_ref.shape[0]):
        out_ref[h] = take_row(store, h, rows, 8).astype(BF16)


def bias_kernel(z_ref, wbt_ref, out_ref, store):
    rows = z_ref.shape[0]

    def body(n, carry):
        bias_rows(store, n, norm(z_ref[n].astype(F32)), wbt_ref)
        return carry
    lax.fori_loop(0, rows, body, 0)
    write_bias(out_ref, store, rows)


def pair_bias(z, wbt, heads):
    rows, length, _ = z.shape
    return call(bias_kernel, (1,), [full_spec(z), full_spec(wbt)], lead_spec((heads, rows, length), 1),
                jax.ShapeDtypeStruct((heads, rows, length), BF16), [bias_scratch(rows, length)], 10 ** 8)(z, wbt)


def row_kernel(transposed, heads, m_ref, mask_ref, bias_ref, w_ref, w_out_ref, out_ref, bias_s, wt_s, proj_s, keep_s, gated_s):
    rows = mask_ref.shape[0]

    @pl.when(pl.program_id(0) == 0)
    def _():
        load_bias(bias_ref, bias_s, transposed)
        wt_s[...] = flip(w_ref[...])

    def project(s):
        yield from project_row(s, row_at(m_ref, s).astype(F32), mask_ref[pl.ds(s, 1), :], wt_s, proj_s, keep_s)
    together(rows, project, 2)
    attend_rows(rows, proj_s, keep_s, gated_s, bias_s, heads, 1)

    def finish(s):
        update = tn(gated_s[s], w_out_ref[...])
        yield
        put_pieces(out_ref, s, residual(row_at(m_ref, s).astype(F32), update)[0])
    together(rows, finish, 2)


def row_attention(m, mask, bias, transposed, w, w_out, pieces, part, parts):
    seqs, length = mask.shape
    chans = m.shape[-1]
    heads = bias.shape[0]
    block = 8
    steps = seqs // block // parts
    shape = (pieces, seqs // parts, length // pieces, chans)
    return call(functools.partial(row_kernel, transposed, heads), (steps,),
                [row_spec_of(m, block, part * steps), pl.BlockSpec((block, length), lambda n: (n + part * steps, 0)),
                 full_spec(bias), full_spec(w), full_spec(w_out)],
                lead_spec((pieces, block) + shape[2:], 1), jax.ShapeDtypeStruct(shape, BF16),
                [pltpu.VMEM((heads, length, length), F32), pltpu.VMEM(w.shape[::-1], BF16)] + attention_scratch(block, length, w, w_out),
                10 ** 10)(m, mask, bias, w, w_out)


def split_store(dst, parts):
    pieces, size, rows, chans = parts[0].shape
    for p, part in enumerate(parts):
        for d in range(pieces):
            flat = part[d].astype(F32).reshape(size * rows, chans)
            place = pl.ds((d * len(parts) + p) * size * rows, size * rows)
            for t in range(chans // 128):
                dst[t, place, :] = flat[:, t * 128:(t + 1) * 128]


def take_row(src, r, count, step):
    return jnp.concatenate([src[t, pl.ds(r, count, stride=step), :] for t in range(src.shape[0])], axis=1)


def put_row(dst, r, count, step, value):
    for t in range(dst.shape[0]):
        dst[t, pl.ds(r, count, stride=step), :] = value[:, t * 128:(t + 1) * 128]


def join_store(src, shape):
    seqs, rows, chans = shape
    return jnp.concatenate([src[t] for t in range(src.shape[0])], axis=1).reshape(seqs, rows, chans).astype(BF16)


def col_kernel(heads, parts, *refs):
    m_refs = refs[:parts]
    mask_ref, w_ref, w_out_ref, tin_ref, tout_ref, op_ref, out_ref, a_ref, b_ref, x_s, b_s, wt_s, opt_s, proj_s, keep_s, gated_s = refs[parts:]
    rows, seqs = mask_ref.shape
    chans = w_ref.shape[0]
    dim = op_ref.shape[1] // 2

    @pl.when(pl.program_id(0) == 0)
    def _():
        wt_s[...] = flip(w_ref[...])
        opt_s[...] = flip(op_ref[...])
    split_store(x_s, m_refs)

    def project(r):
        yield from project_row(r, take_row(x_s, r, seqs, rows), mask_ref[pl.ds(r, 1), :], wt_s, proj_s, keep_s)
    together(rows, project, 2)
    attend_rows(rows, proj_s, keep_s, gated_s, None, heads, 1)

    def finish(r):
        mask_row = mask_ref[pl.ds(r, 1), :]
        x = take_row(x_s, r, seqs, rows)
        update = tn(gated_s[r], w_out_ref[...])
        yield
        x = residual(x, update)[1]
        update = yield from transition_steps(x, tin_ref, tout_ref)
        x = residual(x, update)[1]
        x_norm = yield from norm_steps(x)
        proj = nt(opt_s[...], x_norm).astype(BF16).astype(F32) * mask_row
        yield
        put_row(x_s, r, seqs, rows, x)
        a_ref[r] = proj[:dim].astype(BF16)
        for t in range(seqs // 128):
            b_s[t, pl.ds(r, dim, stride=rows), :] = proj[dim:, t * 128:(t + 1) * 128]
    together(rows, finish, 2)
    out_ref[...] = join_store(x_s, (seqs, rows, chans)).reshape(out_ref.shape)
    b_ref[...] = join_store(b_s, b_ref.shape)


def column_block(m_parts, mask_t, heads, w, w_out, t_in, t_out, o_proj):
    rows, seqs = mask_t.shape
    pieces, size, _, chans = m_parts[0].shape
    parts = len(m_parts)
    dim = o_proj.shape[1] // 2
    block = 16
    weights = (w, w_out, t_in, t_out, o_proj)
    out_shape = (pieces, seqs // pieces, rows, chans)
    return call(functools.partial(col_kernel, heads, parts), (rows // block,),
                [lead_spec((pieces, size, block, chans), 2)] * parts + [lead_spec((block, seqs), 0)] + [full_spec(x) for x in weights],
                [lead_spec(out_shape[:2] + (block, chans), 2), lead_spec((block, dim, seqs), 0), lead_spec((dim, block, seqs), 1)],
                [jax.ShapeDtypeStruct(out_shape, BF16), jax.ShapeDtypeStruct((rows, dim, seqs), BF16), jax.ShapeDtypeStruct((dim, rows, seqs), BF16)],
                [pltpu.VMEM((chans // 128, seqs * block, 128), F32), pltpu.VMEM((seqs // 128, dim * block, 128), F32),
                 pltpu.VMEM(w.shape[::-1], BF16), pltpu.VMEM(o_proj.shape[::-1], BF16)] + attention_scratch(block, seqs, w, w_out),
                3 * 10 ** 10)(*m_parts, mask_t, *weights)


def gate_parts(z_norm, mask_row, wt_ref, tri):
    proj = nt(wt_ref[pl.ds(0, 4 * tri), :], z_norm)
    left = mask_row * jax.nn.sigmoid(proj[2 * tri:3 * tri]) * proj[:tri]
    right = mask_row * jax.nn.sigmoid(proj[3 * tri:]) * proj[tri:2 * tri]
    return left, right


def put_channels(dst, n, step, value):
    for t in range(dst.shape[0]):
        dst[t, pl.ds(n, value.shape[0], stride=step), :] = value[:, t * 128:(t + 1) * 128]


def opm_kernel(a_ref, b_ref, z_ref, rmask_ref, fmask_ref, pmask_ref, w_ref, proj_ref,
               z_out, l_out, r_out, wf_s, wt_s, gt_s, o_s, scale_s, l_s, r_s):
    rows, dim, seqs = a_ref.shape
    tri = l_out.shape[0]

    @pl.when(pl.program_id(0) == 0)
    def _():
        gt_s[...] = flip(proj_ref[...])
        wf_s[...] = w_ref[...].astype(F32)
        swapped = [rows_of(wf_s, e, dim, dim) for e in range(dim)]
        wt_s[...] = jnp.concatenate(swapped, axis=0).T.astype(BF16)
    scale_s[...] = 1.0 / (1e-3 + nt(rmask_ref[...].astype(BF16), fmask_ref[...].astype(BF16)))

    def outer(e, carry):
        prod = nt(a_ref[...].reshape(rows * dim, seqs), b_ref[e]).astype(BF16)
        for i in range(rows):
            o_s[i, pl.ds(pl.multiple_of(e * dim, dim), dim), :] = prod[i * dim:(i + 1) * dim]
        return carry
    lax.fori_loop(0, dim, outer, 0, unroll=2)

    def finish(i):
        update = nn(wt_s[...], o_s[i]) * scale_s[pl.ds(i, 1), :]
        yield
        total, total_f = residual(row_at(z_ref, i).astype(F32), update.T)
        yield
        z_norm = yield from norm_steps(total_f)
        left, right = gate_parts(z_norm, pmask_ref[pl.ds(i, 1), :], gt_s, tri)
        yield
        z_out[i] = total
        put_channels(l_s, i, rows, left)
        put_channels(r_s, i, rows, right)
    together(rows, finish, 2)
    l_out[...] = join_store(l_s, l_out.shape)
    r_out[...] = join_store(r_s, r_out.shape)


def outer_block(a, b_full, z, rmask, fmask, pmask, w_out, tri_proj, part, parts):
    rows, dim, seqs = a.shape
    length, out_dim = pmask.shape[1], z.shape[-1]
    tri = (tri_proj.shape[1] - out_dim) // 4
    block = rows // parts
    consts = (w_out, tri_proj)
    outs = [jax.ShapeDtypeStruct((block, length, out_dim), BF16)] + [jax.ShapeDtypeStruct((tri, block, length), BF16)] * 2
    chan_scratch = pltpu.VMEM((length // 128, tri * block, 128), F32)
    return call(opm_kernel, (1,),
                [pl.BlockSpec((block, dim, seqs), lambda n: (part, 0, 0)), full_spec(b_full), row_spec_of(z, block, part),
                 pl.BlockSpec((block, seqs), lambda n: (part, 0)), full_spec(fmask), pl.BlockSpec((block, length), lambda n: (part, 0))]
                + [full_spec(x) for x in consts], [full_spec(x) for x in outs], outs,
                [pltpu.VMEM(w_out.shape, F32), pltpu.VMEM(w_out.shape[::-1], BF16), pltpu.VMEM(tri_proj.shape[::-1], BF16),
                 pltpu.VMEM((block, dim * dim, length), BF16), pltpu.VMEM((block, length), F32), chan_scratch, chan_scratch],
                10 ** 10)(a, b_full, z, rmask, fmask, pmask, *consts)


def channel(b_refs, c, pieces):
    size = b_refs[0].shape[1] // pieces
    loaded = [ref[c] for ref in b_refs]
    return jnp.concatenate([x[d * size:(d + 1) * size] for d in range(pieces) for x in loaded], axis=0)


def put_product(x_s, c, rows, prod):
    for t in range(x_s.shape[0]):
        x_s[t, pl.ds(pl.multiple_of(c * rows, rows), rows), :] = prod[:, t * 128:(t + 1) * 128]


def tri_finish(x_s, z, i, rows, proj_ref, w_out_ref):
    out_dim = z.shape[1]
    chans = w_out_ref.shape[0]
    x = take_row(x_s, i, chans, rows)
    z_norm = yield from norm_steps(z)
    gate = nn(z_norm, proj_ref[:, 4 * chans:4 * chans + out_dim])
    centered = x - jnp.mean(x, axis=0, keepdims=True)
    variance = jnp.mean(centered * centered, axis=0, keepdims=True)
    x_norm = (centered * lax.rsqrt(variance + 1e-5)).astype(BF16)
    yield
    update = tn(x_norm, w_out_ref[...])
    gate = jax.nn.sigmoid(gate)
    yield
    return residual(z, gate * update)


def outgoing_kernel(parts, pieces, a_ref, *refs):
    b_refs = refs[:parts]
    z_ref, pmask_ref, proj_ref, w_out_ref, next_ref, z_out, l_out, r_out, x_s, r_s, gt_s = refs[parts:]
    step, steps = pl.program_id(0), pl.num_programs(0)
    block, rows, _ = a_ref.shape
    tri = w_out_ref.shape[0]

    def product(c, carry):
        put_product(x_s, step * block + c, rows, nt(a_ref[c], channel(b_refs, c, pieces)))
        return carry
    lax.fori_loop(0, block, product, 0, unroll=4)

    @pl.when(step == steps - 1)
    def _():
        gt_s[...] = flip(next_ref[...])

        def finish(i):
            mask_row = pmask_ref[pl.ds(i, 1), :]
            total, total_f = yield from tri_finish(x_s, z_ref[i].astype(F32), i, rows, proj_ref, w_out_ref)
            z_norm = yield from norm_steps(total_f)
            value = nn(z_norm, next_ref[:, :tri])
            value_gate = nn(z_norm, next_ref[:, 2 * tri:3 * tri])
            right = nt(gt_s[pl.ds(tri, tri), :], z_norm)
            right_gate = nt(gt_s[pl.ds(3 * tri, tri), :], z_norm)
            yield
            left = (key_column(mask_row) * jax.nn.sigmoid(value_gate) * value).astype(BF16)
            right = mask_row * jax.nn.sigmoid(right_gate) * right
            yield
            z_out[i] = total
            put_pieces(l_out, i, left)
            put_channels(r_s, i, rows, right)
        together(rows, finish, 2)
        r_out[...] = join_store(r_s, r_out.shape)


def outgoing(a, b_parts, z, pmask, proj, w_out, next_proj, pieces, part):
    tri, rows, length = a.shape
    block = 16
    parts = len(b_parts)
    weights = (proj, w_out, next_proj)
    scratch = pltpu.VMEM((length // 128, tri * rows, 128), F32)
    outs = [jax.ShapeDtypeStruct(z.shape, BF16), jax.ShapeDtypeStruct((pieces, rows, length // pieces, tri), BF16),
            jax.ShapeDtypeStruct((tri, rows, length), BF16)]
    return call(functools.partial(outgoing_kernel, parts, pieces), (tri // block,),
                [lead_spec((block, rows, length), 0)] + [lead_spec((block,) + x.shape[1:], 0) for x in b_parts]
                + [full_spec(z), pl.BlockSpec((rows, length), lambda n: (part, 0))] + [full_spec(x) for x in weights],
                [full_spec(x) for x in outs], outs, [scratch, scratch, pltpu.VMEM(next_proj.shape[::-1], BF16)],
                10 ** 10)(a, *b_parts, z, pmask, *weights)


def incoming_kernel(parts, *refs):
    a_refs, b_refs, z_refs = (refs[n * parts:(n + 1) * parts] for n in range(3))
    proj_ref, w_out_ref, wbt_ref, z_out, bias_out, af_s, a_s, x_s, bias_s = refs[3 * parts:]
    step, steps = pl.program_id(0), pl.num_programs(0)
    block = b_refs[0].shape[0]
    pieces, _, rows, tri = a_refs[0].shape
    length = z_out.shape[1]
    part_rows = z_refs[0].shape[0]

    @pl.when(step == 0)
    def _():
        split_store(af_s, a_refs)

        def turn(i):
            x = take_row(af_s, i, length, rows)
            yield
            put_channels(a_s, i, rows, x.T)
        together(rows, turn, 2)

    def product(c, carry):
        place = pl.ds(pl.multiple_of((step * block + c) * rows, rows), rows)
        left = jnp.concatenate([a_s[t, place, :] for t in range(a_s.shape[0])], axis=1).astype(BF16)
        put_product(x_s, step * block + c, rows, nn(left, channel(b_refs, c, pieces)))
        return carry
    lax.fori_loop(0, block, product, 0, unroll=4)

    @pl.when(step == steps - 1)
    def _():
        for p, z_ref in enumerate(z_refs):
            def finish(n, z_ref=z_ref, first=p * part_rows):
                i = first + n
                total, total_f = yield from tri_finish(x_s, z_ref[n].astype(F32), i, rows, proj_ref, w_out_ref)
                z_norm = yield from norm_steps(total_f)
                z_out[i] = total
                bias_rows(bias_s, i, z_norm, wbt_ref)
            together(part_rows, finish, 2)
        write_bias(bias_out, bias_s, rows)


def incoming(a_parts, b_parts, z_parts, proj, w_out, wbt, heads):
    pieces, _, rows, tri = a_parts[0].shape
    length, out_dim = z_parts[0].shape[1:]
    block = 16
    consts = (proj, w_out, wbt)
    scratch = pltpu.VMEM((length // 128, tri * rows, 128), F32)
    outs = [jax.ShapeDtypeStruct((rows, length, out_dim), BF16), jax.ShapeDtypeStruct((heads, rows, length), BF16)]
    return call(functools.partial(incoming_kernel, len(a_parts)), (tri // block,),
                [full_spec(x) for x in a_parts] + [lead_spec((block,) + x.shape[1:], 0) for x in b_parts] + [full_spec(x) for x in z_parts]
                + [full_spec(x) for x in consts], [full_spec(x) for x in outs], outs,
                [pltpu.VMEM((tri // 128, length * rows, 128), F32), scratch, scratch, bias_scratch(rows, length)],
                10 ** 10)(*a_parts, *b_parts, *z_parts, *consts)


def start_kernel(heads, z_ref, mask_ref, bias_ref, w_ref, w_out_ref, wbt_ref, z_out, bias_out, bias_s, wt_s, next_s, proj_s, keep_s, gated_s):
    rows = z_ref.shape[0]

    @pl.when(pl.program_id(0) == 0)
    def _():
        load_bias(bias_ref, bias_s, True)
        wt_s[...] = flip(w_ref[...])

    def project(i):
        yield from project_row(i, z_ref[i].astype(F32), mask_ref[pl.ds(i, 1), :], wt_s, proj_s, keep_s)
    together(rows, project, 4)
    attend_rows(rows, proj_s, keep_s, gated_s, bias_s, heads, 2)

    def finish(i):
        update = tn(gated_s[i], w_out_ref[...])
        yield
        total, total_f = residual(z_ref[i].astype(F32), update)
        z_norm = yield from norm_steps(total_f)
        put_pieces(z_out, i, total)
        bias_rows(next_s, i, z_norm, wbt_ref)
    together(rows, finish, 4)
    write_bias(bias_out, next_s, rows)


def start_attention(z, mask, bias, w, w_out, wbt, pieces, part, parts):
    rows, length, chans = z.shape
    heads = bias.shape[0]
    block = rows // parts
    consts = (bias, w, w_out, wbt)
    outs = [jax.ShapeDtypeStruct((pieces, block, length // pieces, chans), BF16), jax.ShapeDtypeStruct((heads, block, length), BF16)]
    return call(functools.partial(start_kernel, heads), (1,),
                [row_spec_of(z, block, part), pl.BlockSpec((block, length), lambda n: (part, 0))] + [full_spec(x) for x in consts],
                [full_spec(x) for x in outs], outs,
                [pltpu.VMEM((heads, length, length), F32), pltpu.VMEM(w.shape[::-1], BF16), bias_scratch(block, length)]
                + attention_scratch(block, length, w, w_out), 10 ** 10)(z, mask, *consts)


def end_kernel(heads, parts, *refs):
    z_refs = refs[:parts]
    mask_ref, bias_ref, w_ref, w_out_ref, tin_ref, tout_ref, wbt_ref, z_out, bias_out, x_s, bias_s, wt_s, next_s, proj_s, keep_s, gated_s = refs[parts:]
    cols, length = mask_ref.shape
    chans = w_ref.shape[0]

    @pl.when(pl.program_id(0) == 0)
    def _():
        load_bias(bias_ref, bias_s, False)
        wt_s[...] = flip(w_ref[...])
    split_store(x_s, z_refs)

    def project(j):
        yield from project_row(j, take_row(x_s, j, length, cols), mask_ref[pl.ds(j, 1), :], wt_s, proj_s, keep_s)
    together(cols, project, 4)
    attend_rows(cols, proj_s, keep_s, gated_s, bias_s, heads, 2)

    def finish(j):
        x = take_row(x_s, j, length, cols)
        update = tn(gated_s[j], w_out_ref[...])
        yield
        x = residual(x, update)[1]
        update = yield from transition_steps(x, tin_ref, tout_ref)
        x = residual(x, update)[1]
        x_norm = yield from norm_steps(x)
        put_row(x_s, j, length, cols, x)
        bias_rows(next_s, j, x_norm, wbt_ref)
    together(cols, finish, 2)
    z_out[...] = join_store(x_s, (length, cols, chans)).reshape(z_out.shape)
    write_bias(bias_out, next_s, cols)


def end_attention(z_parts, mask_t, bias, w, w_out, t_in, t_out, wbt, next_heads):
    cols, length = mask_t.shape
    pieces, size, _, chans = z_parts[0].shape
    parts = len(z_parts)
    heads = bias.shape[0]
    block = 16
    consts = (bias, w, w_out, t_in, t_out, wbt)
    out_shape = (pieces, length // pieces, cols, chans)
    return call(functools.partial(end_kernel, heads, parts), (cols // block,),
                [lead_spec((pieces, size, block, chans), 2)] * parts + [lead_spec((block, length), 0)] + [full_spec(x) for x in consts],
                [lead_spec(out_shape[:2] + (block, chans), 2), lead_spec((next_heads, block, length), 1)],
                [jax.ShapeDtypeStruct(out_shape, BF16), jax.ShapeDtypeStruct((next_heads, cols, length), BF16)],
                [pltpu.VMEM((chans // 128, length * block, 128), F32), pltpu.VMEM((heads, length, length), F32),
                 pltpu.VMEM(w.shape[::-1], BF16), bias_scratch(block, length)] + attention_scratch(block, length, w, w_out),
                10 ** 10)(*z_parts, mask_t, *consts)


def gather(x, axis):
    return lax.all_gather(x, GROUP_AXIS, axis=axis, tiled=True)


def exchange(x):
    return lax.all_to_all(x, GROUP_AXIS, 0, 0, tiled=True)


def rejoin(x):
    pieces, rows, size, chans = x.shape
    return jnp.swapaxes(x, 0, 1).reshape(rows, pieces * size, chans)


def bias_weight(w):
    return jnp.pad(w.T, ((0, 8 - w.shape[1]), (0, 0)))


def solution(mesh):
    row_spec = P((PARTS_AXIS, GROUP_AXIS))

    def local_body(m, z, msa_mask, pair_mask, *weights):
        layers = weights[0].shape[0]
        pieces, parts = mesh.shape[GROUP_AXIS], 2
        res_loc = z.shape[0]
        shard = lax.axis_index(GROUP_AXIS)
        heads = weights[1].shape[2]
        pair_heads = weights[14].shape[2]
        row_bias_w = [bias_weight(weights[1][n]) for n in range(layers)]
        seq_mask, row_mask = msa_mask.astype(F32), pair_mask.astype(F32)
        bias = pair_bias(z, row_bias_w[0], heads)
        packed = gather(jnp.concatenate([bias, msa_mask.astype(BF16)[None], pair_mask.astype(BF16)[None]]), 1)
        bias = packed[:heads]
        masks_t = jnp.swapaxes(packed[heads:].astype(F32), 1, 2)
        full_mask_t = masks_t[0]
        res_mask_t, col_mask = (lax.dynamic_slice_in_dim(x, shard * res_loc, res_loc, 0) for x in masks_t)
        for n in range(layers):
            (row_qkvg, _, row_out, col_qkvg, col_out, mtr_in, mtr_out, opm_proj, opm_out, tmo_proj, tmo_out, tmi_proj, tmi_out,
             tas_qkvg, tas_bias, tas_out, tae_qkvg, tae_bias, tae_out, ptr_in, ptr_out) = (weight[n] for weight in weights)
            m = [exchange(row_attention(m, seq_mask, bias, n == 0, row_qkvg, row_out, pieces, p, parts)) for p in range(parts)]
            m, left, right = column_block(m, res_mask_t, heads, col_qkvg, col_out, mtr_in, mtr_out, opm_proj)
            right = gather(right, 1)
            done = [outer_block(left, right, z, res_mask_t, full_mask_t, row_mask, opm_out, tmo_proj, p, parts) for p in range(parts)]
            full = [gather(x[2], 1) for x in done]
            done = [outgoing(x[1], full, x[0], row_mask, tmo_proj, tmo_out, tmi_proj, pieces, p) for p, x in enumerate(done)]
            left, full = [exchange(x[1]) for x in done], [gather(x[2], 1) for x in done]
            z, bias = incoming(left, full, [x[0] for x in done], tmi_proj, tmi_out, bias_weight(tas_bias), pair_heads)
            bias = gather(bias, 1)
            done = [start_attention(z, row_mask, bias, tas_qkvg, tas_out, bias_weight(tae_bias), pieces, p, parts) for p in range(parts)]
            z = [exchange(x[0]) for x in done]
            bias = gather(jnp.concatenate([x[1] for x in done], axis=1), 1)
            z, bias, m = lax.optimization_barrier((z, bias, m))
            m = exchange(m)
            z, bias = end_attention(z, col_mask, bias, tae_qkvg, tae_out, ptr_in, ptr_out, row_bias_w[min(n + 1, layers - 1)], heads)
            z, bias, m = lax.optimization_barrier((z, bias, m))
            if n < layers - 1:
                bias = gather(bias, 1)
            z = exchange(z)
        return rejoin(m), rejoin(z)

    def run_blocks(*arrays):
        n_weights = len(arrays) - 4
        return jax.shard_map(local_body, mesh=mesh, in_specs=(row_spec,) * 4 + (P(),) * n_weights, out_specs=(row_spec, row_spec), check_vma=False)(*arrays)

    return run_blocks
```

time: 1740 us -> 1420 us (0.82)
  waiting for transfers between devices: 518 us -> 381 us
  Pallas kernels: 802 us -> 705 us
  blocking collectives: 279 us -> 218 us
  local copies, waits for them, and re-layouts: 85.4 us -> 33.4 us
  starting transfers between devices: 32.2 us -> 55.4 us
    all_to_all x7 -> x13, waiting for transfers between devices: 209 us -> 107 us  [exchange(): return lax.all_to_all(x, GROUP_AXIS, 0, 0, tiled=True)]
    pallas_call x14 -> x22, Pallas kernels: 790 us -> 692 us  [the longest x2 166 us: column_block(): call(functools.partial(col_kernel, heads, parts), (rows // block,), [lead...]
    all_gather x4, blocking collectives: 173 us -> 109 us  [gather(): return lax.all_gather(x, GROUP_AXIS, axis=axis, tiled=True)]
    all_to_all x10 -> x0, local copies, waits for them, and re-layouts: 35.6 us -> none  [exchange(): return lax.all_to_all(x, GROUP_AXIS, split, concat, tiled=True)]
    all_gather x8 -> x12, waiting for transfers between devices: 308 us -> 273 us  [gather(): return lax.all_gather(x, GROUP_AXIS, axis=axis, tiled=True)]
    pallas_call x6 -> x0, local copies, waits for them, and re-layouts: 24.4 us -> none  [the longest x2 13.2 us: row_attention(): call(functools.partial(row_kernel, transposed, heads), (seqs // block,),...]
    all_to_all x7 -> x13, starting transfers between devices: 31.4 us -> 54.2 us  [exchange(): return lax.all_to_all(x, GROUP_AXIS, 0, 0, tiled=True)]
  transfers between devices with their start and end apart: 15 -> 25, of which waited for: 12 -> 16; matrix products, arithmetic and copies ran while one was open for 3% -> 2% of each run, Pallas kernels for 7% -> 20%
where the time goes in v2:
time: 1420 us; the launch traced here: 1410 us
  Pallas kernels  705 us (50%)
  waiting for transfers between devices  381 us (27%)
  blocking collectives  218 us (15%)
  starting transfers between devices  55.4 us (4%)
  local copies, waits for them, and re-layouts  33.4 us (2%)
  between operations  15.2 us (1%)
    all_gather x12, waiting for transfers between devices, gather(): return lax.all_gather(x, GROUP_AXIS, axis=axis, tiled=True)  273 us
    pallas_call x2, Pallas kernels, column_block(): call(functools.partial(col_kernel, heads, parts), (rows // block,), [lead...  166 us
    pallas_call x4, Pallas kernels, row_attention(): call(functools.partial(row_kernel, transposed, heads), (steps,), [row_spe...  122 us
    all_gather x4, blocking collectives, gather(): return lax.all_gather(x, GROUP_AXIS, axis=axis, tiled=True)  109 us
    all_to_all x3, blocking collectives, exchange(): return lax.all_to_all(x, GROUP_AXIS, 0, 0, tiled=True)  109 us
    all_to_all x13, waiting for transfers between devices, exchange(): return lax.all_to_all(x, GROUP_AXIS, 0, 0, tiled=True)  107 us
    pallas_call x2, Pallas kernels, end_attention(): call(functools.partial(end_kernel, heads, parts), (cols // block,), [lead...  96.7 us
    pallas_call x4, Pallas kernels, outgoing(): call(functools.partial(outgoing_kernel, parts, pieces), (tri // block,),...  93.6 us
  transfers between devices with their start and end apart: 25, of which 16 were waited for; matrix products, arithmetic and copies ran while one was open for 2% of the time, Pallas kernels for 20%

profile of v2, /device:TPU:112, one launch (start us, length us, event | category | flops | bytes accessed | tf_op | source)
XLA Modules:
  0.0 1411.5 jit_solution(7330747732727152328)
XLA Ops:
  10.1 12.4 shard_map.248
  26.0 20.8 %all-gather.13.cloned.1.call-done = bf16[10,256,256]{2,1,0:T(8,128)(2,1)} async-done(((bf16[10,32,256]{2,1,0:T(8,128)(2,1)}), bf16[10,256,256]{2,1,0:T(8,128)(2,1)}) %all-gather.13.cloned.1.call-update) | async-done | bytes 1310736 | tf_op jit(solution)/shard_map/all_gather | solution.py:607
  49.0 30.8 %shard_map.249 = bf16[8,16,32,256]{3,2,1,0:T(8,128)(2,1)} custom-call(bf16[32,256,256]{2,1,0:T(8,128)(2,1)} %m_ref.3, f32[32,256]{1,0:T(8,128)} %get-tuple-element.160.mask_ref, bf16[8,256,256]{2,1,0:T(8,128)(2,1)} %slice.177.bias_ref, bf16[256,1024]{1,0:T(8,128)(2,1)} %get-tuple-element.125.w_ref, bf16[256,256]{1,0:T(8,128)(2,1)} %get-tuple-element.146.w_out_ref), custom_call_target="tpu_custom_call" | custom-call | flops 10000000000 | bytes 16777216 | tf_op jit(solution)/shard_map/pallas_call | solution.py:238
  83.6 30.8 %shard_map.250 = bf16[8,16,32,256]{3,2,1,0:T(8,128)(2,1)} custom-call(bf16[32,256,256]{2,1,0:T(8,128)(2,1)} %m_ref.3, f32[32,256]{1,0:T(8,128)} %get-tuple-element.160.mask_ref, bf16[8,256,256]{2,1,0:T(8,128)(2,1)} %slice.177.bias_ref, bf16[256,1024]{1,0:T(8,128)(2,1)} %get-tuple-element.125.w_ref, bf16[256,256]{1,0:T(8,128)(2,1)} %get-tuple-element.146.w_out_ref), custom_call_target="tpu_custom_call" | custom-call | flops 10000000000 | bytes 16777216 | tf_op jit(solution)/shard_map/pallas_call | solution.py:238
  126.0 21.5 %all-to-all-done.1.refs_1_ = bf16[8,16,32,256]{3,2,1,0:T(8,128)(2,1)} async-done(((bf16[8,16,32,256]{3,2,1,0:T(8,128)(2,1)}), bf16[8,16,32,256]{3,2,1,0:T(8,128)(2,1)}, u32[]{:S(2)}, u32[]{:S(2)}) %all-to-all-start.1) | async-done | bytes 2097184 | tf_op jit(solution)/shard_map/all_to_all | solution.py:611
  147.6 82.8 %shard_map.251 = (bf16[8,32,32,256]{3,2,1,0:T(8,128)(2,1)}, bf16[32,32,256]{2,1,0:T(8,128)(2,1)}, bf16[32,32,256]{2,1,0:T(8,128)(2,1)}) custom-call(bf16[8,16,32,256]{3,2,1,0:T(8,128)(2,1)} %copy-done.1, bf16[8,16,32,256]{3,2,1,0:T(8,128)(2,1)} %all-to-all-done.1.refs_1_, f32[32,256]{1,0:T(8,128)} %dynamic-slice_bitcast_fusion.1.refs_2_.rmask_ref, ...), custom_call_target="tpu_custom_call" | custom-call | flops 30000001024 | bytes 16777216 | tf_op jit(solution)/shard_map/pallas_call | solution.py:316
  232.3 25.4 %all-gather.15.cloned.1.call-done.b_ref = bf16[32,256,256]{2,1,0:T(8,128)(2,1)} async-done(((bf16[32,32,256]{2,1,0:T(8,128)(2,1)}), bf16[32,256,256]{2,1,0:T(8,128)(2,1)}) %all-gather.15.cloned.1.call-update) | async-done | bytes 4194320 | tf_op jit(solution)/shard_map/all_gather | solution.py:607
  257.7 18.4 %shard_map.252 = (bf16[16,256,128]{2,1,0:T(8,128)(2,1)}, bf16[128,16,256]{2,1,0:T(8,128)(2,1)}, bf16[128,16,256]{2,1,0:T(8,128)(2,1)}) custom-call(bf16[32,32,256]{2,1,0:T(8,128)(2,1)} %get-tuple-element.60.a_ref, bf16[32,256,256]{2,1,0:T(8,128)(2,1)} %all-gather.15.cloned.1.call-done.b_ref, bf16[32,256,128]{2,1,0:T(8,128)(2,1)} %z_ref.5, ...), custom_call_target="tpu_custom_call" | custom-call | flops 10000000000 | bytes 16777216 | tf_op jit(solution)/shard_map/pallas_call | solution.py:381
  276.2 18.4 %shard_map.253 = (bf16[16,256,128]{2,1,0:T(8,128)(2,1)}, bf16[128,16,256]{2,1,0:T(8,128)(2,1)}, bf16[128,16,256]{2,1,0:T(8,128)(2,1)}) custom-call(bf16[32,32,256]{2,1,0:T(8,128)(2,1)} %get-tuple-element.60.a_ref, bf16[32,256,256]{2,1,0:T(8,128)(2,1)} %all-gather.15.cloned.1.call-done.b_ref, bf16[32,256,128]{2,1,0:T(8,128)(2,1)} %z_ref.5, ...), custom_call_target="tpu_custom_call" | custom-call | flops 10000000000 | bytes 16777216 | tf_op jit(solution)/shard_map/pallas_call | solution.py:381
  296.1 25.4 %all-gather.17.cloned.1.call-done.refs_0_ = bf16[128,128,256]{2,1,0:T(8,128)(2,1)} async-done(((bf16[128,16,256]{2,1,0:T(8,128)(2,1)}), bf16[128,128,256]{2,1,0:T(8,128)(2,1)}) %all-gather.17.cloned.1.call-update) | async-done | bytes 8388624 | tf_op jit(solution)/shard_map/all_gather | solution.py:607
  321.6 47.1 %all-gather.19.cloned.1.call-done.refs_1_ = bf16[128,128,256]{2,1,0:T(8,128)(2,1)} async-done(((bf16[128,16,256]{2,1,0:T(8,128)(2,1)}), bf16[128,128,256]{2,1,0:T(8,128)(2,1)}) %all-gather.19.cloned.1.call-update) | async-done | bytes 8388624 | tf_op jit(solution)/shard_map/all_gather | solution.py:607
  368.7 23.3 %shard_map.254 = (bf16[16,256,128]{2,1,0:T(8,128)(2,1)}, bf16[8,16,32,128]{3,2,1,0:T(8,128)(2,1)}, bf16[128,16,256]{2,1,0:T(8,128)(2,1)}) custom-call(bf16[128,16,256]{2,1,0:T(8,128)(2,1)} %get-tuple-element.62.a_ref, bf16[128,128,256]{2,1,0:T(8,128)(2,1)} %all-gather.17.cloned.1.call-done.refs_0_, ...), custom_call_target="tpu_custom_call" | custom-call | flops 10000000000 | bytes 16777216 | tf_op jit(solution)/shard_map/pallas_call | solution.py:460
  392.2 23.4 %shard_map.255 = (bf16[16,256,128]{2,1,0:T(8,128)(2,1)}, bf16[8,16,32,128]{3,2,1,0:T(8,128)(2,1)}, bf16[128,16,256]{2,1,0:T(8,128)(2,1)}) custom-call(bf16[128,16,256]{2,1,0:T(8,128)(2,1)} %get-tuple-element.67.a_ref, bf16[128,128,256]{2,1,0:T(8,128)(2,1)} %all-gather.17.cloned.1.call-done.refs_0_, ...), custom_call_target="tpu_custom_call" | custom-call | flops 10000000000 | bytes 16777216 | tf_op jit(solution)/shard_map/pallas_call | solution.py:460
  415.7 30.8 %all_to_all.80.refs_0_ = bf16[8,16,32,128]{3,2,1,0:T(8,128)(2,1)} all-to-all(bf16[8,16,32,128]{3,2,1,0:T(8,128)(2,1)S(1)} %copy-done.10), channel_id=1, replica_groups=mesh['req'=2,'dap'=8] {'dap'}, dimensions={0} | all-to-all | bytes 2097152 | tf_op jit(solution)/shard_map/all_to_all | solution.py:611
  453.5 17.3 %all-to-all-done.3.refs_1_ = bf16[8,16,32,128]{3,2,1,0:T(8,128)(2,1)S(1)} async-done(((bf16[8,16,32,128]{3,2,1,0:T(8,128)(2,1)}), bf16[8,16,32,128]{3,2,1,0:T(8,128)(2,1)S(1)}, u32[]{:S(2)}, u32[]{:S(2)}) %all-to-all-start.3) | async-done | bytes 1048608 | tf_op jit(solution)/shard_map/all_to_all | solution.py:611
  470.7 29.9 %all-gather.23.cloned.1.call-done.refs_3_ = bf16[128,128,256]{2,1,0:T(8,128)(2,1)} async-done(((bf16[128,16,256]{2,1,0:T(8,128)(2,1)}), bf16[128,128,256]{2,1,0:T(8,128)(2,1)}) %all-gather.23.cloned.1.call-update) | async-done | bytes 8388624 | tf_op jit(solution)/shard_map/all_gather | solution.py:607
  500.6 34.8 %shard_map.256 = (bf16[32,256,128]{2,1,0:T(8,128)(2,1)}, bf16[4,32,256]{2,1,0:T(8,128)(2,1)}) custom-call(bf16[8,16,32,128]{3,2,1,0:T(8,128)(2,1)} %all_to_all.80.refs_0_, bf16[8,16,32,128]{3,2,1,0:T(8,128)(2,1)} %copy-done.7, bf16[128,128,256]{2,1,0:T(8,128)(2,1)} %all-gather.21.cloned.1.call-done.refs_2_, ...), custom_call_target="tpu_custom_call" | custom-call | flops 10000000000 | bytes 16777216 | tf_op jit(solution)/shard_map/pallas_call | solution.py:513
  535.5 23.0 %all_gather.54.bias_ref = bf16[4,256,256]{2,1,0:T(8,128)(2,1)} all-gather(bf16[4,32,256]{2,1,0:T(8,128)(2,1)} %get-tuple-element.75), channel_id=1, replica_groups=mesh['req'=2,'dap'=8] {'dap'}, dimensions={1}, use_global_device_ids=true | all-gather | bytes 589824 | tf_op jit(solution)/shard_map/all_gather | solution.py:607
  558.5 17.7 %shard_map.257 = (bf16[8,16,32,128]{3,2,1,0:T(8,128)(2,1)}, bf16[4,16,256]{2,1,0:T(8,128)(2,1)}) custom-call(bf16[32,256,128]{2,1,0:T(8,128)(2,1)} %get-tuple-element.74.z_ref, f32[32,256]{1,0:T(8,128)} %get-tuple-element.168.pmask_ref.refs_3_.mask_ref, bf16[4,256,256]{2,1,0:T(8,128)(2,1)} %all_gather.54.bias_ref, ...), custom_call_target="tpu_custom_call" | custom-call | flops 10000000000 | bytes 16777216 | tf_op jit(solution)/shard_map/pallas_call | solution.py:550
  580.0 17.7 %shard_map.258 = (bf16[8,16,32,128]{3,2,1,0:T(8,128)(2,1)}, bf16[4,16,256]{2,1,0:T(8,128)(2,1)}) custom-call(bf16[32,256,128]{2,1,0:T(8,128)(2,1)} %get-tuple-element.74.z_ref, f32[32,256]{1,0:T(8,128)} %get-tuple-element.168.pmask_ref.refs_3_.mask_ref, bf16[4,256,256]{2,1,0:T(8,128)(2,1)} %all_gather.54.bias_ref, ...), custom_call_target="tpu_custom_call" | custom-call | flops 10000000000 | bytes 16777216 | tf_op jit(solution)/shard_map/pallas_call | solution.py:550
  602.4 31.6 %all_gather.55.refs_3_ = bf16[4,256,256]{2,1,0:T(8,128)(2,1)} all-gather(bf16[4,32,256]{2,1,0:T(8,128)(2,1)S(1)} %pad_maximum_fusion.1), channel_id=1, replica_groups=mesh['req'=2,'dap'=8] {'dap'}, dimensions={1}, use_global_device_ids=true | all-gather | bytes 589824 | tf_op jit(solution)/shard_map/all_gather | solution.py:607
  635.0 4.7 all-to-all-start.6
  642.8 48.3 %shard_map.259 = (bf16[8,32,32,128]{3,2,1,0:T(8,128)(2,1)}, bf16[8,32,256]{2,1,0:T(8,128)(2,1)}) custom-call(bf16[8,16,32,128]{3,2,1,0:T(8,128)(2,1)} %copy-done.5, bf16[8,16,32,128]{3,2,1,0:T(8,128)(2,1)} %copy-done.8, f32[32,256]{1,0:T(8,128)} %dynamic-slice_bitcast_fusion.refs_2_, bf16[4,256,256]{2,1,0:T(8,128)(2,1)} %all_gather.55.refs_3_, ...), custom_call_target="tpu_custom_call" | custom-call | flops 10000000000 | bytes 16777216 | tf_op jit(solution)/shard_map/pallas_call | solution.py:597
  691.2 20.6 %all-gather.25.cloned.1.call-done.bias_ref = bf16[8,256,256]{2,1,0:T(8,128)(2,1)} async-done(((bf16[8,32,256]{2,1,0:T(8,128)(2,1)}), bf16[8,256,256]{2,1,0:T(8,128)(2,1)}) %all-gather.25.cloned.1.call-update) | async-done | bytes 1048592 | tf_op jit(solution)/shard_map/all_gather | solution.py:607
  711.9 30.3 %shard_map.260 = bf16[8,16,32,256]{3,2,1,0:T(8,128)(2,1)} custom-call(bf16[8,32,32,256]{3,2,1,0:T(8,128)(2,1)} %all-to-all-done.6.m_ref, f32[32,256]{1,0:T(8,128)} %get-tuple-element.160.mask_ref, bf16[8,256,256]{2,1,0:T(8,128)(2,1)} %all-gather.25.cloned.1.call-done.bias_ref, bf16[256,1024]{1,0:T(8,128)(2,1)} %get-tuple-element.124.w_ref, ...), custom_call_target="tpu_custom_call" | custom-call | flops 10000000000 | bytes 16777216 | tf_op jit(solution)/shard_map/pallas_call | solution.py:238
  746.0 30.4 %shard_map.261 = bf16[8,16,32,256]{3,2,1,0:T(8,128)(2,1)} custom-call(bf16[8,32,32,256]{3,2,1,0:T(8,128)(2,1)} %all-to-all-done.6.m_ref, f32[32,256]{1,0:T(8,128)} %get-tuple-element.160.mask_ref, bf16[8,256,256]{2,1,0:T(8,128)(2,1)} %all-gather.25.cloned.1.call-done.bias_ref, bf16[256,1024]{1,0:T(8,128)(2,1)} %get-tuple-element.124.w_ref, ...), custom_call_target="tpu_custom_call" | custom-call | flops 10000000000 | bytes 16777216 | tf_op jit(solution)/shard_map/pallas_call | solution.py:238
  783.1 26.4 %all-to-all-done.8.refs_1_ = bf16[8,16,32,256]{3,2,1,0:T(8,128)(2,1)} async-done(((bf16[8,16,32,256]{3,2,1,0:T(8,128)(2,1)}), bf16[8,16,32,256]{3,2,1,0:T(8,128)(2,1)}, u32[]{:S(2)}, u32[]{:S(2)}) %all-to-all-start.8) | async-done | bytes 2097184 | tf_op jit(solution)/shard_map/all_to_all | solution.py:611
  809.5 82.8 %shard_map.262 = (bf16[8,32,32,256]{3,2,1,0:T(8,128)(2,1)}, bf16[32,32,256]{2,1,0:T(8,128)(2,1)}, bf16[32,32,256]{2,1,0:T(8,128)(2,1)}) custom-call(bf16[8,16,32,256]{3,2,1,0:T(8,128)(2,1)} %copy-done.2, bf16[8,16,32,256]{3,2,1,0:T(8,128)(2,1)} %all-to-all-done.8.refs_1_, f32[32,256]{1,0:T(8,128)} %dynamic-slice_bitcast_fusion.1.refs_2_.rmask_ref, ...), custom_call_target="tpu_custom_call" | custom-call | flops 30000001024 | bytes 16777216 | tf_op jit(solution)/shard_map/pallas_call | solution.py:316
  892.5 47.5 %all_to_all.81.z_ref = bf16[8,32,32,128]{3,2,1,0:T(8,128)(2,1)} all-to-all(bf16[8,32,32,128]{3,2,1,0:T(8,128)(2,1)S(1)} %copy-done), channel_id=1, replica_groups=mesh['req'=2,'dap'=8] {'dap'}, dimensions={0} | all-to-all | bytes 4194304 | tf_op jit(solution)/shard_map/all_to_all | solution.py:611
  940.3 18.4 %shard_map.263 = (bf16[16,256,128]{2,1,0:T(8,128)(2,1)}, bf16[128,16,256]{2,1,0:T(8,128)(2,1)}, bf16[128,16,256]{2,1,0:T(8,128)(2,1)}) custom-call(bf16[32,32,256]{2,1,0:T(8,128)(2,1)} %get-tuple-element.89.a_ref, bf16[32,256,256]{2,1,0:T(8,128)(2,1)} %all-gather.27.cloned.1.call-done.b_ref, bf16[8,32,32,128]{3,2,1,0:T(8,128)(2,1)} %all_to_all.81.z_ref, ...), custom_call_target="tpu_custom_call" | custom-call | flops 10000000000 | bytes 16777216 | tf_op jit(solution)/shard_map/pallas_call | solution.py:381
  958.9 18.4 %shard_map.264 = (bf16[16,256,128]{2,1,0:T(8,128)(2,1)}, bf16[128,16,256]{2,1,0:T(8,128)(2,1)}, bf16[128,16,256]{2,1,0:T(8,128)(2,1)}) custom-call(bf16[32,32,256]{2,1,0:T(8,128)(2,1)} %get-tuple-element.89.a_ref, bf16[32,256,256]{2,1,0:T(8,128)(2,1)} %all-gather.27.cloned.1.call-done.b_ref, bf16[8,32,32,128]{3,2,1,0:T(8,128)(2,1)} %all_to_all.81.z_ref, ...), custom_call_target="tpu_custom_call" | custom-call | flops 10000000000 | bytes 16777216 | tf_op jit(solution)/shard_map/pallas_call | solution.py:381
  977.4 26.6 %all-gather.29.cloned.1.call-done.refs_0_ = bf16[128,128,256]{2,1,0:T(8,128)(2,1)} async-done(((bf16[128,16,256]{2,1,0:T(8,128)(2,1)}), bf16[128,128,256]{2,1,0:T(8,128)(2,1)}) %all-gather.29.cloned.1.call-update) | async-done | bytes 8388624 | tf_op jit(solution)/shard_map/all_gather | solution.py:607
  1004.0 47.1 %all-gather.31.cloned.1.call-done.refs_1_ = bf16[128,128,256]{2,1,0:T(8,128)(2,1)} async-done(((bf16[128,16,256]{2,1,0:T(8,128)(2,1)}), bf16[128,128,256]{2,1,0:T(8,128)(2,1)}) %all-gather.31.cloned.1.call-update) | async-done | bytes 8388624 | tf_op jit(solution)/shard_map/all_gather | solution.py:607
  1051.1 23.5 %shard_map.265 = (bf16[16,256,128]{2,1,0:T(8,128)(2,1)}, bf16[8,16,32,128]{3,2,1,0:T(8,128)(2,1)}, bf16[128,16,256]{2,1,0:T(8,128)(2,1)}) custom-call(bf16[128,16,256]{2,1,0:T(8,128)(2,1)} %get-tuple-element.92.a_ref, bf16[128,128,256]{2,1,0:T(8,128)(2,1)} %all-gather.29.cloned.1.call-done.refs_0_, ...), custom_call_target="tpu_custom_call" | custom-call | flops 10000000000 | bytes 16777216 | tf_op jit(solution)/shard_map/pallas_call | solution.py:460
  1074.7 23.4 %shard_map.266 = (bf16[16,256,128]{2,1,0:T(8,128)(2,1)}, bf16[8,16,32,128]{3,2,1,0:T(8,128)(2,1)}, bf16[128,16,256]{2,1,0:T(8,128)(2,1)}) custom-call(bf16[128,16,256]{2,1,0:T(8,128)(2,1)} %get-tuple-element.97.a_ref, bf16[128,128,256]{2,1,0:T(8,128)(2,1)} %all-gather.29.cloned.1.call-done.refs_0_, ...), custom_call_target="tpu_custom_call" | custom-call | flops 10000000000 | bytes 16777216 | tf_op jit(solution)/shard_map/pallas_call | solution.py:460
  1098.2 30.6 %all_to_all.82.refs_0_ = bf16[8,16,32,128]{3,2,1,0:T(8,128)(2,1)} all-to-all(bf16[8,16,32,128]{3,2,1,0:T(8,128)(2,1)S(1)} %copy-done.11), channel_id=1, replica_groups=mesh['req'=2,'dap'=8] {'dap'}, dimensions={0} | all-to-all | bytes 2097152 | tf_op jit(solution)/shard_map/all_to_all | solution.py:611
  1133.8 19.1 %all-to-all-done.11.refs_1_ = bf16[8,16,32,128]{3,2,1,0:T(8,128)(2,1)S(1)} async-done(((bf16[8,16,32,128]{3,2,1,0:T(8,128)(2,1)}), bf16[8,16,32,128]{3,2,1,0:T(8,128)(2,1)S(1)}, u32[]{:S(2)}, u32[]{:S(2)}) %all-to-all-start.11) | async-done | bytes 1048608 | tf_op jit(solution)/shard_map/all_to_all | solution.py:611
  1152.9 30.1 %all-gather.35.cloned.1.call-done.refs_3_ = bf16[128,128,256]{2,1,0:T(8,128)(2,1)} async-done(((bf16[128,16,256]{2,1,0:T(8,128)(2,1)}), bf16[128,128,256]{2,1,0:T(8,128)(2,1)}) %all-gather.35.cloned.1.call-update) | async-done | bytes 8388624 | tf_op jit(solution)/shard_map/all_gather | solution.py:607
  1183.0 34.8 %shard_map.267 = (bf16[32,256,128]{2,1,0:T(8,128)(2,1)}, bf16[4,32,256]{2,1,0:T(8,128)(2,1)}) custom-call(bf16[8,16,32,128]{3,2,1,0:T(8,128)(2,1)} %all_to_all.82.refs_0_, bf16[8,16,32,128]{3,2,1,0:T(8,128)(2,1)} %copy-done.9, bf16[128,128,256]{2,1,0:T(8,128)(2,1)} %all-gather.33.cloned.1.call-done.refs_2_, ...), custom_call_target="tpu_custom_call" | custom-call | flops 10000000000 | bytes 16777216 | tf_op jit(solution)/shard_map/pallas_call | solution.py:513
  1217.8 22.9 %all_gather.62.bias_ref = bf16[4,256,256]{2,1,0:T(8,128)(2,1)} all-gather(bf16[4,32,256]{2,1,0:T(8,128)(2,1)} %get-tuple-element.105), channel_id=1, replica_groups=mesh['req'=2,'dap'=8] {'dap'}, dimensions={1}, use_global_device_ids=true | all-gather | bytes 589824 | tf_op jit(solution)/shard_map/all_gather | solution.py:607
  1240.7 17.7 %shard_map.268 = (bf16[8,16,32,128]{3,2,1,0:T(8,128)(2,1)}, bf16[4,16,256]{2,1,0:T(8,128)(2,1)}) custom-call(bf16[32,256,128]{2,1,0:T(8,128)(2,1)} %get-tuple-element.104.z_ref, f32[32,256]{1,0:T(8,128)} %get-tuple-element.168.pmask_ref.refs_3_.mask_ref, bf16[4,256,256]{2,1,0:T(8,128)(2,1)} %all_gather.62.bias_ref, ...), custom_call_target="tpu_custom_call" | custom-call | flops 10000000000 | bytes 16777216 | tf_op jit(solution)/shard_map/pallas_call | solution.py:550
  1262.2 17.7 %shard_map.269 = (bf16[8,16,32,128]{3,2,1,0:T(8,128)(2,1)}, bf16[4,16,256]{2,1,0:T(8,128)(2,1)}) custom-call(bf16[32,256,128]{2,1,0:T(8,128)(2,1)} %get-tuple-element.104.z_ref, f32[32,256]{1,0:T(8,128)} %get-tuple-element.168.pmask_ref.refs_3_.mask_ref, bf16[4,256,256]{2,1,0:T(8,128)(2,1)} %all_gather.62.bias_ref, ...), custom_call_target="tpu_custom_call" | custom-call | flops 10000000000 | bytes 16777216 | tf_op jit(solution)/shard_map/pallas_call | solution.py:550
  1280.0 4.6 all-to-all-start.13
  1284.6 31.6 %all_gather.63.refs_3_ = bf16[4,256,256]{2,1,0:T(8,128)(2,1)} all-gather(bf16[4,32,256]{2,1,0:T(8,128)(2,1)S(1)} %pad_maximum_fusion.2), channel_id=1, replica_groups=mesh['req'=2,'dap'=8] {'dap'}, dimensions={1}, use_global_device_ids=true | all-gather | bytes 589824 | tf_op jit(solution)/shard_map/all_gather | solution.py:607
  1317.2 4.7 all-to-all-start.14
  1322.0 48.4 %shard_map.270 = (bf16[8,32,32,128]{3,2,1,0:T(8,128)(2,1)}, bf16[8,32,256]{2,1,0:T(8,128)(2,1)}) custom-call(bf16[8,16,32,128]{3,2,1,0:T(8,128)(2,1)} %copy-done.6, bf16[8,16,32,128]{3,2,1,0:T(8,128)(2,1)} %copy-done.12, f32[32,256]{1,0:T(8,128)} %dynamic-slice_bitcast_fusion.refs_2_, bf16[4,256,256]{2,1,0:T(8,128)(2,1)} %all_gather.63.refs_3_, ...), custom_call_target="tpu_custom_call" | custom-call | flops 10000000000 | bytes 16777216 | tf_op jit(solution)/shard_map/pallas_call | solution.py:597
  1375.2 4.8 copy.46
  1380.1 22.1 %all-to-all-done.15 = bf16[8,32,32,128]{3,2,1,0:T(8,128)(2,1)S(1)} async-done(((bf16[8,32,32,128]{3,2,1,0:T(8,128)(2,1)}), bf16[8,32,32,128]{3,2,1,0:T(8,128)(2,1)S(1)}, u32[]{:S(2)}, u32[]{:S(2)}) %all-to-all-start.15) | async-done | bytes 2097184 | tf_op jit(solution)/shard_map/all_to_all | solution.py:611
  (153 shorter events, 75.0 us)
Async XLA Ops:
  7.2 17.0 %copy-start.18 = (bf16[2,256,256]{2,1,0:T(8,128)(2,1)S(1)}, bf16[2,256,256]{2,1,0:T(8,128)(2,1)}, u32[]{:S(2)}) copy-start(bf16[2,256,256]{2,1,0:T(8,128)(2,1)} %param.31) | copy-start | bytes 786436
  7.2 17.7 %copy-start.3 = (bf16[2,256,1024]{2,1,0:T(8,128)(2,1)S(1)}, bf16[2,256,1024]{2,1,0:T(8,128)(2,1)}, u32[]{:S(2)}) copy-start(bf16[2,256,1024]{2,1,0:T(8,128)(2,1)} %param.29) | copy-start | bytes 3145732
  7.2 39.5 %all-gather.13.cloned.1.call-start = ((), (), s32[]{:S(2)}) async-start(), calls=%async_computation.16 | async-start | bytes 1474560 | tf_op jit(solution)/shard_map/all_gather | solution.py:607
  79.8 34.7 %all-to-all-start = ((bf16[8,16,32,256]{3,2,1,0:T(8,128)(2,1)}), bf16[8,16,32,256]{3,2,1,0:T(8,128)(2,1)S(1)}, u32[]{:S(2)}, u32[]{:S(2)}) async-start(bf16[8,16,32,256]{3,2,1,0:T(8,128)(2,1)} %shard_map.249), calls=%async_computation | async-start | bytes 4194304 | tf_op jit(solution)/shard_map/all_to_all | solution.py:611
  114.5 6.8 copy-start.19
  114.5 7.5 copy-start.4
  115.8 31.7 %all-to-all-start.1 = ((bf16[8,16,32,256]{3,2,1,0:T(8,128)(2,1)}), bf16[8,16,32,256]{3,2,1,0:T(8,128)(2,1)}, u32[]{:S(2)}, u32[]{:S(2)}) async-start(bf16[8,16,32,256]{3,2,1,0:T(8,128)(2,1)} %shard_map.250), calls=%async_computation.1 | async-start | bytes 4194304 | tf_op jit(solution)/shard_map/all_to_all | solution.py:611
  120.4 137.3 %all-gather.15.cloned.1.call-start = ((), (), s32[]{:S(2)}) async-start(), calls=%async_computation.17 | async-start | bytes 4718592 | tf_op jit(solution)/shard_map/all_gather | solution.py:607
  147.5 83.1 %copy-start.16 = (bf16[2,128,640]{2,1,0:T(8,128)(2,1)S(1)}, bf16[2,128,640]{2,1,0:T(8,128)(2,1)}, u32[]{:S(2)}) copy-start(bf16[2,128,640]{2,1,0:T(8,128)(2,1)} %param.38) | copy-start | bytes 983044
  147.5 83.9 %copy-start.15 = (bf16[2,1024,128]{2,1,0:T(8,128)(2,1)S(1)}, bf16[2,1024,128]{2,1,0:T(8,128)(2,1)}, u32[]{:S(2)}) copy-start(bf16[2,1024,128]{2,1,0:T(8,128)(2,1)} %param.37) | copy-start | bytes 1572868
  230.4 91.2 %all-gather.17.cloned.1.call-start = ((), (), s32[]{:S(2)}) async-start(), calls=%async_computation.18 | async-start | bytes 9437184 | tf_op jit(solution)/shard_map/all_gather | solution.py:607
  276.1 18.6 %copy-start.25 = (bf16[2,128,128]{2,1,0:T(8,128)(2,1)S(1)}, bf16[2,128,128]{2,1,0:T(8,128)(2,1)}, u32[]{:S(2)}) copy-start(bf16[2,128,128]{2,1,0:T(8,128)(2,1)} %param.39) | copy-start | bytes 196612
  276.1 19.2 %copy-start.17 = (bf16[2,128,640]{2,1,0:T(8,128)(2,1)S(1)}, bf16[2,128,640]{2,1,0:T(8,128)(2,1)}, u32[]{:S(2)}) copy-start(bf16[2,128,640]{2,1,0:T(8,128)(2,1)} %param.40) | copy-start | bytes 983044
  276.1 92.6 %all-gather.19.cloned.1.call-start = ((), (), s32[]{:S(2)}) async-start(), calls=%async_computation.19 | async-start | bytes 9437184 | tf_op jit(solution)/shard_map/all_gather | solution.py:607
  294.6 176.1 %all-gather.21.cloned.1.call-start = ((), (), s32[]{:S(2)}) async-start(), calls=%async_computation.20 | async-start | bytes 9437184 | tf_op jit(solution)/shard_map/all_gather | solution.py:607
  392.1 108.5 %all-gather.23.cloned.1.call-start = ((), (), s32[]{:S(2)}) async-start(), calls=%async_computation.21 | async-start | bytes 9437184 | tf_op jit(solution)/shard_map/all_gather | solution.py:607
  392.2 23.5 %copy-start.10 = (bf16[8,16,32,128]{3,2,1,0:T(8,128)(2,1)S(1)}, bf16[8,16,32,128]{3,2,1,0:T(8,128)(2,1)}, u32[]{:S(2)}) copy-start(bf16[8,16,32,128]{3,2,1,0:T(8,128)(2,1)} %get-tuple-element.66) | copy-start | bytes 3145732
  415.6 34.6 %copy-start.33 = (bf16[2,128,4]{1,2,0:T(4,128)(2,1)S(1)}, bf16[2,128,4]{1,2,0:T(4,128)(2,1)}, u32[]{:S(2)}) copy-start(bf16[2,128,4]{1,2,0:T(4,128)(2,1)} %param.43) | copy-start | bytes 6148
  415.6 35.2 %copy-start.34 = (bf16[2,128,4]{1,2,0:T(4,128)(2,1)S(1)}, bf16[2,128,4]{1,2,0:T(4,128)(2,1)}, u32[]{:S(2)}) copy-start(bf16[2,128,4]{1,2,0:T(4,128)(2,1)} %param.46) | copy-start | bytes 6148
  415.6 35.8 %copy-start.26 = (bf16[2,128,128]{2,1,0:T(8,128)(2,1)S(1)}, bf16[2,128,128]{2,1,0:T(8,128)(2,1)}, u32[]{:S(2)}) copy-start(bf16[2,128,128]{2,1,0:T(8,128)(2,1)} %param.41) | copy-start | bytes 196612
  415.7 36.4 %copy-start.27 = (bf16[2,128,128]{2,1,0:T(8,128)(2,1)S(1)}, bf16[2,128,128]{2,1,0:T(8,128)(2,1)}, u32[]{:S(2)}) copy-start(bf16[2,128,128]{2,1,0:T(8,128)(2,1)} %param.44) | copy-start | bytes 196612
  415.7 37.1 %copy-start.20 = (bf16[2,128,512]{2,1,0:T(8,128)(2,1)S(1)}, bf16[2,128,512]{2,1,0:T(8,128)(2,1)}, u32[]{:S(2)}) copy-start(bf16[2,128,512]{2,1,0:T(8,128)(2,1)} %param.42) | copy-start | bytes 786436
  446.5 24.3 %all-to-all-start.3 = ((bf16[8,16,32,128]{3,2,1,0:T(8,128)(2,1)}), bf16[8,16,32,128]{3,2,1,0:T(8,128)(2,1)S(1)}, u32[]{:S(2)}, u32[]{:S(2)}) async-start(bf16[8,16,32,128]{3,2,1,0:T(8,128)(2,1)} %get-tuple-element.69), calls=%async_computation.3 | async-start | bytes 2097152 | tf_op jit(solution)/shard_map/all_to_all | solution.py:611
  470.7 29.9 %copy-start.7 = (bf16[8,16,32,128]{3,2,1,0:T(8,128)(2,1)}, bf16[8,16,32,128]{3,2,1,0:T(8,128)(2,1)S(1)}, u32[]{:S(2)}) copy-start(bf16[8,16,32,128]{3,2,1,0:T(8,128)(2,1)S(1)} %all-to-all-done.3.refs_1_) | copy-start | bytes 3145732
  576.2 21.5 %all-to-all-start.4 = ((bf16[8,16,32,128]{3,2,1,0:T(8,128)(2,1)}), bf16[8,16,32,128]{3,2,1,0:T(8,128)(2,1)S(1)}, u32[]{:S(2)}, u32[]{:S(2)}) async-start(bf16[8,16,32,128]{3,2,1,0:T(8,128)(2,1)} %get-tuple-element.76), calls=%async_computation.4 | async-start | bytes 2097152 | tf_op jit(solution)/shard_map/all_to_all | solution.py:611
  597.8 36.3 %copy-start.5 = (bf16[8,16,32,128]{3,2,1,0:T(8,128)(2,1)}, bf16[8,16,32,128]{3,2,1,0:T(8,128)(2,1)S(1)}, u32[]{:S(2)}) copy-start(bf16[8,16,32,128]{3,2,1,0:T(8,128)(2,1)S(1)} %all-to-all-done.4.refs_0_) | copy-start | bytes 3145732
  597.8 36.2 %all-to-all-start.5 = ((bf16[8,16,32,128]{3,2,1,0:T(8,128)(2,1)}), bf16[8,16,32,128]{3,2,1,0:T(8,128)(2,1)S(1)}, u32[]{:S(2)}, u32[]{:S(2)}) async-start(bf16[8,16,32,128]{3,2,1,0:T(8,128)(2,1)} %get-tuple-element.77), calls=%async_computation.5 | async-start | bytes 2097152 | tf_op jit(solution)/shard_map/all_to_all | solution.py:611
  634.0 6.6 copy-start.21
  634.0 7.4 copy-start.22
  634.0 7.4 copy-start.23
  635.0 56.2 %all-to-all-start.6 = ((bf16[8,32,32,256]{3,2,1,0:T(8,128)(2,1)}), bf16[8,32,32,256]{3,2,1,0:T(8,128)(2,1)}, u32[]{:S(2)}, u32[]{:S(2)}) async-start(bf16[8,32,32,256]{3,2,1,0:T(8,128)(2,1)} %get-tuple-element.86), calls=%async_computation.6 | async-start | bytes 8388608 | tf_op jit(solution)/shard_map/all_to_all | solution.py:611
  639.8 72.1 %all-gather.25.cloned.1.call-start = ((), (), s32[]{:S(2)}) async-start(), calls=%async_computation.22 | async-start | bytes 1179648 | tf_op jit(solution)/shard_map/all_gather | solution.py:607
  742.2 34.2 %all-to-all-start.7 = ((bf16[8,16,32,256]{3,2,1,0:T(8,128)(2,1)}), bf16[8,16,32,256]{3,2,1,0:T(8,128)(2,1)S(1)}, u32[]{:S(2)}, u32[]{:S(2)}) async-start(bf16[8,16,32,256]{3,2,1,0:T(8,128)(2,1)} %shard_map.260), calls=%async_computation.7 | async-start | bytes 4194304 | tf_op jit(solution)/shard_map/all_to_all | solution.py:611
  777.8 31.7 %all-to-all-start.8 = ((bf16[8,16,32,256]{3,2,1,0:T(8,128)(2,1)}), bf16[8,16,32,256]{3,2,1,0:T(8,128)(2,1)}, u32[]{:S(2)}, u32[]{:S(2)}) async-start(bf16[8,16,32,256]{3,2,1,0:T(8,128)(2,1)} %shard_map.261), calls=%async_computation.8 | async-start | bytes 4194304 | tf_op jit(solution)/shard_map/all_to_all | solution.py:611
  782.3 158.0 %all-gather.27.cloned.1.call-start = ((), (), s32[]{:S(2)}) async-start(), calls=%async_computation.23 | async-start | bytes 4718592 | tf_op jit(solution)/shard_map/all_gather | solution.py:607
  809.5 83.0 %copy-start = (bf16[8,32,32,128]{3,2,1,0:T(8,128)(2,1)S(1)}, bf16[8,32,32,128]{3,2,1,0:T(8,128)(2,1)}, u32[]{:S(2)}) copy-start(bf16[8,32,32,128]{3,2,1,0:T(8,128)(2,1)} %get-tuple-element.91) | copy-start | bytes 6291460
  892.4 111.6 %all-gather.29.cloned.1.call-start = ((), (), s32[]{:S(2)}) async-start(), calls=%async_computation.24 | async-start | bytes 9437184 | tf_op jit(solution)/shard_map/all_gather | solution.py:607
  958.8 92.3 %all-gather.31.cloned.1.call-start = ((), (), s32[]{:S(2)}) async-start(), calls=%async_computation.25 | async-start | bytes 9437184 | tf_op jit(solution)/shard_map/all_gather | solution.py:607
  977.3 175.6 %all-gather.33.cloned.1.call-start = ((), (), s32[]{:S(2)}) async-start(), calls=%async_computation.26 | async-start | bytes 9437184 | tf_op jit(solution)/shard_map/all_gather | solution.py:607
  1074.7 108.4 %all-gather.35.cloned.1.call-start = ((), (), s32[]{:S(2)}) async-start(), calls=%async_computation.27 | async-start | bytes 9437184 | tf_op jit(solution)/shard_map/all_gather | solution.py:607
  1074.7 23.5 %copy-start.11 = (bf16[8,16,32,128]{3,2,1,0:T(8,128)(2,1)S(1)}, bf16[8,16,32,128]{3,2,1,0:T(8,128)(2,1)}, u32[]{:S(2)}) copy-start(bf16[8,16,32,128]{3,2,1,0:T(8,128)(2,1)} %get-tuple-element.96) | copy-start | bytes 3145732
  1128.8 24.1 %all-to-all-start.11 = ((bf16[8,16,32,128]{3,2,1,0:T(8,128)(2,1)}), bf16[8,16,32,128]{3,2,1,0:T(8,128)(2,1)S(1)}, u32[]{:S(2)}, u32[]{:S(2)}) async-start(bf16[8,16,32,128]{3,2,1,0:T(8,128)(2,1)} %get-tuple-element.99), calls=%async_computation.11 | async-start | bytes 2097152 | tf_op jit(solution)/shard_map/all_to_all | solution.py:611
  1152.9 30.1 %copy-start.9 = (bf16[8,16,32,128]{3,2,1,0:T(8,128)(2,1)}, bf16[8,16,32,128]{3,2,1,0:T(8,128)(2,1)S(1)}, u32[]{:S(2)}) copy-start(bf16[8,16,32,128]{3,2,1,0:T(8,128)(2,1)S(1)} %all-to-all-done.11.refs_1_) | copy-start | bytes 3145732
  1258.5 21.5 %all-to-all-start.12 = ((bf16[8,16,32,128]{3,2,1,0:T(8,128)(2,1)}), bf16[8,16,32,128]{3,2,1,0:T(8,128)(2,1)S(1)}, u32[]{:S(2)}, u32[]{:S(2)}) async-start(bf16[8,16,32,128]{3,2,1,0:T(8,128)(2,1)} %get-tuple-element.106), calls=%async_computation.12 | async-start | bytes 2097152 | tf_op jit(solution)/shard_map/all_to_all | solution.py:611
  1280.0 36.3 %copy-start.6 = (bf16[8,16,32,128]{3,2,1,0:T(8,128)(2,1)}, bf16[8,16,32,128]{3,2,1,0:T(8,128)(2,1)S(1)}, u32[]{:S(2)}) copy-start(bf16[8,16,32,128]{3,2,1,0:T(8,128)(2,1)S(1)} %all-to-all-done.12.refs_0_) | copy-start | bytes 3145732
  1280.0 36.2 %all-to-all-start.13 = ((bf16[8,16,32,128]{3,2,1,0:T(8,128)(2,1)}), bf16[8,16,32,128]{3,2,1,0:T(8,128)(2,1)S(1)}, u32[]{:S(2)}, u32[]{:S(2)}) async-start(bf16[8,16,32,128]{3,2,1,0:T(8,128)(2,1)} %get-tuple-element.107), calls=%async_computation.13 | async-start | bytes 2097152 | tf_op jit(solution)/shard_map/all_to_all | solution.py:611
  1317.2 54.2 %all-to-all-start.14 = ((bf16[8,32,32,256]{3,2,1,0:T(8,128)(2,1)}), bf16[8,32,32,256]{3,2,1,0:T(8,128)(2,1)}, u32[]{:S(2)}, u32[]{:S(2)}) async-start(bf16[8,32,32,256]{3,2,1,0:T(8,128)(2,1)} %get-tuple-element.115), calls=%async_computation.14 | async-start | bytes 8388608 | tf_op jit(solution)/shard_map/all_to_all | solution.py:611
  1371.4 30.8 %all-to-all-start.15 = ((bf16[8,32,32,128]{3,2,1,0:T(8,128)(2,1)}), bf16[8,32,32,128]{3,2,1,0:T(8,128)(2,1)S(1)}, u32[]{:S(2)}, u32[]{:S(2)}) async-start(bf16[8,32,32,128]{3,2,1,0:T(8,128)(2,1)} %get-tuple-element.117), calls=%async_computation.15 | async-start | bytes 4194304 | tf_op jit(solution)/shard_map/all_to_all | solution.py:611
  (13 other events, 41.1 us)
Sparse Core Ops, SparseCore 0:
  24.3 22.3 all-gather.12
  230.5 27.1 all-gather.14
  276.2 45.3 all-gather.16
  323.0 45.6 all-gather.18
  392.2 56.9 all-gather.20
  450.6 49.9 all-gather.22
  691.4 20.4 all-gather.24
  892.5 47.7 all-gather.26
  958.9 45.0 all-gather.28
  1005.4 45.6 all-gather.30
  1074.8 56.9 all-gather.32
  1133.2 49.7 all-gather.34

commit v3 on v2

--- a/solution.py
+++ b/solution.py
@@ -1,4 +1,5 @@
 import functools
+import itertools
 import math
 
 import jax
@@ -267,8 +268,8 @@
     return jnp.concatenate([src[t] for t in range(src.shape[0])], axis=1).reshape(seqs, rows, chans).astype(BF16)
 
 
-def col_kernel(heads, parts, *refs):
-    m_refs = refs[:parts]
+def col_kernel(heads, parts, held, *refs):
+    m_refs, refs = refs[:parts], refs[held:]
     mask_ref, w_ref, w_out_ref, tin_ref, tout_ref, op_ref, out_ref, a_ref, b_ref, x_s, b_s, wt_s, opt_s, proj_s, keep_s, gated_s = refs[parts:]
     rows, seqs = mask_ref.shape
     chans = w_ref.shape[0]
@@ -305,21 +306,27 @@
     b_ref[...] = join_store(b_s, b_ref.shape)
 
 
-def column_block(m_parts, mask_t, heads, w, w_out, t_in, t_out, o_proj):
+def column_block(m_parts, mask_t, heads, w, w_out, t_in, t_out, o_proj, part, parts, before):
     rows, seqs = mask_t.shape
     pieces, size, _, chans = m_parts[0].shape
-    parts = len(m_parts)
     dim = o_proj.shape[1] // 2
-    block = 16
+    block = rows // parts
     weights = (w, w_out, t_in, t_out, o_proj)
     out_shape = (pieces, seqs // pieces, rows, chans)
-    return call(functools.partial(col_kernel, heads, parts), (rows // block,),
-                [lead_spec((pieces, size, block, chans), 2)] * parts + [lead_spec((block, seqs), 0)] + [full_spec(x) for x in weights],
-                [lead_spec(out_shape[:2] + (block, chans), 2), lead_spec((block, dim, seqs), 0), lead_spec((dim, block, seqs), 1)],
-                [jax.ShapeDtypeStruct(out_shape, BF16), jax.ShapeDtypeStruct((rows, dim, seqs), BF16), jax.ShapeDtypeStruct((dim, rows, seqs), BF16)],
-                [pltpu.VMEM((chans // 128, seqs * block, 128), F32), pltpu.VMEM((seqs // 128, dim * block, 128), F32),
-                 pltpu.VMEM(w.shape[::-1], BF16), pltpu.VMEM(o_proj.shape[::-1], BF16)] + attention_scratch(block, seqs, w, w_out),
-                3 * 10 ** 10)(*m_parts, mask_t, *weights)
+    held = 0 if before is None else 1
+    count = len(m_parts)
+    return pl.pallas_call(
+        functools.partial(col_kernel, heads, count, held), grid=(1,),
+        in_specs=[pl.BlockSpec((pieces, size, block, chans), lambda n: (0, 0, part, 0))] * count + [pl.BlockSpec(memory_space=pl.ANY)] * held
+        + [pl.BlockSpec((block, seqs), lambda n: (part, 0))] + [full_spec(x) for x in weights],
+        out_specs=[pl.BlockSpec(out_shape[:2] + (block, chans), lambda n: (0, 0, part, 0)), lead_spec((block, dim, seqs), 0), lead_spec((dim, block, seqs), 0)],
+        out_shape=[jax.ShapeDtypeStruct(out_shape, BF16), jax.ShapeDtypeStruct((block, dim, seqs), BF16), jax.ShapeDtypeStruct((dim, block, seqs), BF16)],
+        scratch_shapes=[pltpu.VMEM((chans // 128, seqs * block, 128), F32), pltpu.VMEM((seqs // 128, dim * block, 128), F32),
+                        pltpu.VMEM(w.shape[::-1], BF16), pltpu.VMEM(o_proj.shape[::-1], BF16)] + attention_scratch(block, seqs, w, w_out),
+        input_output_aliases={count: 0} if held else {},
+        compiler_params=pltpu.CompilerParams(vmem_limit_bytes=VMEM_LIMIT),
+        cost_estimate=pl.CostEstimate(flops=15 * 10 ** 9, bytes_accessed=1 << 24, transcendentals=0),
+    )(*m_parts, *([before] if held else []), mask_t, *weights)
 
 
 def gate_parts(z_norm, mask_row, wt_ref, tri):
@@ -334,8 +341,10 @@
         dst[t, pl.ds(n, value.shape[0], stride=step), :] = value[:, t * 128:(t + 1) * 128]
 
 
-def opm_kernel(a_ref, b_ref, z_ref, rmask_ref, fmask_ref, pmask_ref, w_ref, proj_ref,
-               z_out, l_out, r_out, wf_s, wt_s, gt_s, o_s, scale_s, l_s, r_s):
+def opm_kernel(parts, pieces, a_ref, *refs):
+    b_refs = refs[:parts]
+    (z_ref, rmask_ref, fmask_ref, pmask_ref, w_ref, proj_ref,
+     z_out, l_out, r_out, wf_s, wt_s, gt_s, o_s, scale_s, l_s, r_s) = refs[parts:]
     rows, dim, seqs = a_ref.shape
     tri = l_out.shape[0]
 
@@ -348,7 +357,7 @@
     scale_s[...] = 1.0 / (1e-3 + nt(rmask_ref[...].astype(BF16), fmask_ref[...].astype(BF16)))
 
     def outer(e, carry):
-        prod = nt(a_ref[...].reshape(rows * dim, seqs), b_ref[e]).astype(BF16)
+        prod = nt(a_ref[...].reshape(rows * dim, seqs), channel(b_refs, e, pieces)).astype(BF16)
         for i in range(rows):
             o_s[i, pl.ds(pl.multiple_of(e * dim, dim), dim), :] = prod[i * dim:(i + 1) * dim]
         return carry
@@ -370,21 +379,20 @@
     r_out[...] = join_store(r_s, r_out.shape)
 
 
-def outer_block(a, b_full, z, rmask, fmask, pmask, w_out, tri_proj, part, parts):
-    rows, dim, seqs = a.shape
+def outer_block(a, b_parts, z, rmask, fmask, pmask, w_out, tri_proj, pieces, part):
+    block, dim, seqs = a.shape
     length, out_dim = pmask.shape[1], z.shape[-1]
     tri = (tri_proj.shape[1] - out_dim) // 4
-    block = rows // parts
     consts = (w_out, tri_proj)
     outs = [jax.ShapeDtypeStruct((block, length, out_dim), BF16)] + [jax.ShapeDtypeStruct((tri, block, length), BF16)] * 2
     chan_scratch = pltpu.VMEM((length // 128, tri * block, 128), F32)
-    return call(opm_kernel, (1,),
-                [pl.BlockSpec((block, dim, seqs), lambda n: (part, 0, 0)), full_spec(b_full), row_spec_of(z, block, part),
+    return call(functools.partial(opm_kernel, len(b_parts), pieces), (1,),
+                [full_spec(a)] + [full_spec(x) for x in b_parts] + [row_spec_of(z, block, part),
                  pl.BlockSpec((block, seqs), lambda n: (part, 0)), full_spec(fmask), pl.BlockSpec((block, length), lambda n: (part, 0))]
                 + [full_spec(x) for x in consts], [full_spec(x) for x in outs], outs,
                 [pltpu.VMEM(w_out.shape, F32), pltpu.VMEM(w_out.shape[::-1], BF16), pltpu.VMEM(tri_proj.shape[::-1], BF16),
                  pltpu.VMEM((block, dim * dim, length), BF16), pltpu.VMEM((block, length), F32), chan_scratch, chan_scratch],
-                10 ** 10)(a, b_full, z, rmask, fmask, pmask, *consts)
+                10 ** 10)(a, *b_parts, z, rmask, fmask, pmask, *consts)
 
 
 def channel(b_refs, c, pieces):
@@ -616,6 +624,53 @@
     return jnp.swapaxes(x, 0, 1).reshape(rows, pieces * size, chans)
 
 
+def spread_kernel(count, x_ref, out_ref, own_sem, send_sem, recv_sem, mate_send, mate_recv):
+    me = lax.axis_index(GROUP_AXIS)
+    rows = x_ref.shape[1]
+    mate = me + 1 - 2 * lax.rem(me, 2)
+    hops = [2 * k for k in range(1, count // 2)]
+
+    barrier = pltpu.get_barrier_semaphore()
+    for other in [lax.rem(me + hop, count) for hop in hops] + [mate]:
+        pl.semaphore_signal(barrier, inc=1, device_id={GROUP_AXIS: other}, device_id_type=pl.DeviceIdType.MESH)
+    pl.semaphore_wait(barrier, len(hops) + 1)
+
+    def place(owner):
+        return out_ref.at[:, pl.ds(pl.multiple_of(owner * rows, rows), rows), :]
+
+    def send(src, owner, send_at, recv_at, target):
+        copy = pltpu.make_async_remote_copy(src_ref=src, dst_ref=place(owner), send_sem=send_at, recv_sem=recv_at,
+                                            device_id={GROUP_AXIS: target}, device_id_type=pl.DeviceIdType.MESH)
+        copy.start()
+        return copy
+
+    far = [send(x_ref, me, send_sem.at[k], recv_sem.at[k], lax.rem(me + hop, count)) for k, hop in enumerate(hops)]
+    near = [send(x_ref, me, mate_send.at[len(hops)], mate_recv.at[len(hops)], mate)]
+    own = pltpu.make_async_copy(x_ref, place(me), own_sem)
+    own.start()
+    for k, hop in enumerate(hops):
+        far[k].wait_recv()
+        owner = lax.rem(me + count - hop, count)
+        near.append(send(place(owner), owner, mate_send.at[k], mate_recv.at[k], mate))
+    own.wait()
+    for copy in far:
+        copy.wait_send()
+    for copy in near:
+        copy.wait()
+
+
+def spread_call(x, count, ident):
+    heads, rows, length = x.shape
+    hops = count // 2 - 1
+    return pl.pallas_call(
+        functools.partial(spread_kernel, count), out_shape=jax.ShapeDtypeStruct((heads, rows * count, length), x.dtype),
+        in_specs=[pl.BlockSpec(memory_space=pltpu.VMEM)], out_specs=pl.BlockSpec(memory_space=pltpu.VMEM),
+        scratch_shapes=[pltpu.SemaphoreType.DMA, pltpu.SemaphoreType.DMA((hops,)), pltpu.SemaphoreType.DMA((hops,)),
+                        pltpu.SemaphoreType.DMA((hops + 1,)), pltpu.SemaphoreType.DMA((hops + 1,))],
+        compiler_params=pltpu.CompilerParams(collective_id=ident, has_side_effects=True),
+        cost_estimate=pl.CostEstimate(flops=10 ** 8, bytes_accessed=1 << 21, transcendentals=0))(x)
+
+
 def bias_weight(w):
     return jnp.pad(w.T, ((0, 8 - w.shape[1]), (0, 0)))
 
@@ -626,6 +681,10 @@
     def local_body(m, z, msa_mask, pair_mask, *weights):
         layers = weights[0].shape[0]
         pieces, parts = mesh.shape[GROUP_AXIS], 2
+        idents = itertools.count()
+
+        def spread(x):
+            return spread_call(x, pieces, next(idents))
         res_loc = z.shape[0]
         shard = lax.axis_index(GROUP_AXIS)
         heads = weights[1].shape[2]
@@ -633,7 +692,7 @@
         row_bias_w = [bias_weight(weights[1][n]) for n in range(layers)]
         seq_mask, row_mask = msa_mask.astype(F32), pair_mask.astype(F32)
         bias = pair_bias(z, row_bias_w[0], heads)
-        packed = gather(jnp.concatenate([bias, msa_mask.astype(BF16)[None], pair_mask.astype(BF16)[None]]), 1)
+        packed = spread(jnp.concatenate([bias, msa_mask.astype(BF16)[None], pair_mask.astype(BF16)[None]]))
         bias = packed[:heads]
         masks_t = jnp.swapaxes(packed[heads:].astype(F32), 1, 2)
         full_mask_t = masks_t[0]
@@ -641,24 +700,30 @@
         for n in range(layers):
             (row_qkvg, _, row_out, col_qkvg, col_out, mtr_in, mtr_out, opm_proj, opm_out, tmo_proj, tmo_out, tmi_proj, tmi_out,
              tas_qkvg, tas_bias, tas_out, tae_qkvg, tae_bias, tae_out, ptr_in, ptr_out) = (weight[n] for weight in weights)
-            m = [exchange(row_attention(m, seq_mask, bias, n == 0, row_qkvg, row_out, pieces, p, parts)) for p in range(parts)]
-            m, left, right = column_block(m, res_mask_t, heads, col_qkvg, col_out, mtr_in, mtr_out, opm_proj)
-            right = gather(right, 1)
-            done = [outer_block(left, right, z, res_mask_t, full_mask_t, row_mask, opm_out, tmo_proj, p, parts) for p in range(parts)]
+            rows = [row_attention(m, seq_mask, bias, n == 0, row_qkvg, row_out, pieces, p, parts) for p in range(parts)]
+            if n > 0:
+                rows[0], z = lax.optimization_barrier((rows[0], z))
+            rows = [exchange(x) for x in rows]
+            m, left, right = None, [], []
+            for p in range(parts):
+                m, a_part, b_part = column_block(rows, res_mask_t, heads, col_qkvg, col_out, mtr_in, mtr_out, opm_proj, p, parts, m)
+                left.append(a_part)
+                right.append(gather(b_part, 1))
+            done = [outer_block(left[p], right, z, res_mask_t, full_mask_t, row_mask, opm_out, tmo_proj, pieces, p) for p in range(parts)]
             full = [gather(x[2], 1) for x in done]
             done = [outgoing(x[1], full, x[0], row_mask, tmo_proj, tmo_out, tmi_proj, pieces, p) for p, x in enumerate(done)]
             left, full = [exchange(x[1]) for x in done], [gather(x[2], 1) for x in done]
             z, bias = incoming(left, full, [x[0] for x in done], tmi_proj, tmi_out, bias_weight(tas_bias), pair_heads)
-            bias = gather(bias, 1)
+            bias = spread(bias)
             done = [start_attention(z, row_mask, bias, tas_qkvg, tas_out, bias_weight(tae_bias), pieces, p, parts) for p in range(parts)]
             z = [exchange(x[0]) for x in done]
-            bias = gather(jnp.concatenate([x[1] for x in done], axis=1), 1)
+            bias = spread(jnp.concatenate([x[1] for x in done], axis=1))
             z, bias, m = lax.optimization_barrier((z, bias, m))
             m = exchange(m)
             z, bias = end_attention(z, col_mask, bias, tae_qkvg, tae_out, ptr_in, ptr_out, row_bias_w[min(n + 1, layers - 1)], heads)
             z, bias, m = lax.optimization_barrier((z, bias, m))
             if n < layers - 1:
-                bias = gather(bias, 1)
+                bias, z = lax.optimization_barrier((spread(bias), z))
             z = exchange(z)
         return rejoin(m), rejoin(z)
 

time: 1420 us -> 1350 us (0.951)
  blocking collectives: 218 us -> 61.4 us
  Pallas kernels: 705 us -> 803 us
  waiting for transfers between devices: 381 us -> 356 us
    all_gather x4 -> x0, blocking collectives: 109 us -> none  [gather(): return lax.all_gather(x, GROUP_AXIS, axis=axis, tiled=True)]
    pallas_call x6 -> x14, Pallas kernels: 239 us -> 337 us  [the longest x4 173 us: column_block(): pl.pallas_call(functools.partial(col_kernel, heads, count, held), grid=(1...]
    all_to_all x3 -> x2, blocking collectives: 109 us -> 61.4 us  [exchange(): return lax.all_to_all(x, GROUP_AXIS, 0, 0, tiled=True)]
    all_gather x12, waiting for transfers between devices: 273 us -> 247 us  [gather(): return lax.all_gather(x, GROUP_AXIS, axis=axis, tiled=True)]
    all_to_all x13 -> x14, starting transfers between devices: 54.2 us -> 60.1 us  [exchange(): return lax.all_to_all(x, GROUP_AXIS, 0, 0, tiled=True)]
    all_to_all x13 -> x14, waiting for transfers between devices: 107 us -> 108 us  [exchange(): return lax.all_to_all(x, GROUP_AXIS, 0, 0, tiled=True)]
  transfers between devices with their start and end apart: 25 -> 26, of which waited for: 16 -> 14; matrix products, arithmetic and copies ran while one was open for 2% -> 2% of each run, Pallas kernels for 20% -> 32%
where the time goes in v3:
time: 1350 us; the launch traced here: 1340 us
  Pallas kernels  803 us (59%)
  waiting for transfers between devices  356 us (26%)
  blocking collectives  61.4 us (5%)
  starting transfers between devices  61.3 us (5%)
  local copies, waits for them, and re-layouts  34.6 us (3%)
  between operations  15.2 us (1%)
    all_gather x12, waiting for transfers between devices, gather(): return lax.all_gather(x, GROUP_AXIS, axis=axis, tiled=True)  247 us
    pallas_call x4, Pallas kernels, column_block(): pl.pallas_call(functools.partial(col_kernel, heads, count, held), grid=(1...  173 us
    pallas_call x4, Pallas kernels, row_attention(): call(functools.partial(row_kernel, transposed, heads), (steps,), [row_spe...  122 us
    all_to_all x14, waiting for transfers between devices, exchange(): return lax.all_to_all(x, GROUP_AXIS, 0, 0, tiled=True)  108 us
    pallas_call x2, Pallas kernels, end_attention(): call(functools.partial(end_kernel, heads, parts), (cols // block,), [lead...  96.7 us
    pallas_call x4, Pallas kernels, outgoing(): call(functools.partial(outgoing_kernel, parts, pieces), (tri // block,),...  93.5 us
    pallas_call x6, Pallas kernels, spread_call(): pl.pallas_call(functools.partial(spread_kernel, count), out_shape=jax.Sha...  90.4 us
    pallas_call x4, Pallas kernels, outer_block(): call(functools.partial(opm_kernel, len(b_parts), pieces), (1,), [full_spe...  73.6 us
  transfers between devices with their start and end apart: 26, of which 14 were waited for; matrix products, arithmetic and copies ran while one was open for 2% of the time, Pallas kernels for 32%

profile of v3, /device:TPU:112, one launch (start us, length us, event | category | flops | bytes accessed | tf_op | source)
XLA Modules:
  0.0 1335.8 jit_solution(986391406590294537)
XLA Ops:
  9.9 12.4 shard_map.248
  24.0 16.4 %shard_map.249 = bf16[10,256,256]{2,1,0:T(8,128)(2,1)} custom-call(bf16[10,32,256]{2,1,0:T(8,128)(2,1)} %pad_maximum_fusion.x_ref), custom_call_target="tpu_custom_call" | custom-call | flops 100000000 | bytes 2097152 | tf_op jit(solution)/shard_map/pallas_call | solution.py:665
  44.6 30.8 %shard_map.250 = bf16[8,16,32,256]{3,2,1,0:T(8,128)(2,1)} custom-call(bf16[32,256,256]{2,1,0:T(8,128)(2,1)} %m_ref.3, f32[32,256]{1,0:T(8,128)} %get-tuple-element.180.mask_ref, bf16[8,256,256]{2,1,0:T(8,128)(2,1)} %slice.134.bias_ref, bf16[256,1024]{1,0:T(8,128)(2,1)} %get-tuple-element.145.w_ref, bf16[256,256]{1,0:T(8,128)(2,1)} %get-tuple-element.166.w_out_ref), custom_call_target="tpu_custom_call" | custom-call | flops 10000000000 | bytes 16777216 | tf_op jit(solution)/shard_map/pallas_call | solution.py:239
  79.2 30.8 %shard_map.251 = bf16[8,16,32,256]{3,2,1,0:T(8,128)(2,1)} custom-call(bf16[32,256,256]{2,1,0:T(8,128)(2,1)} %m_ref.3, f32[32,256]{1,0:T(8,128)} %get-tuple-element.180.mask_ref, bf16[8,256,256]{2,1,0:T(8,128)(2,1)} %slice.134.bias_ref, bf16[256,1024]{1,0:T(8,128)(2,1)} %get-tuple-element.145.w_ref, bf16[256,256]{1,0:T(8,128)(2,1)} %get-tuple-element.166.w_out_ref), custom_call_target="tpu_custom_call" | custom-call | flops 10000000000 | bytes 16777216 | tf_op jit(solution)/shard_map/pallas_call | solution.py:239
  121.6 21.6 %all-to-all-done.1.refs_1_ = bf16[8,16,32,256]{3,2,1,0:T(8,128)(2,1)} async-done(((bf16[8,16,32,256]{3,2,1,0:T(8,128)(2,1)}), bf16[8,16,32,256]{3,2,1,0:T(8,128)(2,1)}, u32[]{:S(2)}, u32[]{:S(2)}) %all-to-all-start.1) | async-done | bytes 2097184 | tf_op jit(solution)/shard_map/all_to_all | solution.py:619
  143.1 43.3 %shard_map.252 = (bf16[8,32,32,256]{3,2,1,0:T(8,128)(2,1)}, bf16[16,32,256]{2,1,0:T(8,128)(2,1)}, bf16[32,16,256]{2,1,0:T(8,128)(2,1)}) custom-call(bf16[8,16,32,256]{3,2,1,0:T(8,128)(2,1)} %copy-done.1, bf16[8,16,32,256]{3,2,1,0:T(8,128)(2,1)} %all-to-all-done.1.refs_1_, f32[32,256]{1,0:T(8,128)} %dynamic-slice_bitcast_fusion.1.refs_2_.refs_3_, ...), custom_call_target="tpu_custom_call" | custom-call | flops 15000000512 | bytes 16777216 | tf_op jit(solution)/shard_map/pallas_call | solution.py:318
  186.8 43.3 %shard_map.253 = (bf16[8,32,32,256]{3,2,1,0:T(8,128)(2,1)}, bf16[16,32,256]{2,1,0:T(8,128)(2,1)}, bf16[32,16,256]{2,1,0:T(8,128)(2,1)}) custom-call(bf16[8,16,32,256]{3,2,1,0:T(8,128)(2,1)} %copy-done.1, bf16[8,16,32,256]{3,2,1,0:T(8,128)(2,1)} %all-to-all-done.1.refs_1_, ...), custom_call_target="tpu_custom_call", output_to_operand_aliasing={{0}: (2, {})} | custom-call | flops 15000000512 | bytes 16777216 | tf_op jit(solution)/shard_map/pallas_call | solution.py:318
  231.9 19.4 %all-gather.15.cloned.1.call-done.refs_1_ = bf16[32,128,256]{2,1,0:T(8,128)(2,1)} async-done(((bf16[32,16,256]{2,1,0:T(8,128)(2,1)}), bf16[32,128,256]{2,1,0:T(8,128)(2,1)}) %all-gather.15.cloned.1.call-update) | async-done | bytes 2097168 | tf_op jit(solution)/shard_map/all_gather | solution.py:615
  251.3 18.4 %shard_map.254 = (bf16[16,256,128]{2,1,0:T(8,128)(2,1)}, bf16[128,16,256]{2,1,0:T(8,128)(2,1)}, bf16[128,16,256]{2,1,0:T(8,128)(2,1)}) custom-call(bf16[16,32,256]{2,1,0:T(8,128)(2,1)} %get-tuple-element.70.a_ref, bf16[32,128,256]{2,1,0:T(8,128)(2,1)} %all-gather.13.cloned.1.call-done.refs_0_, bf16[32,128,256]{2,1,0:T(8,128)(2,1)} %all-gather.15.cloned.1.call-done.refs_1_, ...), custom_call_target="tpu_custom_call" | custom-call | flops 10000000000 | bytes 16777216 | tf_op jit(solution)/shard_map/pallas_call | solution.py:389
  269.8 18.4 %shard_map.255 = (bf16[16,256,128]{2,1,0:T(8,128)(2,1)}, bf16[128,16,256]{2,1,0:T(8,128)(2,1)}, bf16[128,16,256]{2,1,0:T(8,128)(2,1)}) custom-call(bf16[16,32,256]{2,1,0:T(8,128)(2,1)} %get-tuple-element.76.a_ref, bf16[32,128,256]{2,1,0:T(8,128)(2,1)} %all-gather.13.cloned.1.call-done.refs_0_, bf16[32,128,256]{2,1,0:T(8,128)(2,1)} %all-gather.15.cloned.1.call-done.refs_1_, ...), custom_call_target="tpu_custom_call" | custom-call | flops 10000000000 | bytes 16777216 | tf_op jit(solution)/shard_map/pallas_call | solution.py:389
  289.8 26.0 %all-gather.17.cloned.1.call-done.refs_0_ = bf16[128,128,256]{2,1,0:T(8,128)(2,1)} async-done(((bf16[128,16,256]{2,1,0:T(8,128)(2,1)}), bf16[128,128,256]{2,1,0:T(8,128)(2,1)}) %all-gather.17.cloned.1.call-update) | async-done | bytes 8388624 | tf_op jit(solution)/shard_map/all_gather | solution.py:615
  315.9 47.1 %all-gather.19.cloned.1.call-done.refs_1_ = bf16[128,128,256]{2,1,0:T(8,128)(2,1)} async-done(((bf16[128,16,256]{2,1,0:T(8,128)(2,1)}), bf16[128,128,256]{2,1,0:T(8,128)(2,1)}) %all-gather.19.cloned.1.call-update) | async-done | bytes 8388624 | tf_op jit(solution)/shard_map/all_gather | solution.py:615
  363.0 23.4 %shard_map.256 = (bf16[16,256,128]{2,1,0:T(8,128)(2,1)}, bf16[8,16,32,128]{3,2,1,0:T(8,128)(2,1)}, bf16[128,16,256]{2,1,0:T(8,128)(2,1)}) custom-call(bf16[128,16,256]{2,1,0:T(8,128)(2,1)} %get-tuple-element.74.a_ref, bf16[128,128,256]{2,1,0:T(8,128)(2,1)} %all-gather.17.cloned.1.call-done.refs_0_, ...), custom_call_target="tpu_custom_call" | custom-call | flops 10000000000 | bytes 16777216 | tf_op jit(solution)/shard_map/pallas_call | solution.py:468
  386.5 23.4 %shard_map.257 = (bf16[16,256,128]{2,1,0:T(8,128)(2,1)}, bf16[8,16,32,128]{3,2,1,0:T(8,128)(2,1)}, bf16[128,16,256]{2,1,0:T(8,128)(2,1)}) custom-call(bf16[128,16,256]{2,1,0:T(8,128)(2,1)} %get-tuple-element.80.a_ref, bf16[128,128,256]{2,1,0:T(8,128)(2,1)} %all-gather.17.cloned.1.call-done.refs_0_, ...), custom_call_target="tpu_custom_call" | custom-call | flops 10000000000 | bytes 16777216 | tf_op jit(solution)/shard_map/pallas_call | solution.py:468
  410.0 30.8 %all_to_all.80.refs_0_ = bf16[8,16,32,128]{3,2,1,0:T(8,128)(2,1)} all-to-all(bf16[8,16,32,128]{3,2,1,0:T(8,128)(2,1)S(1)} %copy-done.10), channel_id=1, replica_groups=mesh['req'=2,'dap'=8] {'dap'}, dimensions={0} | all-to-all | bytes 2097152 | tf_op jit(solution)/shard_map/all_to_all | solution.py:619
  448.1 17.7 %all-to-all-done.3.refs_1_ = bf16[8,16,32,128]{3,2,1,0:T(8,128)(2,1)S(1)} async-done(((bf16[8,16,32,128]{3,2,1,0:T(8,128)(2,1)}), bf16[8,16,32,128]{3,2,1,0:T(8,128)(2,1)S(1)}, u32[]{:S(2)}, u32[]{:S(2)}) %all-to-all-start.3) | async-done | bytes 1048608 | tf_op jit(solution)/shard_map/all_to_all | solution.py:619
  465.8 29.6 %all-gather.23.cloned.1.call-done.refs_3_ = bf16[128,128,256]{2,1,0:T(8,128)(2,1)} async-done(((bf16[128,16,256]{2,1,0:T(8,128)(2,1)}), bf16[128,128,256]{2,1,0:T(8,128)(2,1)}) %all-gather.23.cloned.1.call-update) | async-done | bytes 8388624 | tf_op jit(solution)/shard_map/all_gather | solution.py:615
  495.5 34.8 %shard_map.258 = (bf16[32,256,128]{2,1,0:T(8,128)(2,1)}, bf16[4,32,256]{2,1,0:T(8,128)(2,1)}) custom-call(bf16[8,16,32,128]{3,2,1,0:T(8,128)(2,1)} %all_to_all.80.refs_0_, bf16[8,16,32,128]{3,2,1,0:T(8,128)(2,1)} %copy-done.7, bf16[128,128,256]{2,1,0:T(8,128)(2,1)} %all-gather.21.cloned.1.call-done.refs_2_, ...), custom_call_target="tpu_custom_call" | custom-call | flops 10000000000 | bytes 16777216 | tf_op jit(solution)/shard_map/pallas_call | solution.py:521
  530.3 9.9 shard_map.259.bias_ref
  540.2 17.7 %shard_map.260 = (bf16[8,16,32,128]{3,2,1,0:T(8,128)(2,1)}, bf16[4,16,256]{2,1,0:T(8,128)(2,1)}) custom-call(bf16[32,256,128]{2,1,0:T(8,128)(2,1)} %get-tuple-element.87.z_ref, f32[32,256]{1,0:T(8,128)} %get-tuple-element.188.refs_5_.refs_3_.mask_ref, bf16[4,256,256]{2,1,0:T(8,128)(2,1)} %shard_map.259.bias_ref, bf16[128,512]{1,0:T(8,128)(2,1)} %get-tuple-element.162.w_ref, ...), custom_call_target="tpu_custom_call" | custom-call | flops 10000000000 | bytes 16777216 | tf_op jit(solution)/shard_map/pallas_call | solution.py:558
  561.7 17.8 %shard_map.261 = (bf16[8,16,32,128]{3,2,1,0:T(8,128)(2,1)}, bf16[4,16,256]{2,1,0:T(8,128)(2,1)}) custom-call(bf16[32,256,128]{2,1,0:T(8,128)(2,1)} %get-tuple-element.87.z_ref, f32[32,256]{1,0:T(8,128)} %get-tuple-element.188.refs_5_.refs_3_.mask_ref, bf16[4,256,256]{2,1,0:T(8,128)(2,1)} %shard_map.259.bias_ref, bf16[128,512]{1,0:T(8,128)(2,1)} %get-tuple-element.162.w_ref, ...), custom_call_target="tpu_custom_call" | custom-call | flops 10000000000 | bytes 16777216 | tf_op jit(solution)/shard_map/pallas_call | solution.py:558
  584.8 19.9 %shard_map.262.refs_3_ = bf16[4,256,256]{2,1,0:T(8,128)(2,1)} custom-call(bf16[4,32,256]{2,1,0:T(8,128)(2,1)} %pad_maximum_fusion.1.x_ref), custom_call_target="tpu_custom_call" | custom-call | flops 100000000 | bytes 2097152 | tf_op jit(solution)/shard_map/pallas_call | solution.py:665
  613.4 48.4 %shard_map.263 = (bf16[8,32,32,128]{3,2,1,0:T(8,128)(2,1)}, bf16[8,32,256]{2,1,0:T(8,128)(2,1)}) custom-call(bf16[8,16,32,128]{3,2,1,0:T(8,128)(2,1)} %copy-done.5, bf16[8,16,32,128]{3,2,1,0:T(8,128)(2,1)} %copy-done.8, f32[32,256]{1,0:T(8,128)} %dynamic-slice_bitcast_fusion.refs_2_, bf16[4,256,256]{2,1,0:T(8,128)(2,1)} %shard_map.262.refs_3_, ...), custom_call_target="tpu_custom_call" | custom-call | flops 10000000000 | bytes 16777216 | tf_op jit(solution)/shard_map/pallas_call | solution.py:605
  661.7 14.2 %shard_map.264.bias_ref = bf16[8,256,256]{2,1,0:T(8,128)(2,1)} custom-call(bf16[8,32,256]{2,1,0:T(8,128)(2,1)} %get-tuple-element.101.x_ref), custom_call_target="tpu_custom_call" | custom-call | flops 100000000 | bytes 2097152 | tf_op jit(solution)/shard_map/pallas_call | solution.py:665
  680.0 30.3 %shard_map.266 = bf16[8,16,32,256]{3,2,1,0:T(8,128)(2,1)} custom-call(bf16[8,32,32,256]{3,2,1,0:T(8,128)(2,1)} %all-to-all-done.6.m_ref, f32[32,256]{1,0:T(8,128)} %get-tuple-element.180.mask_ref, bf16[8,256,256]{2,1,0:T(8,128)(2,1)} %shard_map.264.bias_ref, bf16[256,1024]{1,0:T(8,128)(2,1)} %get-tuple-element.144.w_ref, ...), custom_call_target="tpu_custom_call" | custom-call | flops 10000000000 | bytes 16777216 | tf_op jit(solution)/shard_map/pallas_call | solution.py:239
  716.4 30.3 %shard_map.265 = bf16[8,16,32,256]{3,2,1,0:T(8,128)(2,1)} custom-call(bf16[8,32,32,256]{3,2,1,0:T(8,128)(2,1)} %all-to-all-done.6.m_ref, f32[32,256]{1,0:T(8,128)} %get-tuple-element.180.mask_ref, bf16[8,256,256]{2,1,0:T(8,128)(2,1)} %shard_map.264.bias_ref, bf16[256,1024]{1,0:T(8,128)(2,1)} %get-tuple-element.144.w_ref, ...), custom_call_target="tpu_custom_call" | custom-call | flops 10000000000 | bytes 16777216 | tf_op jit(solution)/shard_map/pallas_call | solution.py:239
  746.8 4.8 all-to-all-start.8
  752.4 26.4 %all-to-all-done.8.refs_0_ = bf16[8,16,32,256]{3,2,1,0:T(8,128)(2,1)S(1)} async-done(((bf16[8,16,32,256]{3,2,1,0:T(8,128)(2,1)}), bf16[8,16,32,256]{3,2,1,0:T(8,128)(2,1)S(1)}, u32[]{:S(2)}, u32[]{:S(2)}) %all-to-all-start.8) | async-done | bytes 2097184 | tf_op jit(solution)/shard_map/all_to_all | solution.py:619
  780.1 43.2 %shard_map.267 = (bf16[8,32,32,256]{3,2,1,0:T(8,128)(2,1)}, bf16[16,32,256]{2,1,0:T(8,128)(2,1)}, bf16[32,16,256]{2,1,0:T(8,128)(2,1)}) custom-call(bf16[8,16,32,256]{3,2,1,0:T(8,128)(2,1)} %copy-done.2, bf16[8,16,32,256]{3,2,1,0:T(8,128)(2,1)} %all-to-all-done.9.refs_1_, f32[32,256]{1,0:T(8,128)} %dynamic-slice_bitcast_fusion.1.refs_2_.refs_3_, ...), custom_call_target="tpu_custom_call" | custom-call | flops 15000000512 | bytes 16777216 | tf_op jit(solution)/shard_map/pallas_call | solution.py:318
  823.6 43.2 %shard_map.268 = (bf16[8,32,32,256]{3,2,1,0:T(8,128)(2,1)}, bf16[16,32,256]{2,1,0:T(8,128)(2,1)}, bf16[32,16,256]{2,1,0:T(8,128)(2,1)}) custom-call(bf16[8,16,32,256]{3,2,1,0:T(8,128)(2,1)} %copy-done.2, bf16[8,16,32,256]{3,2,1,0:T(8,128)(2,1)} %all-to-all-done.9.refs_1_, ...), custom_call_target="tpu_custom_call", output_to_operand_aliasing={{0}: (2, {})} | custom-call | flops 15000000512 | bytes 16777216 | tf_op jit(solution)/shard_map/pallas_call | solution.py:318
  867.0 20.4 %all-gather.27.cloned.1.call-done.refs_1_ = bf16[32,128,256]{2,1,0:T(8,128)(2,1)} async-done(((bf16[32,16,256]{2,1,0:T(8,128)(2,1)}), bf16[32,128,256]{2,1,0:T(8,128)(2,1)}) %all-gather.27.cloned.1.call-update) | async-done | bytes 2097168 | tf_op jit(solution)/shard_map/all_gather | solution.py:615
  887.5 18.4 %shard_map.269 = (bf16[16,256,128]{2,1,0:T(8,128)(2,1)}, bf16[128,16,256]{2,1,0:T(8,128)(2,1)}, bf16[128,16,256]{2,1,0:T(8,128)(2,1)}) custom-call(bf16[16,32,256]{2,1,0:T(8,128)(2,1)} %get-tuple-element.106.a_ref, bf16[32,128,256]{2,1,0:T(8,128)(2,1)} %all-gather.25.cloned.1.call-done.refs_0_, bf16[32,128,256]{2,1,0:T(8,128)(2,1)} %all-gather.27.cloned.1.call-done.refs_1_, ...), custom_call_target="tpu_custom_call" | custom-call | flops 10000000000 | bytes 16777216 | tf_op jit(solution)/shard_map/pallas_call | solution.py:389
  906.0 18.4 %shard_map.270 = (bf16[16,256,128]{2,1,0:T(8,128)(2,1)}, bf16[128,16,256]{2,1,0:T(8,128)(2,1)}, bf16[128,16,256]{2,1,0:T(8,128)(2,1)}) custom-call(bf16[16,32,256]{2,1,0:T(8,128)(2,1)} %get-tuple-element.113.a_ref, bf16[32,128,256]{2,1,0:T(8,128)(2,1)} %all-gather.25.cloned.1.call-done.refs_0_, bf16[32,128,256]{2,1,0:T(8,128)(2,1)} %all-gather.27.cloned.1.call-done.refs_1_, ...), custom_call_target="tpu_custom_call" | custom-call | flops 10000000000 | bytes 16777216 | tf_op jit(solution)/shard_map/pallas_call | solution.py:389
  924.5 27.6 %all-gather.29.cloned.1.call-done.refs_0_ = bf16[128,128,256]{2,1,0:T(8,128)(2,1)} async-done(((bf16[128,16,256]{2,1,0:T(8,128)(2,1)}), bf16[128,128,256]{2,1,0:T(8,128)(2,1)}) %all-gather.29.cloned.1.call-update) | async-done | bytes 8388624 | tf_op jit(solution)/shard_map/all_gather | solution.py:615
  952.1 47.1 %all-gather.31.cloned.1.call-done.refs_1_ = bf16[128,128,256]{2,1,0:T(8,128)(2,1)} async-done(((bf16[128,16,256]{2,1,0:T(8,128)(2,1)}), bf16[128,128,256]{2,1,0:T(8,128)(2,1)}) %all-gather.31.cloned.1.call-update) | async-done | bytes 8388624 | tf_op jit(solution)/shard_map/all_gather | solution.py:615
  999.2 23.3 %shard_map.271 = (bf16[16,256,128]{2,1,0:T(8,128)(2,1)}, bf16[8,16,32,128]{3,2,1,0:T(8,128)(2,1)}, bf16[128,16,256]{2,1,0:T(8,128)(2,1)}) custom-call(bf16[128,16,256]{2,1,0:T(8,128)(2,1)} %get-tuple-element.111.a_ref, bf16[128,128,256]{2,1,0:T(8,128)(2,1)} %all-gather.29.cloned.1.call-done.refs_0_, ...), custom_call_target="tpu_custom_call" | custom-call | flops 10000000000 | bytes 16777216 | tf_op jit(solution)/shard_map/pallas_call | solution.py:468
  1022.7 23.4 %shard_map.272 = (bf16[16,256,128]{2,1,0:T(8,128)(2,1)}, bf16[8,16,32,128]{3,2,1,0:T(8,128)(2,1)}, bf16[128,16,256]{2,1,0:T(8,128)(2,1)}) custom-call(bf16[128,16,256]{2,1,0:T(8,128)(2,1)} %get-tuple-element.117.a_ref, bf16[128,128,256]{2,1,0:T(8,128)(2,1)} %all-gather.29.cloned.1.call-done.refs_0_, ...), custom_call_target="tpu_custom_call" | custom-call | flops 10000000000 | bytes 16777216 | tf_op jit(solution)/shard_map/pallas_call | solution.py:468
  1046.2 30.6 %all_to_all.81.refs_0_ = bf16[8,16,32,128]{3,2,1,0:T(8,128)(2,1)} all-to-all(bf16[8,16,32,128]{3,2,1,0:T(8,128)(2,1)S(1)} %copy-done.11), channel_id=1, replica_groups=mesh['req'=2,'dap'=8] {'dap'}, dimensions={0} | all-to-all | bytes 2097152 | tf_op jit(solution)/shard_map/all_to_all | solution.py:619
  1082.0 19.5 %all-to-all-done.11.refs_1_ = bf16[8,16,32,128]{3,2,1,0:T(8,128)(2,1)S(1)} async-done(((bf16[8,16,32,128]{3,2,1,0:T(8,128)(2,1)}), bf16[8,16,32,128]{3,2,1,0:T(8,128)(2,1)S(1)}, u32[]{:S(2)}, u32[]{:S(2)}) %all-to-all-start.11) | async-done | bytes 1048608 | tf_op jit(solution)/shard_map/all_to_all | solution.py:619
  1101.5 29.8 %all-gather.35.cloned.1.call-done.refs_3_ = bf16[128,128,256]{2,1,0:T(8,128)(2,1)} async-done(((bf16[128,16,256]{2,1,0:T(8,128)(2,1)}), bf16[128,128,256]{2,1,0:T(8,128)(2,1)}) %all-gather.35.cloned.1.call-update) | async-done | bytes 8388624 | tf_op jit(solution)/shard_map/all_gather | solution.py:615
  1131.3 34.9 %shard_map.273 = (bf16[32,256,128]{2,1,0:T(8,128)(2,1)}, bf16[4,32,256]{2,1,0:T(8,128)(2,1)}) custom-call(bf16[8,16,32,128]{3,2,1,0:T(8,128)(2,1)} %all_to_all.81.refs_0_, bf16[8,16,32,128]{3,2,1,0:T(8,128)(2,1)} %copy-done.9, bf16[128,128,256]{2,1,0:T(8,128)(2,1)} %all-gather.33.cloned.1.call-done.refs_2_, ...), custom_call_target="tpu_custom_call" | custom-call | flops 10000000000 | bytes 16777216 | tf_op jit(solution)/shard_map/pallas_call | solution.py:521
  1166.2 9.9 shard_map.274.bias_ref
  1176.1 17.7 %shard_map.275 = (bf16[8,16,32,128]{3,2,1,0:T(8,128)(2,1)}, bf16[4,16,256]{2,1,0:T(8,128)(2,1)}) custom-call(bf16[32,256,128]{2,1,0:T(8,128)(2,1)} %get-tuple-element.124.z_ref, f32[32,256]{1,0:T(8,128)} %get-tuple-element.188.refs_5_.refs_3_.mask_ref, bf16[4,256,256]{2,1,0:T(8,128)(2,1)} %shard_map.274.bias_ref, bf16[128,512]{1,0:T(8,128)(2,1)} %get-tuple-element.161.w_ref, ...), custom_call_target="tpu_custom_call" | custom-call | flops 10000000000 | bytes 16777216 | tf_op jit(solution)/shard_map/pallas_call | solution.py:558
  1197.6 17.7 %shard_map.276 = (bf16[8,16,32,128]{3,2,1,0:T(8,128)(2,1)}, bf16[4,16,256]{2,1,0:T(8,128)(2,1)}) custom-call(bf16[32,256,128]{2,1,0:T(8,128)(2,1)} %get-tuple-element.124.z_ref, f32[32,256]{1,0:T(8,128)} %get-tuple-element.188.refs_5_.refs_3_.mask_ref, bf16[4,256,256]{2,1,0:T(8,128)(2,1)} %shard_map.274.bias_ref, bf16[128,512]{1,0:T(8,128)(2,1)} %get-tuple-element.161.w_ref, ...), custom_call_target="tpu_custom_call" | custom-call | flops 10000000000 | bytes 16777216 | tf_op jit(solution)/shard_map/pallas_call | solution.py:558
  1220.6 19.9 %shard_map.277.refs_3_ = bf16[4,256,256]{2,1,0:T(8,128)(2,1)} custom-call(bf16[4,32,256]{2,1,0:T(8,128)(2,1)} %pad_maximum_fusion.2.x_ref), custom_call_target="tpu_custom_call" | custom-call | flops 100000000 | bytes 2097152 | tf_op jit(solution)/shard_map/pallas_call | solution.py:665
  1246.3 48.4 %shard_map.278 = (bf16[8,32,32,128]{3,2,1,0:T(8,128)(2,1)}, bf16[8,32,256]{2,1,0:T(8,128)(2,1)}) custom-call(bf16[8,16,32,128]{3,2,1,0:T(8,128)(2,1)} %copy-done.6, bf16[8,16,32,128]{3,2,1,0:T(8,128)(2,1)} %copy-done.12, f32[32,256]{1,0:T(8,128)} %dynamic-slice_bitcast_fusion.refs_2_, bf16[4,256,256]{2,1,0:T(8,128)(2,1)} %shard_map.277.refs_3_, ...), custom_call_target="tpu_custom_call" | custom-call | flops 10000000000 | bytes 16777216 | tf_op jit(solution)/shard_map/pallas_call | solution.py:605
  1299.6 4.8 copy.35
  1304.4 22.1 %all-to-all-done.15 = bf16[8,32,32,128]{3,2,1,0:T(8,128)(2,1)S(1)} async-done(((bf16[8,32,32,128]{3,2,1,0:T(8,128)(2,1)}), bf16[8,32,32,128]{3,2,1,0:T(8,128)(2,1)S(1)}, u32[]{:S(2)}, u32[]{:S(2)}) %all-to-all-start.15) | async-done | bytes 2097184 | tf_op jit(solution)/shard_map/all_to_all | solution.py:619
  (158 shorter events, 92.5 us)
Async XLA Ops:
  22.4 20.5 %copy-start.3 = (bf16[2,256,1024]{2,1,0:T(8,128)(2,1)S(1)}, bf16[2,256,1024]{2,1,0:T(8,128)(2,1)}, u32[]{:S(2)}) copy-start(bf16[2,256,1024]{2,1,0:T(8,128)(2,1)} %param.29) | copy-start | bytes 3145732
  75.4 34.7 %all-to-all-start = ((bf16[8,16,32,256]{3,2,1,0:T(8,128)(2,1)}), bf16[8,16,32,256]{3,2,1,0:T(8,128)(2,1)S(1)}, u32[]{:S(2)}, u32[]{:S(2)}) async-start(bf16[8,16,32,256]{3,2,1,0:T(8,128)(2,1)} %shard_map.250), calls=%async_computation | async-start | bytes 4194304 | tf_op jit(solution)/shard_map/all_to_all | solution.py:619
  110.1 6.0 slice-start
  110.1 6.1 copy-start.24
  111.4 31.7 %all-to-all-start.1 = ((bf16[8,16,32,256]{3,2,1,0:T(8,128)(2,1)}), bf16[8,16,32,256]{3,2,1,0:T(8,128)(2,1)}, u32[]{:S(2)}, u32[]{:S(2)}) async-start(bf16[8,16,32,256]{3,2,1,0:T(8,128)(2,1)} %shard_map.251), calls=%async_computation.1 | async-start | bytes 4194304 | tf_op jit(solution)/shard_map/all_to_all | solution.py:619
  116.0 115.9 %all-gather.13.cloned.1.call-start = ((), (), s32[]{:S(2)}) async-start(), calls=%async_computation.16 | async-start | bytes 2359296 | tf_op jit(solution)/shard_map/all_gather | solution.py:615
  186.5 64.8 %all-gather.15.cloned.1.call-start = ((), (), s32[]{:S(2)}) async-start(), calls=%async_computation.17 | async-start | bytes 2359296 | tf_op jit(solution)/shard_map/all_gather | solution.py:615
  186.7 43.5 %copy-start.16 = (bf16[2,128,640]{2,1,0:T(8,128)(2,1)S(1)}, bf16[2,128,640]{2,1,0:T(8,128)(2,1)}, u32[]{:S(2)}) copy-start(bf16[2,128,640]{2,1,0:T(8,128)(2,1)} %param.38) | copy-start | bytes 983044
  186.8 44.2 %copy-start.15 = (bf16[2,1024,128]{2,1,0:T(8,128)(2,1)S(1)}, bf16[2,1024,128]{2,1,0:T(8,128)(2,1)}, u32[]{:S(2)}) copy-start(bf16[2,1024,128]{2,1,0:T(8,128)(2,1)} %param.37) | copy-start | bytes 1572868
  230.1 85.7 %all-gather.17.cloned.1.call-start = ((), (), s32[]{:S(2)}) async-start(), calls=%async_computation.18 | async-start | bytes 9437184 | tf_op jit(solution)/shard_map/all_gather | solution.py:615
  269.7 93.3 %all-gather.19.cloned.1.call-start = ((), (), s32[]{:S(2)}) async-start(), calls=%async_computation.19 | async-start | bytes 9437184 | tf_op jit(solution)/shard_map/all_gather | solution.py:615
  269.8 18.6 %copy-start.25 = (bf16[2,128,128]{2,1,0:T(8,128)(2,1)S(1)}, bf16[2,128,128]{2,1,0:T(8,128)(2,1)}, u32[]{:S(2)}) copy-start(bf16[2,128,128]{2,1,0:T(8,128)(2,1)} %param.39) | copy-start | bytes 196612
  269.8 19.2 %copy-start.17 = (bf16[2,128,640]{2,1,0:T(8,128)(2,1)S(1)}, bf16[2,128,640]{2,1,0:T(8,128)(2,1)}, u32[]{:S(2)}) copy-start(bf16[2,128,640]{2,1,0:T(8,128)(2,1)} %param.40) | copy-start | bytes 983044
  288.3 177.5 %all-gather.21.cloned.1.call-start = ((), (), s32[]{:S(2)}) async-start(), calls=%async_computation.20 | async-start | bytes 9437184 | tf_op jit(solution)/shard_map/all_gather | solution.py:615
  386.4 109.1 %all-gather.23.cloned.1.call-start = ((), (), s32[]{:S(2)}) async-start(), calls=%async_computation.21 | async-start | bytes 9437184 | tf_op jit(solution)/shard_map/all_gather | solution.py:615
  386.5 23.4 %copy-start.10 = (bf16[8,16,32,128]{3,2,1,0:T(8,128)(2,1)S(1)}, bf16[8,16,32,128]{3,2,1,0:T(8,128)(2,1)}, u32[]{:S(2)}) copy-start(bf16[8,16,32,128]{3,2,1,0:T(8,128)(2,1)} %get-tuple-element.79) | copy-start | bytes 3145732
  409.9 35.0 %copy-start.33 = (bf16[2,128,4]{1,2,0:T(4,128)(2,1)S(1)}, bf16[2,128,4]{1,2,0:T(4,128)(2,1)}, u32[]{:S(2)}) copy-start(bf16[2,128,4]{1,2,0:T(4,128)(2,1)} %param.43) | copy-start | bytes 6148
  409.9 35.6 %copy-start.34 = (bf16[2,128,4]{1,2,0:T(4,128)(2,1)S(1)}, bf16[2,128,4]{1,2,0:T(4,128)(2,1)}, u32[]{:S(2)}) copy-start(bf16[2,128,4]{1,2,0:T(4,128)(2,1)} %param.46) | copy-start | bytes 6148
  409.9 36.2 %copy-start.26 = (bf16[2,128,128]{2,1,0:T(8,128)(2,1)S(1)}, bf16[2,128,128]{2,1,0:T(8,128)(2,1)}, u32[]{:S(2)}) copy-start(bf16[2,128,128]{2,1,0:T(8,128)(2,1)} %param.41) | copy-start | bytes 196612
  409.9 36.8 %copy-start.27 = (bf16[2,128,128]{2,1,0:T(8,128)(2,1)S(1)}, bf16[2,128,128]{2,1,0:T(8,128)(2,1)}, u32[]{:S(2)}) copy-start(bf16[2,128,128]{2,1,0:T(8,128)(2,1)} %param.44) | copy-start | bytes 196612
  410.0 37.4 %copy-start.20 = (bf16[2,128,512]{2,1,0:T(8,128)(2,1)S(1)}, bf16[2,128,512]{2,1,0:T(8,128)(2,1)}, u32[]{:S(2)}) copy-start(bf16[2,128,512]{2,1,0:T(8,128)(2,1)} %param.42) | copy-start | bytes 786436
  440.7 25.1 %all-to-all-start.3 = ((bf16[8,16,32,128]{3,2,1,0:T(8,128)(2,1)}), bf16[8,16,32,128]{3,2,1,0:T(8,128)(2,1)S(1)}, u32[]{:S(2)}, u32[]{:S(2)}) async-start(bf16[8,16,32,128]{3,2,1,0:T(8,128)(2,1)} %get-tuple-element.82), calls=%async_computation.3 | async-start | bytes 2097152 | tf_op jit(solution)/shard_map/all_to_all | solution.py:619
  465.8 29.6 %copy-start.7 = (bf16[8,16,32,128]{3,2,1,0:T(8,128)(2,1)}, bf16[8,16,32,128]{3,2,1,0:T(8,128)(2,1)S(1)}, u32[]{:S(2)}) copy-start(bf16[8,16,32,128]{3,2,1,0:T(8,128)(2,1)S(1)} %all-to-all-done.3.refs_1_) | copy-start | bytes 3145732
  558.0 21.6 %all-to-all-start.4 = ((bf16[8,16,32,128]{3,2,1,0:T(8,128)(2,1)}), bf16[8,16,32,128]{3,2,1,0:T(8,128)(2,1)S(1)}, u32[]{:S(2)}, u32[]{:S(2)}) async-start(bf16[8,16,32,128]{3,2,1,0:T(8,128)(2,1)} %get-tuple-element.89), calls=%async_computation.4 | async-start | bytes 2097152 | tf_op jit(solution)/shard_map/all_to_all | solution.py:619
  579.5 25.3 %copy-start.5 = (bf16[8,16,32,128]{3,2,1,0:T(8,128)(2,1)}, bf16[8,16,32,128]{3,2,1,0:T(8,128)(2,1)S(1)}, u32[]{:S(2)}) copy-start(bf16[8,16,32,128]{3,2,1,0:T(8,128)(2,1)S(1)} %all-to-all-done.4.refs_0_) | copy-start | bytes 3145732
  579.5 25.2 %all-to-all-start.5 = ((bf16[8,16,32,128]{3,2,1,0:T(8,128)(2,1)}), bf16[8,16,32,128]{3,2,1,0:T(8,128)(2,1)S(1)}, u32[]{:S(2)}, u32[]{:S(2)}) async-start(bf16[8,16,32,128]{3,2,1,0:T(8,128)(2,1)} %get-tuple-element.90), calls=%async_computation.5 | async-start | bytes 2097152 | tf_op jit(solution)/shard_map/all_to_all | solution.py:619
  604.7 6.5 copy-start.28
  604.7 7.1 copy-start.21
  604.7 7.8 copy-start.22
  604.8 7.8 copy-start.23
  605.8 56.0 %all-to-all-start.6 = ((bf16[8,32,32,256]{3,2,1,0:T(8,128)(2,1)}), bf16[8,32,32,256]{3,2,1,0:T(8,128)(2,1)}, u32[]{:S(2)}, u32[]{:S(2)}) async-start(bf16[8,32,32,256]{3,2,1,0:T(8,128)(2,1)} %get-tuple-element.99), calls=%async_computation.6 | async-start | bytes 8388608 | tf_op jit(solution)/shard_map/all_to_all | solution.py:619
  676.0 34.4 %all-to-all-start.7 = ((bf16[8,32,32,128]{3,2,1,0:T(8,128)(2,1)}), bf16[8,32,32,128]{3,2,1,0:T(8,128)(2,1)S(1)}, u32[]{:S(2)}, u32[]{:S(2)}) async-start(bf16[8,32,32,128]{3,2,1,0:T(8,128)(2,1)} %get-tuple-element.104), calls=%async_computation.7 | async-start | bytes 4194304 | tf_op jit(solution)/shard_map/all_to_all | solution.py:619
  711.7 35.1 %all-to-all-start.9 = ((bf16[8,16,32,256]{3,2,1,0:T(8,128)(2,1)}), bf16[8,16,32,256]{3,2,1,0:T(8,128)(2,1)}, u32[]{:S(2)}, u32[]{:S(2)}) async-start(bf16[8,16,32,256]{3,2,1,0:T(8,128)(2,1)} %shard_map.266), calls=%async_computation.9 | async-start | bytes 4194304 | tf_op jit(solution)/shard_map/all_to_all | solution.py:619
  746.8 32.0 %all-to-all-start.8 = ((bf16[8,16,32,256]{3,2,1,0:T(8,128)(2,1)}), bf16[8,16,32,256]{3,2,1,0:T(8,128)(2,1)S(1)}, u32[]{:S(2)}, u32[]{:S(2)}) async-start(bf16[8,16,32,256]{3,2,1,0:T(8,128)(2,1)} %shard_map.265), calls=%async_computation.8 | async-start | bytes 4194304 | tf_op jit(solution)/shard_map/all_to_all | solution.py:619
  751.6 115.5 %all-gather.25.cloned.1.call-start = ((), (), s32[]{:S(2)}) async-start(), calls=%async_computation.22 | async-start | bytes 2359296 | tf_op jit(solution)/shard_map/all_gather | solution.py:615
  823.4 64.1 %all-gather.27.cloned.1.call-start = ((), (), s32[]{:S(2)}) async-start(), calls=%async_computation.23 | async-start | bytes 2359296 | tf_op jit(solution)/shard_map/all_gather | solution.py:615
  866.9 85.1 %all-gather.29.cloned.1.call-start = ((), (), s32[]{:S(2)}) async-start(), calls=%async_computation.24 | async-start | bytes 9437184 | tf_op jit(solution)/shard_map/all_gather | solution.py:615
  905.9 93.3 %all-gather.31.cloned.1.call-start = ((), (), s32[]{:S(2)}) async-start(), calls=%async_computation.25 | async-start | bytes 9437184 | tf_op jit(solution)/shard_map/all_gather | solution.py:615
  924.4 177.1 %all-gather.33.cloned.1.call-start = ((), (), s32[]{:S(2)}) async-start(), calls=%async_computation.26 | async-start | bytes 9437184 | tf_op jit(solution)/shard_map/all_gather | solution.py:615
  1022.6 108.7 %all-gather.35.cloned.1.call-start = ((), (), s32[]{:S(2)}) async-start(), calls=%async_computation.27 | async-start | bytes 9437184 | tf_op jit(solution)/shard_map/all_gather | solution.py:615
  1022.7 23.5 %copy-start.11 = (bf16[8,16,32,128]{3,2,1,0:T(8,128)(2,1)S(1)}, bf16[8,16,32,128]{3,2,1,0:T(8,128)(2,1)}, u32[]{:S(2)}) copy-start(bf16[8,16,32,128]{3,2,1,0:T(8,128)(2,1)} %get-tuple-element.116) | copy-start | bytes 3145732
  1076.8 24.7 %all-to-all-start.11 = ((bf16[8,16,32,128]{3,2,1,0:T(8,128)(2,1)}), bf16[8,16,32,128]{3,2,1,0:T(8,128)(2,1)S(1)}, u32[]{:S(2)}, u32[]{:S(2)}) async-start(bf16[8,16,32,128]{3,2,1,0:T(8,128)(2,1)} %get-tuple-element.119), calls=%async_computation.11 | async-start | bytes 2097152 | tf_op jit(solution)/shard_map/all_to_all | solution.py:619
  1101.5 29.8 %copy-start.9 = (bf16[8,16,32,128]{3,2,1,0:T(8,128)(2,1)}, bf16[8,16,32,128]{3,2,1,0:T(8,128)(2,1)S(1)}, u32[]{:S(2)}) copy-start(bf16[8,16,32,128]{3,2,1,0:T(8,128)(2,1)S(1)} %all-to-all-done.11.refs_1_) | copy-start | bytes 3145732
  1193.8 21.5 %all-to-all-start.12 = ((bf16[8,16,32,128]{3,2,1,0:T(8,128)(2,1)}), bf16[8,16,32,128]{3,2,1,0:T(8,128)(2,1)S(1)}, u32[]{:S(2)}, u32[]{:S(2)}) async-start(bf16[8,16,32,128]{3,2,1,0:T(8,128)(2,1)} %get-tuple-element.126), calls=%async_computation.12 | async-start | bytes 2097152 | tf_op jit(solution)/shard_map/all_to_all | solution.py:619
  1215.4 25.2 %copy-start.6 = (bf16[8,16,32,128]{3,2,1,0:T(8,128)(2,1)}, bf16[8,16,32,128]{3,2,1,0:T(8,128)(2,1)S(1)}, u32[]{:S(2)}) copy-start(bf16[8,16,32,128]{3,2,1,0:T(8,128)(2,1)S(1)} %all-to-all-done.12.refs_0_) | copy-start | bytes 3145732
  1215.4 25.2 %all-to-all-start.13 = ((bf16[8,16,32,128]{3,2,1,0:T(8,128)(2,1)}), bf16[8,16,32,128]{3,2,1,0:T(8,128)(2,1)S(1)}, u32[]{:S(2)}, u32[]{:S(2)}) async-start(bf16[8,16,32,128]{3,2,1,0:T(8,128)(2,1)} %get-tuple-element.127), calls=%async_computation.13 | async-start | bytes 2097152 | tf_op jit(solution)/shard_map/all_to_all | solution.py:619
  1241.6 54.2 %all-to-all-start.14 = ((bf16[8,32,32,256]{3,2,1,0:T(8,128)(2,1)}), bf16[8,32,32,256]{3,2,1,0:T(8,128)(2,1)}, u32[]{:S(2)}, u32[]{:S(2)}) async-start(bf16[8,32,32,256]{3,2,1,0:T(8,128)(2,1)} %get-tuple-element.135), calls=%async_computation.14 | async-start | bytes 8388608 | tf_op jit(solution)/shard_map/all_to_all | solution.py:619
  1295.7 30.8 %all-to-all-start.15 = ((bf16[8,32,32,128]{3,2,1,0:T(8,128)(2,1)}), bf16[8,32,32,128]{3,2,1,0:T(8,128)(2,1)S(1)}, u32[]{:S(2)}, u32[]{:S(2)}) async-start(bf16[8,32,32,128]{3,2,1,0:T(8,128)(2,1)} %get-tuple-element.137), calls=%async_computation.15 | async-start | bytes 4194304 | tf_op jit(solution)/shard_map/all_to_all | solution.py:619
  (14 other events, 39.9 us)
Sparse Core Ops, SparseCore 0:
  186.6 20.9 all-gather.12
  230.3 20.9 all-gather.14
  269.8 45.9 all-gather.16
  317.3 45.6 all-gather.18
  386.5 56.9 all-gather.20
  444.9 50.4 all-gather.22
  823.5 20.3 all-gather.24
  867.1 20.3 all-gather.26
  906.0 46.0 all-gather.28
  953.5 45.6 all-gather.30
  1022.7 56.9 all-gather.32
  1081.1 50.1 all-gather.34
